TPU v7x, 128 devices: a whole 4x4x4 slice. The times are simulated.
128 devices in a mesh: row: 16 (over z_hi, y, core), col: 8 (over x, z_lo).
Axes of the slice: x: 4, y: 4, z: 4 (z_hi: 2, z_lo: 2; z = z_hi * 2 + z_lo), core: 2. Of those that a mesh axis runs over, the one named last changes fastest.
Arguments:
- tokens: bfloat16 [16384, 2048], P(('row', 'col')), may hold values from -30 to 30
- ln1_gain: float32 [2048], replicated, may hold values from 0.25 to 1.75
- qkv_weight: bfloat16 [2048, 16, 3, 128], P('row', 'col'), may hold values from -4 to 4
- out_weight: bfloat16 [2048, 2048], P('col', 'row'), may hold values from -0.125 to 0.125
- ln2_gain: float32 [2048], replicated, may hold values from 0.25 to 1.75
- ffn_in: bfloat16 [2048, 8192], P('row', 'col'), may hold values from -0.125 to 0.125
- ffn_out: bfloat16 [8192, 2048], P('col', 'row'), may hold values from -0.0625 to 0.0625
- expert_ids: int32 [16384, 1], P(('row', 'col')), may hold values from 0 to 63; in each aligned block of 128 rows (0 to 127, 128 to 255, ...) at most 4 rows name the same one
- expert_in: bfloat16 [128, 2048, 2048], P(('row', 'col')), may hold values from -0.125 to 0.125
- expert_out: bfloat16 [128, 2048, 2048], P(('row', 'col')), may hold values from -0.09375 to 0.09375
Outputs:
- block_out: bfloat16 [16384, 2048], P(('row', 'col'))
Inputs may be any that keep to these rules, and one draw needn't show every extreme that they name: `expert_ids`: among the tokens of one device no expert is named more than 4 times, and in every draw some expert is named exactly 4 times by the tokens of some device.
All inputs are finite; a program needn't handle non-finite values.
Results may differ from a plain program's by a relative error of at most 0.013.
Values may be sent and summed in bfloat16 or wider, within the bound.
A program may use at most 128 MiB of HBM per device.

v0:
```python
import functools
import jax
import jax.numpy as jnp
from jax import lax
from jax.experimental import pallas as pl
from jax.experimental.pallas import tpu as pltpu
from jax.sharding import PartitionSpec as P

MESH = pl.DeviceIdType.MESH


def flipped(index, bit):
    return index + bit - 2 * bit * ((index // bit) % 2)


def comm_body(plan, row_total, col_total, *refs):
    gathers, spreads, swaps, shuffles = plan
    count = len(gathers) + len(spreads) + len(swaps) + len(shuffles)
    ins, outs, stages = refs[:count], refs[count : 2 * count], refs[2 * count : 3 * count]
    send, recv, local = refs[3 * count :]
    row = lax.axis_index("row")
    col = lax.axis_index("col")

    barrier = pltpu.get_barrier_semaphore()
    peers = 0
    if gathers or shuffles:
        for step in range(1, row_total):
            pl.semaphore_signal(
                barrier, inc=1, device_id=(lax.rem(row + step, row_total), col), device_id_type=MESH
            )
            peers += 1
    if spreads or swaps:
        for step in range(1, col_total):
            pl.semaphore_signal(
                barrier, inc=1, device_id=(row, lax.rem(col + step, col_total)), device_id_type=MESH
            )
            peers += 1

    loads = []
    for i in range(count):
        load = pltpu.make_async_copy(ins[i], stages[i], local.at[i])
        load.start()
        loads.append(load)
    pl.semaphore_wait(barrier, peers)

    serial = [0]
    finish = []

    def copy(src, dst, arriving, device):
        k = serial[0]
        serial[0] += 1
        out = pltpu.make_async_remote_copy(
            src, dst, send.at[k], recv.at[k], device_id=device, device_id_type=MESH
        )
        arrival = pltpu.make_async_remote_copy(
            src, arriving, send.at[k], recv.at[k], device_id=device, device_id_type=MESH
        )
        out.start()
        finish.append(out)
        return arrival

    pending = []
    kept = []

    def keep(i, dst):
        own = pltpu.make_async_copy(stages[i], dst, local.at[count + i])
        own.start()
        kept.append(own)

    base = len(gathers)
    for i in range(base, base + len(spreads)):
        loads[i].wait()
        size = ins[i].shape[0]
        block = lambda index, i=i, size=size: outs[i].at[pl.ds(pl.multiple_of(index * size, size), size)]
        for step in range(1, col_total):
            to = lax.rem(col + step, col_total)
            source = lax.rem(col + col_total - step, col_total)
            pending.append(copy(stages[i], block(col), block(source), (row, to)))
        keep(i, block(col))
    base += len(spreads)
    for i in range(base, base + len(swaps)):
        loads[i].wait()
        for step in range(1, col_total):
            to = lax.rem(col + step, col_total)
            slot = outs[i].at[step - 1]
            pending.append(copy(stages[i].at[to], slot, slot, (row, to)))
    base += len(swaps)
    for i in range(base, base + len(shuffles)):
        loads[i].wait()
        for step in range(1, row_total):
            to = lax.rem(row + (step if shuffles[i - base] > 0 else row_total - step), row_total)
            slot = outs[i].at[step]
            pending.append(copy(stages[i].at[step], slot, slot, (to, col)))
        own = pltpu.make_async_copy(stages[i].at[0], outs[i].at[0], local.at[count + i])
        own.start()
        kept.append(own)

    partner = flipped(row, 1)
    relay = row_total == 8

    def piece(i, index, half):
        depth, width = ins[i].shape
        start, size = (0, depth) if half is None else (half * (depth // 2), depth // 2)
        if gathers[i] == 0:
            return outs[i].at[pl.ds(pl.multiple_of(index * depth + start, size), size)]
        return outs[i].at[pl.ds(start, size), pl.ds(pl.multiple_of(index * width, width), width)]

    arrivals = []
    for i in range(len(gathers)):
        loads[i].wait()
        mine = piece(i, row, None)
        if relay:
            sources = [flipped(row, 2), flipped(row, 4)]
            targets = sources
        else:
            sources = [lax.rem(row + row_total - 2 * d, row_total) for d in range(1, row_total // 2)]
            targets = [lax.rem(row + 2 * d, row_total) for d in range(1, row_total // 2)]
        first = [
            (source, copy(stages[i], mine, piece(i, source, None), (target, col)))
            for source, target in zip(sources, targets)
        ]
        pending.append(copy(stages[i], mine, piece(i, partner, None), (partner, col)))
        keep(i, mine)
        arrivals.append(first)
    if relay:
        seconds = []
        for i in range(len(gathers)):
            (by_x, from_x), (by_y, from_y) = arrivals[i]
            across = flipped(by_x, 4)
            from_x.wait_recv()
            got = piece(i, by_x, 0)
            diag_a = copy(got, got, piece(i, across, 0), (by_y, col))
            whole = piece(i, by_x, None)
            pending.append(copy(whole, whole, piece(i, flipped(by_x, 1), None), (partner, col)))
            from_y.wait_recv()
            got = piece(i, by_y, 1)
            diag_b = copy(got, got, piece(i, across, 1), (by_x, col))
            whole = piece(i, by_y, None)
            pending.append(copy(whole, whole, piece(i, flipped(by_y, 1), None), (partner, col)))
            seconds.append((across, diag_a, diag_b))
        for i in range(len(gathers)):
            across, diag_a, diag_b = seconds[i]
            for half, arrival in ((0, diag_a), (1, diag_b)):
                arrival.wait_recv()
                got = piece(i, across, half)
                pending.append(copy(got, got, piece(i, flipped(across, 1), half), (partner, col)))
    else:
        for i in range(len(gathers)):
            for source, arrival in arrivals[i]:
                arrival.wait_recv()
                got = piece(i, source, None)
                pending.append(copy(got, got, piece(i, flipped(source, 1), None), (partner, col)))
    for arrival in pending:
        arrival.wait_recv()
    for out in finish:
        out.wait_send()
    for own in kept:
        own.wait()


def exchange(name, collective_id, gathers=(), spreads=(), swaps=(), shuffles=()):
    row_total = lax.axis_size("row")
    col_total = lax.axis_size("col")
    arrays, shapes, copies = [], [], 0
    for array, axis in gathers:
        depth, width = array.shape
        arrays.append(array)
        shapes.append((depth * row_total, width) if axis == 0 else (depth, width * row_total))
        copies += 9 if row_total == 8 else row_total
    for array in spreads:
        arrays.append(array)
        shapes.append((array.shape[0] * col_total,) + array.shape[1:])
        copies += col_total - 1
    for array in swaps:
        arrays.append(array)
        shapes.append((col_total - 1,) + array.shape[1:])
        copies += col_total - 1
    for array, _ in shuffles:
        arrays.append(array)
        shapes.append(array.shape)
        copies += row_total - 1
    plan = ([axis for _, axis in gathers], list(spreads), list(swaps), [sign for _, sign in shuffles])
    plan = (plan[0], [0] * len(spreads), [0] * len(swaps), plan[3])
    return pl.pallas_call(
        functools.partial(comm_body, plan, row_total, col_total),
        out_shape=[jax.ShapeDtypeStruct(s, a.dtype) for s, a in zip(shapes, arrays)],
        in_specs=[pl.BlockSpec(memory_space=pl.ANY)] * len(arrays),
        out_specs=[pl.BlockSpec(memory_space=pl.ANY)] * len(arrays),
        scratch_shapes=[pltpu.VMEM(a.shape, a.dtype) for a in arrays]
        + [
            pltpu.SemaphoreType.DMA((copies,)),
            pltpu.SemaphoreType.DMA((copies,)),
            pltpu.SemaphoreType.DMA((2 * len(arrays),)),
        ],
        compiler_params=pltpu.CompilerParams(
            collective_id=collective_id, has_side_effects=True, vmem_limit_bytes=24 * 2**20
        ),
        name=name,
    )(*arrays)


def up_body(x_ref, w_ref, o_ref):
    inner = jnp.dot(x_ref[...], w_ref[...], preferred_element_type=jnp.float32)
    o_ref[...] = (inner * (1.0 + lax.erf(inner * (0.5**0.5))) * 0.5).astype(o_ref.dtype)


def up_gelu(x, w):
    rows, depth = x.shape
    width = w.shape[1]
    tile = min(width, 256)
    return pl.pallas_call(
        up_body,
        grid=(width // tile,),
        out_shape=jax.ShapeDtypeStruct((rows, width), jnp.bfloat16),
        in_specs=[
            pl.BlockSpec((rows, depth), lambda j: (0, 0)),
            pl.BlockSpec((depth, tile), lambda j: (0, j)),
        ],
        out_specs=pl.BlockSpec((rows, tile), lambda j: (0, j)),
        compiler_params=pltpu.CompilerParams(vmem_limit_bytes=32 * 2**20),
        cost_estimate=pl.CostEstimate(
            flops=2 * rows * depth * width,
            bytes_accessed=2 * (rows * depth + depth * width + rows * width),
            transcendentals=0,
        ),
        name="up_gelu",
    )(x, w)


def layer_norm(row_data, gain_vector):
    row_data = row_data.astype(jnp.float32)
    centered = row_data - jnp.mean(row_data, axis=-1, keepdims=True)
    spread = jnp.mean(centered * centered, axis=-1, keepdims=True)
    return centered * lax.rsqrt(spread + 1e-06) * gain_vector


def matmul(a, b):
    return jnp.dot(a, b, preferred_element_type=jnp.float32)


def shards(
    tokens,
    ln1_gain,
    qkv_weight,
    out_weight,
    ln2_gain,
    ffn_in,
    ffn_out,
    expert_ids,
    expert_in,
    expert_out,
):
    tok_count, model_width = tokens.shape
    row_total = lax.axis_size("row")
    col_total = lax.axis_size("col")
    row_index = lax.axis_index("row")
    col_index = lax.axis_index("col")
    expert_count = row_total * col_total // 2
    capacity = max(2, 2 * tok_count // expert_count)
    head_count, head_dim = qkv_weight.shape[1], qkv_weight.shape[3]
    seq_len = tok_count * col_total

    ids_block = jnp.broadcast_to(expert_ids[:, 0][None, :], (8, tok_count))
    qkv_whole, out_whole, image_rows, ids_all = exchange(
        "enter",
        0,
        gathers=((qkv_weight.reshape(qkv_weight.shape[0], -1), 0), (out_weight, 1)),
        spreads=(tokens, ids_block),
    )
    normed = layer_norm(image_rows, ln1_gain).astype(jnp.bfloat16)
    projected = matmul(normed, qkv_whole).astype(jnp.bfloat16)
    projected = projected.reshape(seq_len, head_count, 3, head_dim)
    queries, keys, values = projected[:, :, 0], projected[:, :, 1], projected[:, :, 2]
    scores = jnp.einsum("qhd,khd->hqk", queries, keys, preferred_element_type=jnp.float32)
    scores = scores * (head_dim ** (-0.5))
    weights = jnp.exp(scores - jnp.max(scores, axis=-1, keepdims=True))
    probabilities = (weights / jnp.sum(weights, axis=-1, keepdims=True)).astype(jnp.bfloat16)
    attended = jnp.einsum("hqk,khd->qhd", probabilities, values, preferred_element_type=jnp.float32)
    attended = attended.astype(jnp.bfloat16).reshape(seq_len, head_count * head_dim)
    head_terms = matmul(attended, out_whole).astype(jnp.bfloat16)
    head_terms = head_terms.reshape(col_total, tok_count, model_width)

    up_whole, head_parts = exchange("heads", 1, gathers=((ffn_in, 0),), swaps=(head_terms,))
    own_terms = lax.dynamic_index_in_dim(head_terms, col_index, 0, keepdims=False)
    mixed_heads = own_terms.astype(jnp.float32) + jnp.sum(head_parts.astype(jnp.float32), axis=0)
    hidden_mine = (tokens.astype(jnp.float32) + mixed_heads).astype(jnp.bfloat16)
    normed_mine = layer_norm(hidden_mine, ln2_gain).astype(jnp.bfloat16)

    down_whole, normed_image = exchange(
        "norms", 2, gathers=((ffn_out, 1),), spreads=(normed_mine,)
    )

    ids_rows = ids_all.reshape(col_total, 8, tok_count)[:, 0]
    expert_range = jnp.arange(expert_count, dtype=jnp.int32)
    one_hot = (ids_rows[:, :, None] == expert_range).astype(jnp.int32)
    earlier = jnp.cumsum(one_hot, axis=1) - one_hot
    slot_index = jnp.sum(earlier * one_hot, axis=2)
    block_index = jnp.arange(col_total, dtype=jnp.int32)[:, None]
    home_row = 2 * ids_rows // col_total
    mine = (2 * ids_rows % col_total) // 2 == col_index // 2
    step = (home_row - row_index + row_total) % row_total
    position = (step * col_total + block_index) * capacity + slot_index
    position = jnp.where(mine, position, -1).reshape(seq_len)
    slot_count = row_total * col_total * capacity
    slots = jnp.arange(slot_count, dtype=jnp.int32)
    placing = (slots[:, None] == position[None, :]).astype(jnp.bfloat16)
    picking = (position[:, None] == slots[None, :]).astype(jnp.bfloat16)

    table = matmul(placing, normed_image).astype(jnp.bfloat16)
    table = table.reshape(row_total, col_total * capacity, model_width)
    (expert_rows,) = exchange("dispatch", 3, shuffles=((table, 1),))
    expert_units = up_gelu(expert_rows.reshape(slot_count, model_width), expert_in[0])
    partial_out = matmul(expert_units, expert_out[0]).astype(jnp.bfloat16)
    partial_out = partial_out.reshape(row_total, col_total * capacity, model_width)
    (returned,) = exchange("collect", 4, shuffles=((partial_out, -1),))

    hidden_units = up_gelu(normed_image, up_whole)
    rows_two = returned.reshape(slot_count, model_width)
    partial = matmul(hidden_units, down_whole) + matmul(picking, rows_two)
    partial = partial.astype(jnp.bfloat16).reshape(col_total, tok_count, model_width)
    (parts,) = exchange("leave", 5, swaps=(partial,))
    own_part = lax.dynamic_index_in_dim(partial, col_index, 0, keepdims=False)
    total = own_part.astype(jnp.float32) + jnp.sum(parts.astype(jnp.float32), axis=0)
    return (hidden_mine.astype(jnp.float32) + total).astype(jnp.bfloat16)


def solution(mesh):
    in_specs = (
        P(("row", "col"), None),
        P(),
        P("row", "col", None, None),
        P("col", "row"),
        P(),
        P("row", "col"),
        P("col", "row"),
        P(("row", "col"), None),
        P(("row", "col"), None, None),
        P(("row", "col"), None, None),
    )
    out_specs = P(("row", "col"), None)
    return jax.shard_map(shards, mesh=mesh, in_specs=in_specs, out_specs=out_specs, check_vma=False)
```

profile of v0, /device:TPU:52, one launch (start us, length us, event | category | flops | bytes accessed | tf_op | source)
XLA Modules:
  0.0 473.6 jit_solution(10885556277206395195)
XLA Ops:
  0.0 1.1 copy.31
  1.1 0.2 copy.32.refs_0_
  1.3 0.7 broadcast_in_dim.6.refs_3_
  1.9 0.0 copy-start.1
  1.9 1.0 copy-done.1
  3.0 0.0 copy-start.5
  3.0 0.8 copy-done.5
  3.8 89.4 %enter.1 = (bf16[2048,768]{1,0:T(8,128)(2,1)S(1)}, bf16[256,2048]{1,0:T(8,128)(2,1)S(1)}, bf16[1024,2048]{1,0:T(8,128)(2,1)S(1)}, s32[64,128]{1,0:T(8,128)S(1)}) custom-call(bf16[128,768]{1,0:T(8,128)(2,1)S(1)} %copy.32.refs_0_, bf16[256,128]{1,0:T(8,128)(2,1)S(1)} %copy-done.5, bf16[128,2048]{1,0:T(8,128)(2,1)S(1)} %copy-done.1, ...), custom_call_target="tpu_custom_call" | custom-call | tf_op jit(solution)/shard_map/enter/pallas_call | solution.py:184
  93.2 0.0 copy-start.14
  93.2 0.6 convert_reduce_fusion
  93.8 1.2 fusion.3
  95.1 0.0 copy-done.14
  95.1 4.1 fusion.21
  99.2 5.0 %fusion.58 = (f32[2,1024]{1,0:T(2,128)S(1)}, f32[2,1024,1024]{1,2,0:T(8,128)}) fusion(bf16[1024,2,3,128]{0,3,2,1:T(8,128)(2,1)S(1)} %bitcast.84), kind=kOutput, calls=%fused_computation.89 | convolution fusion | flops 543163392 | bytes 9445376 | tf_op jit(solution)/shard_map/sub | solution.py:276
  104.2 4.1 fusion.24
  108.3 0.0 copy-start.3
  108.3 1.3 convolution_convert_fusion
  109.6 0.0 copy-start
  109.6 0.0 copy-done.3
  109.6 0.0 copy-start.2
  109.6 79.1 %heads.1 = (bf16[2048,1024]{1,0:T(8,128)(2,1)S(1)}, bf16[7,128,2048]{2,1,0:T(8,128)(2,1)S(1)}) custom-call(bf16[128,1024]{1,0:T(8,128)(2,1)S(1)} %copy-done.3, bf16[8,128,2048]{2,1,0:T(8,128)(2,1)S(1)} %bitcast.69), custom_call_target="tpu_custom_call" | custom-call | tf_op jit(solution)/shard_map/heads/pallas_call | solution.py:184
  188.7 0.0 copy-start.7
  188.8 1.9 copy-done.7
  190.7 0.0 copy-start.13
  190.7 0.0 copy-start.4
  190.7 0.6 convert_reduce_fusion.2
  191.3 0.0 copy-done
  191.3 0.0 copy-done.2
  191.3 1.3 convert_reduce_fusion.3
  192.7 0.3 fusion.27
  193.0 0.0 copy-done.13
  193.0 0.4 fusion.29.refs_1_
  193.4 0.0 copy-done.4
  193.4 86.4 %norms.1 = (bf16[1024,2048]{1,0:T(8,128)(2,1)S(1)}, bf16[1024,2048]{1,0:T(8,128)(2,1)S(1)}) custom-call(bf16[1024,128]{1,0:T(8,128)(2,1)S(1)} %copy-done.4, bf16[128,2048]{1,0:T(8,128)(2,1)S(1)} %fusion.29.refs_1_), custom_call_target="tpu_custom_call" | custom-call | tf_op jit(solution)/shard_map/norms/pallas_call | solution.py:184
  279.8 0.0 copy-start.9
  279.8 2.0 copy-done.9
  281.8 0.0 copy-start.11
  281.8 2.0 copy-done.11
  283.7 0.1 copy.37
  283.9 2.5 select_reduce_fusion
  286.5 4.5 convolution_convert_fusion.1
  291.0 41.8 %dispatch.1 = bf16[16,32,2048]{2,1,0:T(8,128)(2,1)S(1)} custom-call(bf16[16,32,2048]{2,1,0:T(8,128)(2,1)S(1)} %bitcast.76), custom_call_target="tpu_custom_call" | custom-call | tf_op jit(solution)/shard_map/dispatch/pallas_call | solution.py:184
  332.8 0.0 copy-start.6
  332.8 3.4 copy-done.6
  336.2 7.2 %up_gelu.3 = bf16[512,2048]{1,0:T(8,128)(2,1)S(1)} custom-call(bf16[512,2048]{1,0:T(8,128)(2,1)S(1)} %bitcast.74, bf16[2048,2048]{1,0:T(8,128)(2,1)S(1)} %bitcast.78), custom_call_target="tpu_custom_call" | custom-call | flops 4294967296 | bytes 12582912 | tf_op jit(solution)/shard_map/up_gelu/pallas_call | solution.py:211
  343.5 0.0 copy-start.12
  343.5 8.3 %fusion.18 = bf16[512,2048]{1,0:T(8,128)(2,1)S(1)} fusion(bf16[512,2048]{1,0:T(8,128)(2,1)S(1)} %up_gelu.3, bf16[1,2048,2048]{2,1,0:T(8,128)(2,1)} %param.19), kind=kOutput, calls=%fused_computation.25 | convolution fusion | flops 4296015872 | bytes 12582912 | tf_op jit(solution)/shard_map/dot_general | solution.py:238
  351.8 0.0 copy-start.8
  351.8 35.2 %collect.1 = bf16[16,32,2048]{2,1,0:T(8,128)(2,1)S(1)} custom-call(bf16[16,32,2048]{2,1,0:T(8,128)(2,1)S(1)} %bitcast.75), custom_call_target="tpu_custom_call" | custom-call | tf_op jit(solution)/shard_map/collect/pallas_call | solution.py:184
  386.9 0.0 copy-done.12
  386.9 0.0 copy-done.8
  387.0 0.0 copy-start.10
  387.0 6.1 %up_gelu.2 = bf16[1024,1024]{1,0:T(8,128)(2,1)S(1)} custom-call(bf16[1024,2048]{1,0:T(8,128)(2,1)S(1)} %copy-done.12, bf16[2048,1024]{1,0:T(8,128)(2,1)S(1)} %copy-done.8), custom_call_target="tpu_custom_call" | custom-call | flops 4294967296 | bytes 10485760 | tf_op jit(solution)/shard_map/up_gelu/pallas_call | solution.py:211
  393.1 0.0 copy-done.10
  393.1 4.5 fusion.59
  397.6 2.5 add_convert_fusion
  400.1 71.9 %leave.1 = bf16[7,128,2048]{2,1,0:T(8,128)(2,1)S(1)} custom-call(bf16[8,128,2048]{2,1,0:T(8,128)(2,1)S(1)} %bitcast.71), custom_call_target="tpu_custom_call" | custom-call | tf_op jit(solution)/shard_map/leave/pallas_call | solution.py:184
  472.0 0.6 convert_reduce_fusion.1
  472.6 1.0 fusion.30
  (7 shorter events, 0.1 us)
Async XLA Ops:
  1.9 1.0 copy-start.1
  3.0 0.8 copy-start.5
  93.2 1.9 copy-start.14
  108.3 1.3 copy-start.3
  109.6 81.7 %copy-start = (bf16[1024,2048]{1,0:T(8,128)(2,1)}, bf16[1024,2048]{1,0:T(8,128)(2,1)S(1)}, u32[]{:S(2)}) copy-start(bf16[1024,2048]{1,0:T(8,128)(2,1)S(1)} %convolution_convert_fusion) | copy-start | bytes 12582916
  109.6 81.7 %copy-start.2 = (bf16[128,2048]{1,0:T(8,128)(2,1)S(1)}, bf16[128,2048]{1,0:T(8,128)(2,1)}, u32[]{:S(2)}) copy-start(bf16[128,2048]{1,0:T(8,128)(2,1)} %refs_2_.1) | copy-start | bytes 1572868
  188.7 1.9 copy-start.7
  190.7 2.3 copy-start.13
  190.7 2.7 copy-start.4
  279.8 2.0 copy-start.9
  281.8 2.0 copy-start.11
  332.8 3.4 copy-start.6
  343.5 43.5 %copy-start.12 = (bf16[1024,2048]{1,0:T(8,128)(2,1)S(1)}, bf16[1024,2048]{1,0:T(8,128)(2,1)}, u32[]{:S(2)}) copy-start(bf16[1024,2048]{1,0:T(8,128)(2,1)} %copy-done.11) | copy-start | bytes 12582916
  351.8 35.2 %copy-start.8 = (bf16[2048,1024]{1,0:T(8,128)(2,1)S(1)}, bf16[2048,1024]{1,0:T(8,128)(2,1)}, u32[]{:S(2)}) copy-start(bf16[2048,1024]{1,0:T(8,128)(2,1)} %copy-done.7) | copy-start | bytes 12582916
  387.0 6.1 %copy-start.10 = (bf16[1024,2048]{1,0:T(8,128)(2,1)S(1)}, bf16[1024,2048]{1,0:T(8,128)(2,1)}, u32[]{:S(2)}) copy-start(bf16[1024,2048]{1,0:T(8,128)(2,1)} %copy-done.9) | copy-start | bytes 12582916
where the time goes:
time: 474 us
  Pallas kernels  417 us (88%)
  matrix products  34.3 us (7%)
  local copies, waits for them, and re-layouts  13.2 us (3%)
  other arithmetic  8.7 us (2%)
    pallas_call x6, Pallas kernels, exchange(): pl.pallas_call(functools.partial(comm_body, plan, row_total, col_total),...  404 us
    dot_general x6, matrix products, matmul(): return jnp.dot(a, b, preferred_element_type=jnp.float32)  25.2 us
    pallas_call x2, Pallas kernels, up_gelu(): pl.pallas_call(up_body, grid=(width // tile,), out_shape=jax.ShapeDtypeSt...  13.4 us
    unnamed x31, local copies, waits for them, and re-layouts  12.3 us

commit v1 on v0

v1 whole, which is shorter than its diff:
```python
import functools
import heapq
import jax
import jax.numpy as jnp
from jax import lax
from jax.experimental import pallas as pl
from jax.experimental.pallas import tpu as pltpu
from jax.sharding import PartitionSpec as P

MESH = pl.DeviceIdType.MESH
SPLIT = 32


class Net:
    def __init__(self, send, recv):
        row, col = lax.axis_index("row"), lax.axis_index("col")
        self.row, self.col = row, col
        self.high, self.y, self.core = row // 8, lax.rem(row // 2, 4), lax.rem(row, 2)
        self.x, self.low = col // 2, lax.rem(col, 2)
        self.send, self.recv = send, recv
        self.count = 0
        self.finish = []
        self.queue = []
        self.serial = 0

    def row_of(self, high, y, core):
        return high * 8 + lax.rem(y + 8, 4) * 2 + core

    def col_of(self, x, low):
        return lax.rem(x + 8, 4) * 2 + low

    def peer(self, name):
        high, y, core, x, low = self.high, self.y, self.core, self.x, self.low
        at = {
            "x+": (high, y, core, x + 1, low),
            "x-": (high, y, core, x - 1, low),
            "z": (high, y, core, x, 1 - low),
            "y+": (high, y + 1, core, x, low),
            "y-": (high, y - 1, core, x, low),
            "h": (1 - high, y, core, x, low),
            "c": (high, y, 1 - core, x, low),
        }[name]
        return self.row_of(*at[:3]), self.col_of(*at[3:])

    def greet(self, names):
        barrier = pltpu.get_barrier_semaphore()
        for name in names:
            pl.semaphore_signal(barrier, inc=1, device_id=self.peer(name), device_id_type=MESH)
        pl.semaphore_wait(barrier, len(names))

    def copy(self, src, dst, arriving, name):
        k = self.count
        self.count += 1
        make = lambda target: pltpu.make_async_remote_copy(
            src, target, self.send.at[k], self.recv.at[k], device_id=self.peer(name), device_id_type=MESH
        )
        out, arrival = make(dst), make(arriving)
        out.start()
        self.finish.append(out)
        return arrival

    def at(self, time, action):
        heapq.heappush(self.queue, (time, self.serial, action))
        self.serial += 1

    def when(self, time, arrival, action=None):
        def run():
            arrival.wait_recv()
            if action is not None:
                action()

        self.at(time, run)

    def run(self):
        while self.queue:
            heapq.heappop(self.queue)[2]()
        for out in self.finish:
            out.wait_send()


def rows_of(ref, start, size, step=16):
    return ref.at[pl.ds(pl.multiple_of(start, step), size)]


def spread(net, src, out):
    size = src.shape[0]
    a, half_a, half_b = SPLIT, SPLIT // 2, (size - SPLIT) // 2
    b = size - a
    x, low = net.x, net.low

    def part(dx, other, start, rows):
        plane = 1 - low if other else low
        return rows_of(out, net.col_of(x + dx, plane) * size + start, rows)

    def own(start, rows):
        return src.at[pl.ds(start, rows)]

    def from_a(side):
        step = 1 if side == "x-" else -1
        at = -step
        forward = "x+" if step > 0 else "x-"
        start = 0 if step > 0 else half_a
        got = part(at, 0, start, half_a)
        far = net.copy(got, got, part(at - step, 0, start, half_a), forward)
        net.when(6.0, far, lambda: to_z(part(2, 0, start, half_a), part(2, 1, start, half_a)))
        to_z(part(at, 0, 0, a), part(at, 1, 0, a))

    def to_z(got, arriving):
        net.when(27.0, net.copy(got, got, arriving, "z"))

    def from_b(side, other):
        step = 1 if side == "x-" else -1
        start = a if step > 0 else a + half_b
        got = part(-step, other, start, half_b)
        forward = "x+" if step > 0 else "x-"
        net.when(27.0, net.copy(got, got, part(-2 * step, other, start, half_b), forward))

    def from_z():
        got = part(0, 1, a, b)
        for side, forward in (("x-", "x+"), ("x+", "x-")):
            dx = -1 if side == "x-" else 1
            arrival = net.copy(got, got, part(dx, 1, a, b), forward)
            net.when(20.0, arrival, lambda side=side: from_b(side, 1))

    arrival = net.copy(own(a, b), part(0, 0, a, b), part(0, 1, a, b), "z")
    net.when(9.0, arrival, from_z)
    for side, forward in (("x-", "x+"), ("x+", "x-")):
        dx = -1 if side == "x-" else 1
        arrival = net.copy(own(0, a), part(0, 0, 0, a), part(dx, 0, 0, a), forward)
        net.when(4.0, arrival, lambda side=side: from_a(side))
    for side, forward in (("x-", "x+"), ("x+", "x-")):
        dx = -1 if side == "x-" else 1
        arrival = net.copy(own(a, b), part(0, 0, a, b), part(dx, 0, a, b), forward)
        net.when(12.0, arrival, lambda side=side: from_b(side, 0))
    to_z_own = net.copy(own(0, a), part(0, 0, 0, a), part(0, 1, 0, a), "z")
    net.when(27.0, to_z_own)
    out[pl.ds(pl.multiple_of(net.col * size, size), size), :] = src[...]


def spread_small(net, src, out):
    size = src.shape[0]
    x, low = net.x, net.low

    def part(dx, other):
        plane = 1 - low if other else low
        return rows_of(out, net.col_of(x + dx, plane) * size, size, 8)

    def onward(other):
        got = part(-1, other)
        net.when(27.0, net.copy(got, got, part(-2, other), "x+"))

    def around(other, got):
        arrival = net.copy(got, part(0, other), part(-1, other), "x+")
        net.when(5.0 + other, arrival, lambda: onward(other))
        net.when(27.0, net.copy(got, part(0, other), part(1, other), "x-"))

    around(0, src)
    arrival = net.copy(src, part(0, 0), part(0, 1), "z")
    net.when(3.0, arrival, lambda: around(1, part(0, 1)))
    out[pl.ds(pl.multiple_of(net.col * size, size), size), :] = src[...]


def gather(net, src, out, axis, early, late):
    depth, width = src.shape
    high, y, core = net.high, net.y, net.core
    middle = depth // 2

    def part(dy, other, core, half=None):
        index = net.row_of(1 - high if other else high, y + dy, core)
        start, size = (0, depth) if half is None else (half * middle, middle)
        if axis == 0:
            return rows_of(out, index * depth + start, size)
        return out.at[pl.ds(start, size), pl.ds(pl.multiple_of(index * width, width), width)]

    def to_core(dy, other, half=None):
        got = part(dy, other, core, half)
        net.when(late, net.copy(got, got, part(dy, other, 1 - core, half), "c"))

    def from_y(dy, other):
        got = part(dy, other, core, 0 if dy < 0 else 1)
        forward = "y+" if dy < 0 else "y-"
        half = 0 if dy < 0 else 1
        arrival = net.copy(got, got, part(2, other, core, half), forward)
        net.when(late - 1, arrival, lambda: to_core(2, other, half))
        to_core(dy, other)

    def around(other, got, time):
        for dy, forward in ((-1, "y+"), (1, "y-")):
            arrival = net.copy(got, part(0, other, core), part(dy, other, core), forward)
            net.when(time, arrival, lambda dy=dy: from_y(dy, other))

    around(0, src, early + 0.5)
    mine = part(0, 0, core)
    arrival = net.copy(src, mine, part(0, 1, core), "h")

    def from_high():
        around(1, part(0, 1, core), early + 0.6 * (late - early))
        to_core(0, 1)

    net.when(early + 0.3 * (late - early), arrival, from_high)
    net.when(late, net.copy(src, mine, part(0, 0, 1 - core), "c"))
    index = net.row
    if axis == 0:
        out[pl.ds(pl.multiple_of(index * depth, depth), depth), :] = src[...]
    else:
        out[:, pl.ds(pl.multiple_of(index * width, width), width)] = src[...]


def reduce_scatter(net, src, out, scratch):
    from_z, sums, far_a, near_a, acc_a, far_b, near_b, acc_b, plane, last = scratch
    size = out.shape[0]
    a = SPLIT
    b = size - a
    x, low = net.x, net.low

    def rows(dx, other, start, count):
        index = net.col_of(x + dx, 1 - low if other else low)
        return pl.ds(pl.multiple_of(index * size + start, 16), count)

    def ring(block, start, count, far, near, acc, times, done):
        half = count // 2
        halves = {"x+": (0, half), "x-": (half, half)}
        waiting = [4]

        def arrived():
            waiting[0] -= 1
            if waiting[0] == 0:
                done()

        for index, forward in ((0, "x+"), (1, "x-")):
            first = halves[forward][0]
            arrival = net.copy(block(2, first, half), far.at[index], far.at[index], forward)

            def add(index=index, forward=forward, first=first):
                term = block(1 if forward == "x+" else -1, first, half)
                acc[index] = far[index] + term[...]
                dst = near.at[index, pl.ds(first, half)]
                net.when(times[2], net.copy(acc.at[index], dst, dst, forward), arrived)

            net.when(times[0], arrival, add)
        for index, forward in ((0, "x+"), (1, "x-")):
            first = half - halves[forward][0]
            dst = near.at[index, pl.ds(first, half)]
            term = block(1 if forward == "x+" else -1, first, half)
            net.when(times[1], net.copy(term, dst, dst, forward), arrived)

    def block_b(other):
        return lambda dx, first, count: src.at[rows(dx, other, a + first, count)]

    def block_a(dx, first, count):
        return sums.at[pl.ds((dx % 4) * a + first, count)]

    arrivals = []
    for k in (2, 1, 3, 0):
        arrivals.append((k, net.copy(
            src.at[rows(k, 1, 0, a)], from_z.at[pl.ds(k * a, a)], from_z.at[pl.ds(k * a, a)], "z"
        )))

    def plane_done():
        index = rows(0, 1, a, b)
        total = near_b[0, 0].astype(jnp.float32) + near_b[0, 1].astype(jnp.float32)
        plane[...] = (total + src[index, :].astype(jnp.float32)).astype(plane.dtype)
        net.when(31.0, net.copy(plane, last, last, "z"), finish_b)

    def finish_b():
        out[pl.ds(a, b), :] = out[pl.ds(a, b), :] + last[...].astype(jnp.float32)

    def own_done():
        total = near_b[1, 0].astype(jnp.float32) + near_b[1, 1].astype(jnp.float32)
        out[pl.ds(a, b), :] = total + src[rows(0, 0, a, b), :].astype(jnp.float32)

    def a_done():
        total = near_a[0].astype(jnp.float32) + near_a[1].astype(jnp.float32)
        out[pl.ds(0, a), :] = total + sums[pl.ds(0, a), :].astype(jnp.float32)

    def start_a():
        for k, arrival in arrivals:
            arrival.wait_recv()
            sums[pl.ds(k * a, a), :] = from_z[pl.ds(k * a, a), :] + src[rows(k, 0, 0, a), :]
        ring(block_a, 0, a, far_a, near_a, acc_a, (26.0, 29.0, 29.5), a_done)

    ring(block_b(1), a, b, far_b.at[0], near_b.at[0], acc_b.at[0], (5.0, 18.0, 18.5), plane_done)
    ring(block_b(0), a, b, far_b.at[1], near_b.at[1], acc_b.at[1], (9.0, 27.0, 27.5), own_done)
    net.at(13.0, start_a)


def scatter_scratch(size, width, dtype):
    a = SPLIT
    b = size - a
    shapes = [(4 * a, width), (4 * a, width), (2, a // 2, width), (2, a, width), (2, a // 2, width)]
    shapes += [(2, 2, b // 2, width), (2, 2, b, width), (2, 2, b // 2, width), (b, width), (b, width)]
    return [pltpu.VMEM(shape, dtype) for shape in shapes]


def comm_body(spreads, smalls, gathers, sums, *refs):
    count = spreads + smalls + len(gathers) + sums
    ins, outs, rest = refs[:count], refs[count : 2 * count], refs[2 * count :]
    scratch, (send, recv) = rest[:-2], rest[-2:]
    net = Net(send, recv)
    names = []
    if spreads or smalls or sums:
        names += ["x+", "x-", "z"]
    if gathers:
        names += ["y+", "y-", "h", "c"]
    net.greet(names)
    k = 0
    for _ in range(sums):
        reduce_scatter(net, ins[k], outs[k], scratch)
        k += 1
    for _ in range(spreads):
        spread(net, ins[k], outs[k])
        k += 1
    for _ in range(smalls):
        spread_small(net, ins[k], outs[k])
        k += 1
    for axis, early, late in gathers:
        gather(net, ins[k], outs[k], axis, early, late)
        k += 1
    net.run()


def exchange(name, collective_id, sums=(), spreads=(), smalls=(), gathers=()):
    row_total = lax.axis_size("row")
    col_total = lax.axis_size("col")
    arrays, shapes, scratch, copies = [], [], [], 0
    for array in sums:
        size = array.shape[0] // col_total
        arrays.append(array)
        shapes.append(jax.ShapeDtypeStruct((size, array.shape[1]), jnp.float32))
        scratch += scatter_scratch(size, array.shape[1], array.dtype)
        copies += 24
    for array in spreads:
        arrays.append(array)
        shapes.append(jax.ShapeDtypeStruct((array.shape[0] * col_total, array.shape[1]), array.dtype))
        copies += 20
    for array in smalls:
        arrays.append(array)
        shapes.append(jax.ShapeDtypeStruct((array.shape[0] * col_total, array.shape[1]), array.dtype))
        copies += 8
    for array, axis, _, _ in gathers:
        depth, width = array.shape
        arrays.append(array)
        shape = (depth * row_total, width) if axis == 0 else (depth, width * row_total)
        shapes.append(jax.ShapeDtypeStruct(shape, array.dtype))
        copies += 20
    return pl.pallas_call(
        functools.partial(comm_body, len(spreads), len(smalls), [g[1:] for g in gathers], len(sums)),
        out_shape=shapes,
        in_specs=[pl.BlockSpec(memory_space=pltpu.VMEM)] * len(arrays),
        out_specs=[pl.BlockSpec(memory_space=pltpu.VMEM)] * len(arrays),
        scratch_shapes=scratch + [pltpu.SemaphoreType.DMA((copies,)), pltpu.SemaphoreType.DMA((copies,))],
        compiler_params=pltpu.CompilerParams(
            collective_id=collective_id, has_side_effects=True, vmem_limit_bytes=40 * 2**20
        ),
        name=name,
    )(*arrays)


def shuffle_body(sign, row_total, source, out, stage, send, recv, local):
    row = lax.axis_index("row")
    col = lax.axis_index("col")
    barrier = pltpu.get_barrier_semaphore()
    for step in range(1, row_total):
        pl.semaphore_signal(
            barrier, inc=1, device_id=(lax.rem(row + step, row_total), col), device_id_type=MESH
        )
    load = pltpu.make_async_copy(source, stage, local.at[0])
    load.start()
    pl.semaphore_wait(barrier, row_total - 1)
    load.wait()
    copies = []
    for step in range(1, row_total):
        to = lax.rem(row + (step if sign > 0 else row_total - step), row_total)
        copy = pltpu.make_async_remote_copy(
            stage.at[step], out.at[step], send.at[step - 1], recv.at[step - 1], device_id=(to, col), device_id_type=MESH
        )
        copy.start()
        copies.append(copy)
    own = pltpu.make_async_copy(stage.at[0], out.at[0], local.at[1])
    own.start()
    for copy in copies:
        copy.wait()
    own.wait()


def shuffle(name, collective_id, array, sign):
    row_total = lax.axis_size("row")
    return pl.pallas_call(
        functools.partial(shuffle_body, sign, row_total),
        out_shape=jax.ShapeDtypeStruct(array.shape, array.dtype),
        in_specs=[pl.BlockSpec(memory_space=pl.ANY)],
        out_specs=pl.BlockSpec(memory_space=pl.ANY),
        scratch_shapes=[
            pltpu.VMEM(array.shape, array.dtype),
            pltpu.SemaphoreType.DMA((row_total - 1,)),
            pltpu.SemaphoreType.DMA((row_total - 1,)),
            pltpu.SemaphoreType.DMA((2,)),
        ],
        compiler_params=pltpu.CompilerParams(
            collective_id=collective_id, has_side_effects=True, vmem_limit_bytes=24 * 2**20
        ),
        name=name,
    )(array)


def up_body(x_ref, w_ref, o_ref):
    inner = jnp.dot(x_ref[...], w_ref[...], preferred_element_type=jnp.float32)
    o_ref[...] = (inner * (1.0 + lax.erf(inner * (0.5**0.5))) * 0.5).astype(o_ref.dtype)


def up_gelu(x, w):
    rows, depth = x.shape
    width = w.shape[1]
    tile = min(width, 256)
    return pl.pallas_call(
        up_body,
        grid=(width // tile,),
        out_shape=jax.ShapeDtypeStruct((rows, width), jnp.bfloat16),
        in_specs=[
            pl.BlockSpec((rows, depth), lambda j: (0, 0)),
            pl.BlockSpec((depth, tile), lambda j: (0, j)),
        ],
        out_specs=pl.BlockSpec((rows, tile), lambda j: (0, j)),
        compiler_params=pltpu.CompilerParams(vmem_limit_bytes=32 * 2**20),
        cost_estimate=pl.CostEstimate(
            flops=2 * rows * depth * width,
            bytes_accessed=2 * (rows * depth + depth * width + rows * width),
            transcendentals=0,
        ),
        name="up_gelu",
    )(x, w)


def layer_norm(row_data, gain_vector):
    row_data = row_data.astype(jnp.float32)
    centered = row_data - jnp.mean(row_data, axis=-1, keepdims=True)
    spread = jnp.mean(centered * centered, axis=-1, keepdims=True)
    return centered * lax.rsqrt(spread + 1e-06) * gain_vector


def matmul(a, b):
    return jnp.dot(a, b, preferred_element_type=jnp.float32)


def shards(
    tokens,
    ln1_gain,
    qkv_weight,
    out_weight,
    ln2_gain,
    ffn_in,
    ffn_out,
    expert_ids,
    expert_in,
    expert_out,
):
    tok_count, model_width = tokens.shape
    row_total = lax.axis_size("row")
    col_total = lax.axis_size("col")
    row_index = lax.axis_index("row")
    col_index = lax.axis_index("col")
    expert_count = row_total * col_total // 2
    capacity = max(2, 2 * tok_count // expert_count)
    head_count, head_dim = qkv_weight.shape[1], qkv_weight.shape[3]
    seq_len = tok_count * col_total

    ids_block = jnp.broadcast_to(expert_ids[:, 0][None, :], (8, tok_count))
    image_rows, ids_all, qkv_whole, out_whole = exchange(
        "enter",
        0,
        spreads=(tokens,),
        smalls=(ids_block,),
        gathers=((qkv_weight.reshape(qkv_weight.shape[0], -1), 0, 3.0, 14.0), (out_weight, 1, 13.0, 19.0)),
    )
    normed = layer_norm(image_rows, ln1_gain).astype(jnp.bfloat16)
    projected = matmul(normed, qkv_whole).astype(jnp.bfloat16)
    projected = projected.reshape(seq_len, head_count, 3, head_dim)
    queries, keys, values = projected[:, :, 0], projected[:, :, 1], projected[:, :, 2]
    scores = jnp.einsum("qhd,khd->hqk", queries, keys, preferred_element_type=jnp.float32)
    scores = scores * (head_dim ** (-0.5))
    weights = jnp.exp(scores - jnp.max(scores, axis=-1, keepdims=True))
    probabilities = (weights / jnp.sum(weights, axis=-1, keepdims=True)).astype(jnp.bfloat16)
    attended = jnp.einsum("hqk,khd->qhd", probabilities, values, preferred_element_type=jnp.float32)
    attended = attended.astype(jnp.bfloat16).reshape(seq_len, head_count * head_dim)
    head_terms = matmul(attended, out_whole).astype(jnp.bfloat16)
    mixed_heads, up_whole = exchange("heads", 1, sums=(head_terms,), gathers=((ffn_in, 0, 5.0, 19.0),))
    hidden_mine = (tokens.astype(jnp.float32) + mixed_heads).astype(jnp.bfloat16)
    normed_mine = layer_norm(hidden_mine, ln2_gain).astype(jnp.bfloat16)

    normed_image, down_whole = exchange(
        "norms", 2, spreads=(normed_mine,), gathers=((ffn_out, 1, 5.0, 19.0),)
    )

    ids_rows = ids_all.reshape(col_total, 8, tok_count)[:, 0]
    expert_range = jnp.arange(expert_count, dtype=jnp.int32)
    one_hot = (ids_rows[:, :, None] == expert_range).astype(jnp.int32)
    earlier = jnp.cumsum(one_hot, axis=1) - one_hot
    slot_index = jnp.sum(earlier * one_hot, axis=2)
    block_index = jnp.arange(col_total, dtype=jnp.int32)[:, None]
    home_row = 2 * ids_rows // col_total
    mine = (2 * ids_rows % col_total) // 2 == col_index // 2
    step = (home_row - row_index + row_total) % row_total
    position = (step * col_total + block_index) * capacity + slot_index
    position = jnp.where(mine, position, -1).reshape(seq_len)
    slot_count = row_total * col_total * capacity
    slots = jnp.arange(slot_count, dtype=jnp.int32)
    placing = (slots[:, None] == position[None, :]).astype(jnp.bfloat16)
    picking = (position[:, None] == slots[None, :]).astype(jnp.bfloat16)

    table = matmul(placing, normed_image).astype(jnp.bfloat16)
    table = table.reshape(row_total, col_total * capacity, model_width)
    expert_rows = shuffle("dispatch", 3, table, 1)
    expert_units = up_gelu(expert_rows.reshape(slot_count, model_width), expert_in[0])
    partial_out = matmul(expert_units, expert_out[0]).astype(jnp.bfloat16)
    partial_out = partial_out.reshape(row_total, col_total * capacity, model_width)
    returned = shuffle("collect", 4, partial_out, -1)

    hidden_units = up_gelu(normed_image, up_whole)
    rows_two = returned.reshape(slot_count, model_width)
    partial = matmul(hidden_units, down_whole) + matmul(picking, rows_two)
    (total,) = exchange("leave", 5, sums=(partial.astype(jnp.bfloat16),))
    return (hidden_mine.astype(jnp.float32) + total).astype(jnp.bfloat16)


def solution(mesh):
    in_specs = (
        P(("row", "col"), None),
        P(),
        P("row", "col", None, None),
        P("col", "row"),
        P(),
        P("row", "col"),
        P("col", "row"),
        P(("row", "col"), None),
        P(("row", "col"), None, None),
        P(("row", "col"), None, None),
    )
    out_specs = P(("row", "col"), None)
    return jax.shard_map(shards, mesh=mesh, in_specs=in_specs, out_specs=out_specs, check_vma=False)
```

time: 474 us -> 308 us (0.65)
  the two profiles are of different devices: /device:TPU:52 before, /device:TPU:2 now
where the time goes in v1:
time: 308 us; the launch traced here: 305 us
  Pallas kernels  251 us (81%)
  matrix products  34.5 us (11%)
  local copies, waits for them, and re-layouts  13.2 us (4%)
  other arithmetic  6.2 us (2%)
    pallas_call x4, Pallas kernels, exchange(): pl.pallas_call(functools.partial(comm_body, len(spreads), len(smalls), [g...  166 us
    pallas_call x2, Pallas kernels, shuffle(): pl.pallas_call(functools.partial(shuffle_body, sign, row_total), out_shap...  71.6 us
    dot_general x6, matrix products, matmul(): return jnp.dot(a, b, preferred_element_type=jnp.float32)  25.3 us
    pallas_call x2, Pallas kernels, up_gelu(): pl.pallas_call(up_body, grid=(width // tile,), out_shape=jax.ShapeDtypeSt...  13.1 us
    unnamed x29, local copies, waits for them, and re-layouts  12.3 us

profile of v1, /device:TPU:2, one launch (start us, length us, event | category | flops | bytes accessed | tf_op | source)
XLA Modules:
  0.0 305.4 jit_solution(660660470898855190)
XLA Ops:
  0.0 1.1 copy.31
  1.1 0.2 copy.32.refs_2_
  1.3 0.7 broadcast_in_dim.6.refs_1_
  1.9 0.0 copy-start
  1.9 1.0 copy-done
  3.0 0.0 copy-start.4
  3.0 0.8 copy-done.4
  3.8 50.0 %enter.1 = (bf16[1024,2048]{1,0:T(8,128)(2,1)S(1)}, s32[64,128]{1,0:T(8,128)S(1)}, bf16[2048,768]{1,0:T(8,128)(2,1)S(1)}, bf16[256,2048]{1,0:T(8,128)(2,1)S(1)}) custom-call(bf16[128,2048]{1,0:T(8,128)(2,1)S(1)} %copy-done, s32[8,128]{1,0:T(8,128)S(1)} %broadcast_in_dim.6.refs_1_, bf16[128,768]{1,0:T(8,128)(2,1)S(1)} %copy.32.refs_2_, ...), custom_call_target="tpu_custom_call" | custom-call | tf_op jit(solution)/shard_map/enter/pallas_call | solution.py:346
  53.9 0.0 copy-start.13
  53.9 0.6 convert_reduce_fusion
  54.5 1.2 fusion.3
  55.7 0.0 copy-done.13
  55.7 3.9 %fusion.21 = bf16[1024,768]{0,1:T(8,128)(2,1)S(1)} fusion(bf16[2048,768]{1,0:T(8,128)(2,1)S(1)} %get-tuple-element.14, bf16[1024,2048]{1,0:T(8,128)(2,1)S(1)} %get-tuple-element.13, f32[2048]{0:T(1024)S(1)} %copy-done.13, f32[1024]{0:T(1024)S(1)} %add_rsqrt_fusion, f32[1024]{0:T(1024)S(1)} %broadcast_multiply_fusion.1), kind=kOutput, calls=%fused_computation.26 | convolution fusion | flops 3232497664 | bytes 8929280 | tf_op jit(solution)/shard_map/dot_general | solution.py:442
  59.7 5.1 %fusion.55 = (f32[2,1024]{1,0:T(2,128)S(1)}, f32[2,1024,1024]{1,2,0:T(8,128)}) fusion(bf16[1024,2,3,128]{0,3,2,1:T(8,128)(2,1)S(1)} %bitcast.71), kind=kOutput, calls=%fused_computation.84 | convolution fusion | flops 543163392 | bytes 9445376 | tf_op jit(solution)/shard_map/sub | solution.py:481
  64.8 4.1 %fusion.24 = bf16[2,128,1024]{2,1,0:T(8,128)(2,1)S(1)} fusion(f32[2,1024,1024]{1,2,0:T(8,128)} %get-tuple-element.26, f32[2,1024]{1,0:T(2,128)S(1)} %get-tuple-element.25, bf16[1024,2,3,128]{0,3,2,1:T(8,128)(2,1)S(1)} %bitcast.72), kind=kOutput, calls=%fused_computation.30 | convolution fusion | flops 541327360 | bytes 9445376 | tf_op jit(solution)/shard_map/hqk,khd->qhd/dot_general | solution.py:483
  68.9 0.0 copy-start.2
  68.9 1.3 convolution_convert_fusion.refs_0_
  70.2 0.0 copy-done.2
  70.3 0.0 copy-start.1
  70.3 0.0 copy-start.12
  70.3 0.0 copy-start.3
  70.3 42.7 %heads.1 = (f32[128,2048]{1,0:T(8,128)S(1)}, bf16[2048,1024]{1,0:T(8,128)(2,1)S(1)}) custom-call(bf16[1024,2048]{1,0:T(8,128)(2,1)S(1)} %convolution_convert_fusion.refs_0_, bf16[128,1024]{1,0:T(8,128)(2,1)S(1)} %copy-done.2), custom_call_target="tpu_custom_call" | custom-call | tf_op jit(solution)/shard_map/heads/pallas_call | solution.py:346
  113.0 0.0 copy-start.6
  113.0 1.9 copy-done.6
  114.9 0.0 copy-done.1
  114.9 0.2 convert_reduce_fusion.1
  115.1 0.3 fusion.27
  115.4 0.0 copy-done.12
  115.4 0.4 fusion.29.refs_0_
  115.8 0.0 copy-done.3
  115.8 41.7 %norms.1 = (bf16[1024,2048]{1,0:T(8,128)(2,1)S(1)}, bf16[1024,2048]{1,0:T(8,128)(2,1)S(1)}) custom-call(bf16[128,2048]{1,0:T(8,128)(2,1)S(1)} %fusion.29.refs_0_, bf16[1024,128]{1,0:T(8,128)(2,1)S(1)} %copy-done.3), custom_call_target="tpu_custom_call" | custom-call | tf_op jit(solution)/shard_map/norms/pallas_call | solution.py:346
  157.5 0.0 copy-start.8
  157.5 2.0 copy-done.8
  159.5 0.0 copy-start.10
  159.5 2.0 copy-done.10
  161.5 0.1 copy.37
  161.6 2.5 select_reduce_fusion
  164.2 4.5 %convolution_convert_fusion.1 = bf16[512,2048]{1,0:T(8,128)(2,1)S(1)} fusion(bf16[1024,2048]{1,0:T(8,128)(2,1)} %copy-done.10, s32[1024]{0:T(1024)S(1)} %fusion.50), kind=kOutput, calls=%fused_computation.22 | convolution fusion | flops 2149056512 | bytes 6295552 | tf_op jit(solution)/shard_map/dot_general | solution.py:442
  168.7 35.1 %dispatch.1 = bf16[16,32,2048]{2,1,0:T(8,128)(2,1)S(1)} custom-call(bf16[16,32,2048]{2,1,0:T(8,128)(2,1)S(1)} %bitcast.63), custom_call_target="tpu_custom_call" | custom-call | tf_op jit(solution)/shard_map/dispatch/pallas_call | solution.py:388
  203.9 0.0 copy-start.5
  203.9 3.4 %copy-done.5 = bf16[1,2048,2048]{2,1,0:T(8,128)(2,1)S(1)} copy-done((bf16[1,2048,2048]{2,1,0:T(8,128)(2,1)S(1)}, bf16[1,2048,2048]{2,1,0:T(8,128)(2,1)}, u32[]{:S(2)}) %copy-start.5) | copy-done | bytes 8388632
  207.2 7.2 %up_gelu.3 = bf16[512,2048]{1,0:T(8,128)(2,1)S(1)} custom-call(bf16[512,2048]{1,0:T(8,128)(2,1)S(1)} %bitcast.61, bf16[2048,2048]{1,0:T(8,128)(2,1)S(1)} %bitcast.65), custom_call_target="tpu_custom_call" | custom-call | flops 4294967296 | bytes 12582912 | tf_op jit(solution)/shard_map/up_gelu/pallas_call | solution.py:415
  214.5 0.0 copy-start.11
  214.5 8.5 %fusion.18 = bf16[512,2048]{1,0:T(8,128)(2,1)S(1)} fusion(bf16[512,2048]{1,0:T(8,128)(2,1)S(1)} %up_gelu.3, bf16[1,2048,2048]{2,1,0:T(8,128)(2,1)} %param.19), kind=kOutput, calls=%fused_computation.23 | convolution fusion | flops 4296015872 | bytes 12582912 | tf_op jit(solution)/shard_map/dot_general | solution.py:442
  223.0 0.0 copy-start.7
  223.0 36.5 %collect.1 = bf16[16,32,2048]{2,1,0:T(8,128)(2,1)S(1)} custom-call(bf16[16,32,2048]{2,1,0:T(8,128)(2,1)S(1)} %bitcast.62), custom_call_target="tpu_custom_call" | custom-call | tf_op jit(solution)/shard_map/collect/pallas_call | solution.py:388
  259.5 0.0 copy-done.11
  259.5 0.0 copy-done.7
  259.5 0.0 copy-start.9
  259.5 5.9 %up_gelu.2 = bf16[1024,1024]{1,0:T(8,128)(2,1)S(1)} custom-call(bf16[1024,2048]{1,0:T(8,128)(2,1)S(1)} %copy-done.11, bf16[2048,1024]{1,0:T(8,128)(2,1)S(1)} %copy-done.7), custom_call_target="tpu_custom_call" | custom-call | flops 4294967296 | bytes 10485760 | tf_op jit(solution)/shard_map/up_gelu/pallas_call | solution.py:415
  265.4 0.0 copy-done.9
  265.4 4.5 %fusion.56 = f32[1024,2048]{1,0:T(8,128)S(1)} fusion(bf16[1024,1024]{1,0:T(8,128)(2,1)S(1)} %up_gelu.2, bf16[1024,2048]{1,0:T(8,128)(2,1)S(1)} %copy-done.9), kind=kOutput, calls=%fused_computation.85 | convolution fusion | flops 4294967296 | bytes 14680064 | tf_op jit(solution)/shard_map/dot_general | solution.py:442
  270.0 2.5 add_convert_fusion.refs_0_
  272.5 32.0 %leave.1 = f32[128,2048]{1,0:T(8,128)S(1)} custom-call(bf16[1024,2048]{1,0:T(8,128)(2,1)S(1)} %add_convert_fusion.refs_0_), custom_call_target="tpu_custom_call" | custom-call | tf_op jit(solution)/shard_map/leave/pallas_call | solution.py:346
  304.5 0.9 fusion.30
  (7 shorter events, 0.1 us)
Async XLA Ops:
  1.9 1.0 copy-start
  3.0 0.8 copy-start.4
  53.9 1.9 copy-start.13
  68.9 1.3 copy-start.2
  70.3 44.6 %copy-start.1 = (bf16[128,2048]{1,0:T(8,128)(2,1)S(1)}, bf16[128,2048]{1,0:T(8,128)(2,1)}, u32[]{:S(2)}) copy-start(bf16[128,2048]{1,0:T(8,128)(2,1)} %refs_0_.1) | copy-start | bytes 1572868
  70.3 45.2 %copy-start.12 = (f32[2048]{0:T(1024)S(1)}, f32[2048]{0:T(1024)}, u32[]{:S(2)}) copy-start(f32[2048]{0:T(1024)} %param.14) | copy-start | bytes 24580
  70.3 45.5 %copy-start.3 = (bf16[1024,128]{1,0:T(8,128)(2,1)S(1)}, bf16[1024,128]{1,0:T(8,128)(2,1)}, u32[]{:S(2)}) copy-start(bf16[1024,128]{1,0:T(8,128)(2,1)} %refs_1_.3) | copy-start | bytes 786436
  113.0 1.9 copy-start.6
  157.5 2.0 copy-start.8
  159.5 2.0 copy-start.10
  203.9 3.4 %copy-start.5 = (bf16[1,2048,2048]{2,1,0:T(8,128)(2,1)S(1)}, bf16[1,2048,2048]{2,1,0:T(8,128)(2,1)}, u32[]{:S(2)}) copy-start(bf16[1,2048,2048]{2,1,0:T(8,128)(2,1)} %param.18) | copy-start | bytes 25165828
  214.5 45.0 %copy-start.11 = (bf16[1024,2048]{1,0:T(8,128)(2,1)S(1)}, bf16[1024,2048]{1,0:T(8,128)(2,1)}, u32[]{:S(2)}) copy-start(bf16[1024,2048]{1,0:T(8,128)(2,1)} %copy-done.10) | copy-start | bytes 12582916
  223.0 36.5 %copy-start.7 = (bf16[2048,1024]{1,0:T(8,128)(2,1)S(1)}, bf16[2048,1024]{1,0:T(8,128)(2,1)}, u32[]{:S(2)}) copy-start(bf16[2048,1024]{1,0:T(8,128)(2,1)} %copy-done.6) | copy-start | bytes 12582916
  259.5 5.9 %copy-start.9 = (bf16[1024,2048]{1,0:T(8,128)(2,1)S(1)}, bf16[1024,2048]{1,0:T(8,128)(2,1)}, u32[]{:S(2)}) copy-start(bf16[1024,2048]{1,0:T(8,128)(2,1)} %copy-done.8) | copy-start | bytes 12582916

commit v2 on v1

--- a/solution.py
+++ b/solution.py
@@ -37,8 +37,10 @@
             "z": (high, y, core, x, 1 - low),
             "y+": (high, y + 1, core, x, low),
             "y-": (high, y - 1, core, x, low),
-            "h": (1 - high, y, core, x, low),
+            "w": (1 - high, y, core, x, 1 - low),
             "c": (high, y, 1 - core, x, low),
+            "y+c": (high, y + 1, 1 - core, x, low),
+            "y-c": (high, y - 1, 1 - core, x, low),
         }[name]
         return self.row_of(*at[:3]), self.col_of(*at[3:])
 
@@ -160,7 +162,7 @@
     out[pl.ds(pl.multiple_of(net.col * size, size), size), :] = src[...]
 
 
-def gather(net, src, out, axis, early, late):
+def gather(net, src, out, relay, axis, early, late):
     depth, width = src.shape
     high, y, core = net.high, net.y, net.core
     middle = depth // 2
@@ -190,14 +192,25 @@
             net.when(time, arrival, lambda dy=dy: from_y(dy, other))
 
     around(0, src, early + 0.5)
+    span = late - early
+    waiting = [2]
+
+    def arrived():
+        waiting[0] -= 1
+        if waiting[0] == 0:
+            around(1, part(0, 1, core), early + 0.6 * span)
+            to_core(0, 1)
+
+    for half, first, second in ((0, "z", "w"), (1, "w", "z")):
+        arrival = net.copy(src.at[pl.ds(half * middle, middle)], relay.at[half], relay.at[half], first)
+
+        def onward(half=half, second=second):
+            got = relay.at[half]
+            arrival = net.copy(got, part(0, half, core, half), part(0, 1, core, half), second)
+            net.when(early + 0.45 * span, arrival, arrived)
+
+        net.when(early + 0.2 * span, arrival, onward)
     mine = part(0, 0, core)
-    arrival = net.copy(src, mine, part(0, 1, core), "h")
-
-    def from_high():
-        around(1, part(0, 1, core), early + 0.6 * (late - early))
-        to_core(0, 1)
-
-    net.when(early + 0.3 * (late - early), arrival, from_high)
     net.when(late, net.copy(src, mine, part(0, 0, 1 - core), "c"))
     index = net.row
     if axis == 0:
@@ -301,11 +314,12 @@
     if spreads or smalls or sums:
         names += ["x+", "x-", "z"]
     if gathers:
-        names += ["y+", "y-", "h", "c"]
+        names += ["y+", "y-", "w", "c"] + ([] if names else ["z"])
     net.greet(names)
+    relays = list(scratch[10 * sums :])
     k = 0
     for _ in range(sums):
-        reduce_scatter(net, ins[k], outs[k], scratch)
+        reduce_scatter(net, ins[k], outs[k], scratch[:10])
         k += 1
     for _ in range(spreads):
         spread(net, ins[k], outs[k])
@@ -314,7 +328,7 @@
         spread_small(net, ins[k], outs[k])
         k += 1
     for axis, early, late in gathers:
-        gather(net, ins[k], outs[k], axis, early, late)
+        gather(net, ins[k], outs[k], relays.pop(0), axis, early, late)
         k += 1
     net.run()
 
@@ -342,7 +356,8 @@
         arrays.append(array)
         shape = (depth * row_total, width) if axis == 0 else (depth, width * row_total)
         shapes.append(jax.ShapeDtypeStruct(shape, array.dtype))
-        copies += 20
+        scratch.append(pltpu.VMEM((2, depth // 2, width), array.dtype))
+        copies += 22
     return pl.pallas_call(
         functools.partial(comm_body, len(spreads), len(smalls), [g[1:] for g in gathers], len(sums)),
         out_shape=shapes,
@@ -356,51 +371,140 @@
     )(*arrays)
 
 
-def shuffle_body(sign, row_total, source, out, stage, send, recv, local):
-    row = lax.axis_index("row")
-    col = lax.axis_index("col")
-    barrier = pltpu.get_barrier_semaphore()
-    for step in range(1, row_total):
-        pl.semaphore_signal(
-            barrier, inc=1, device_id=(lax.rem(row + step, row_total), col), device_id_type=MESH
-        )
-    load = pltpu.make_async_copy(source, stage, local.at[0])
-    load.start()
-    pl.semaphore_wait(barrier, row_total - 1)
-    load.wait()
-    copies = []
-    for step in range(1, row_total):
-        to = lax.rem(row + (step if sign > 0 else row_total - step), row_total)
-        copy = pltpu.make_async_remote_copy(
-            stage.at[step], out.at[step], send.at[step - 1], recv.at[step - 1], device_id=(to, col), device_id_type=MESH
-        )
-        copy.start()
-        copies.append(copy)
-    own = pltpu.make_async_copy(stage.at[0], out.at[0], local.at[1])
-    own.start()
-    for copy in copies:
-        copy.wait()
-    own.wait()
-
-
-def shuffle(name, collective_id, array, sign):
-    row_total = lax.axis_size("row")
+def y_exchange(net, src, dst, relay, times, ready=None, arrived=None):
+    core = net.core
+    half = src.shape[2] // 2
+    tell = arrived or (lambda d: None)
+
+    def opposite():
+        for index, forward in ((0, "y+"), (1, "y-")):
+            rows = pl.ds(index * half, half)
+            arrival = net.copy(src.at[2, :, rows], relay.at[index], relay.at[index], forward)
+
+            def onward(index=index, forward=forward, rows=rows):
+                for c, name in ((core, forward), (1 - core, forward + "c")):
+                    arrival = net.copy(relay.at[index, c], dst.at[2, core, rows], dst.at[2, c, rows], name)
+                    net.when(times[3], arrival, lambda: tell(2))
+
+            net.when(times[1], arrival, onward)
+
+    def beside(d):
+        forward = "y+" if d == 1 else "y-"
+        for c, name in ((core, forward), (1 - core, forward + "c")):
+            arrival = net.copy(src.at[d, c], dst.at[4 - d, core], dst.at[4 - d, c], name)
+            net.when(times[2], arrival, lambda: tell(4 - d))
+
+    def here():
+        net.when(times[2], net.copy(src.at[0, 1 - core], dst.at[0, core], dst.at[0, 1 - core], "c"), lambda: tell(0))
+        dst[0, core] = src[0, core]
+
+    steps = {2: opposite, 1: lambda: beside(1), 3: lambda: beside(3), 0: here}
+    if ready is None:
+        for d in (2, 1, 3, 0):
+            steps[d]()
+    else:
+        ready(steps)
+
+
+def dispatch_body(x_ref, w_ref, table, hidden, out, far, relay, send, recv):
+    net = Net(send, recv)
+    net.greet(["y+", "y-", "y+c", "y-c", "c", "z", "w"])
+    low = net.low
+    half = table.shape[3] // 2
+    mine, theirs = pl.ds(pl.multiple_of(low * half, half), half), pl.ds(pl.multiple_of((1 - low) * half, half), half)
+
+    def ready(steps):
+        for k, d in enumerate((2, 1, 3, 0)):
+            arrival = net.copy(table.at[1, d, :, mine], far.at[d, :, mine], far.at[d, :, theirs], "w")
+
+            def onward(k=k, d=d):
+                arrival = net.copy(far.at[d, :, theirs], far.at[d, :, theirs], far.at[d, :, mine], "z")
+                net.when(7.0 + 2.5 * k, arrival, steps[d])
+
+            net.when(3.5 + 2.5 * k, arrival, onward)
+
+    y_exchange(net, table.at[0], out.at[0], relay.at[0], (0.0, 5.0, 12.0, 16.0))
+    y_exchange(net, far, out.at[1], relay.at[1], (0.0, 17.0, 24.0, 25.0), ready)
+    up_tasks(net, x_ref, w_ref, hidden, 1.0, 1.2)
+    net.run()
+
+
+def up_tasks(net, x_ref, w_ref, out, start, every):
+    rows, width = out.shape
+    tile = min(256, rows)
+    span = min(256, width)
+
+    def piece(j):
+        columns = pl.ds(j * span, span)
+
+        @pl.loop(0, rows // tile)
+        def _(i):
+            at = pl.ds(pl.multiple_of(i * tile, tile), tile)
+            inner = jnp.dot(x_ref[at, :], w_ref[:, columns], preferred_element_type=jnp.float32)
+            out[at, columns] = (inner * (1.0 + lax.erf(inner * (0.5**0.5))) * 0.5).astype(out.dtype)
+
+    for j in range(width // span):
+        net.at(start + every * j, lambda j=j: piece(j))
+
+
+def down_tasks(net, x_ref, w_ref, out, start, every):
+    rows, width = out.shape
+    tile = min(256, rows)
+    span = min(512, width)
+
+    def piece(j):
+        columns = pl.ds(j * span, span)
+
+        @pl.loop(0, rows // tile)
+        def _(i):
+            at = pl.ds(pl.multiple_of(i * tile, tile), tile)
+            product = jnp.dot(x_ref[at, :], w_ref[:, columns], preferred_element_type=jnp.float32)
+            out[at, columns] = product.astype(out.dtype)
+
+    for j in range(width // span):
+        net.at(start + every * j, lambda j=j: piece(j))
+
+
+def collect_body(x_ref, w_ref, parts, dense, near, across, far, other, total, relay, send, recv):
+    net = Net(send, recv)
+    net.greet(["y+", "y-", "y+c", "y-c", "c", "z", "w"])
+    low = net.low
+    half = parts.shape[3] // 2
+    mine, theirs = pl.ds(pl.multiple_of(low * half, half), half), pl.ds(pl.multiple_of((1 - low) * half, half), half)
+    left = {0: 1, 1: 2, 2: 4, 3: 2}
+    after = {0: 9.0, 1: 13.0, 3: 15.0, 2: 18.0}
+
+    def arrived(d):
+        left[d] -= 1
+        if left[d]:
+            return
+
+        def add():
+            total[d] = far[d, :, theirs] + other[d]
+            net.when(27.0, net.copy(total.at[d], across.at[d], across.at[d], "w"))
+
+        net.when(after[d], net.copy(far.at[d, :, mine], other.at[d], other.at[d], "z"), add)
+
+    y_exchange(net, parts.at[1], far, relay.at[1], (0.0, 5.0, 9.0, 14.0), None, arrived)
+    y_exchange(net, parts.at[0], near, relay.at[0], (0.0, 14.5, 22.0, 25.0))
+    down_tasks(net, x_ref, w_ref, dense, 0.5, 2.0)
+    net.run()
+
+
+def expert_call(name, body, collective_id, arrays, shapes, scratch):
+    copies = 40
     return pl.pallas_call(
-        functools.partial(shuffle_body, sign, row_total),
-        out_shape=jax.ShapeDtypeStruct(array.shape, array.dtype),
-        in_specs=[pl.BlockSpec(memory_space=pl.ANY)],
-        out_specs=pl.BlockSpec(memory_space=pl.ANY),
-        scratch_shapes=[
-            pltpu.VMEM(array.shape, array.dtype),
-            pltpu.SemaphoreType.DMA((row_total - 1,)),
-            pltpu.SemaphoreType.DMA((row_total - 1,)),
-            pltpu.SemaphoreType.DMA((2,)),
-        ],
+        body,
+        out_shape=[jax.ShapeDtypeStruct(shape, jnp.bfloat16) for shape in shapes],
+        in_specs=[pl.BlockSpec(memory_space=pltpu.VMEM)] * len(arrays),
+        out_specs=[pl.BlockSpec(memory_space=pltpu.VMEM)] * len(shapes),
+        scratch_shapes=[pltpu.VMEM(shape, jnp.bfloat16) for shape in scratch]
+        + [pltpu.SemaphoreType.DMA((copies,)), pltpu.SemaphoreType.DMA((copies,))],
         compiler_params=pltpu.CompilerParams(
-            collective_id=collective_id, has_side_effects=True, vmem_limit_bytes=24 * 2**20
+            collective_id=collective_id, has_side_effects=True, vmem_limit_bytes=48 * 2**20
         ),
         name=name,
-    )(array)
+    )(*arrays)
 
 
 def up_body(x_ref, w_ref, o_ref):
@@ -499,25 +603,45 @@
     block_index = jnp.arange(col_total, dtype=jnp.int32)[:, None]
     home_row = 2 * ids_rows // col_total
     mine = (2 * ids_rows % col_total) // 2 == col_index // 2
-    step = (home_row - row_index + row_total) % row_total
-    position = (step * col_total + block_index) * capacity + slot_index
-    position = jnp.where(mine, position, -1).reshape(seq_len)
-    slot_count = row_total * col_total * capacity
+    other = (home_row // 8 != row_index // 8).astype(jnp.int32)
+    step = (home_row // 2 - row_index // 2 + 8) % 4
+    chunk = step * 2 + home_row % 2
+    place = block_index * capacity + slot_index
+    rows = col_total * capacity
+    position = jnp.where(mine, (other * 8 + chunk) * rows + place, -1).reshape(seq_len)
+    slot_count = row_total * rows
     slots = jnp.arange(slot_count, dtype=jnp.int32)
     placing = (slots[:, None] == position[None, :]).astype(jnp.bfloat16)
-    picking = (position[:, None] == slots[None, :]).astype(jnp.bfloat16)
+    half = rows // 2
+    crossed = jnp.where(place // half == col_index % 2, 8 * rows + chunk * half + place % half, -1)
+    source = jnp.where(mine, jnp.where(other == 1, crossed, chunk * rows + place), -1).reshape(seq_len)
+    returned_slots = jnp.arange(8 * (rows + half), dtype=jnp.int32)
+    picking = (source[:, None] == returned_slots[None, :]).astype(jnp.bfloat16)
 
     table = matmul(placing, normed_image).astype(jnp.bfloat16)
-    table = table.reshape(row_total, col_total * capacity, model_width)
-    expert_rows = shuffle("dispatch", 3, table, 1)
+    table = table.reshape(2, 4, 2, rows, model_width)
+    full, part = (4, 2, rows, model_width), (4, 2, half, model_width)
+    relays = (2, 2, 2, half, model_width)
+    hidden_units, expert_rows = expert_call(
+        "dispatch",
+        dispatch_body,
+        3,
+        (normed_image, up_whole, table),
+        ((seq_len, up_whole.shape[1]), table.shape),
+        (full, relays),
+    )
     expert_units = up_gelu(expert_rows.reshape(slot_count, model_width), expert_in[0])
-    partial_out = matmul(expert_units, expert_out[0]).astype(jnp.bfloat16)
-    partial_out = partial_out.reshape(row_total, col_total * capacity, model_width)
-    returned = shuffle("collect", 4, partial_out, -1)
-
-    hidden_units = up_gelu(normed_image, up_whole)
-    rows_two = returned.reshape(slot_count, model_width)
-    partial = matmul(hidden_units, down_whole) + matmul(picking, rows_two)
+    partial_out = matmul(expert_units, expert_out[0]).astype(jnp.bfloat16).reshape(table.shape)
+    dense, near, across = expert_call(
+        "collect",
+        collect_body,
+        4,
+        (hidden_units, down_whole, partial_out),
+        ((seq_len, model_width), full, part),
+        (full, part, part, relays),
+    )
+    rows_two = jnp.concatenate((near.reshape(-1, model_width), across.reshape(-1, model_width)))
+    partial = dense.astype(jnp.float32) + matmul(picking, rows_two)
     (total,) = exchange("leave", 5, sums=(partial.astype(jnp.bfloat16),))
     return (hidden_mine.astype(jnp.float32) + total).astype(jnp.bfloat16)
 

time: 308 us -> 315 us (1.023)
  Pallas kernels: 251 us -> 268 us
  local copies, waits for them, and re-layouts: 13.2 us -> 9.32 us
  matrix products: 34.5 us -> 31.1 us
    pallas_call x4, Pallas kernels: 166 us -> 186 us  [exchange(): pl.pallas_call(functools.partial(comm_body, len(spreads), len(smalls), [g...]
    pallas_call x2 -> x1, Pallas kernels: 13.1 us -> 7.24 us  [up_gelu(): pl.pallas_call(up_body, grid=(width // tile,), out_shape=jax.ShapeDtypeSt...]
    unnamed x29 -> x23, local copies, waits for them, and re-layouts: 12.3 us -> 8.36 us
    dot_general x6 -> x5, matrix products: 25.3 us -> 21.8 us  [matmul(): return jnp.dot(a, b, preferred_element_type=jnp.float32)]
where the time goes in v2:
time: 315 us
  Pallas kernels  268 us (85%)
  matrix products  31.1 us (10%)
  local copies, waits for them, and re-layouts  9.32 us (3%)
  other arithmetic  6.28 us (2%)
    pallas_call x4, Pallas kernels, exchange(): pl.pallas_call(functools.partial(comm_body, len(spreads), len(smalls), [g...  186 us
    pallas_call x2, Pallas kernels, expert_call(): pl.pallas_call(body, out_shape=[jax.ShapeDtypeStruct(shape, jnp.bfloat16)...  74.1 us
    dot_general x5, matrix products, matmul(): return jnp.dot(a, b, preferred_element_type=jnp.float32)  21.8 us
    unnamed x23, local copies, waits for them, and re-layouts  8.36 us
    pallas_call x1, Pallas kernels, up_gelu(): pl.pallas_call(up_body, grid=(width // tile,), out_shape=jax.ShapeDtypeSt...  7.24 us

profile of v2, /device:TPU:2, one launch (start us, length us, event | category | flops | bytes accessed | tf_op | source)
XLA Modules:
  0.0 314.5 jit_solution(5784519031504832208)
XLA Ops:
  0.0 0.7 broadcast_in_dim.8.refs_1_
  0.7 1.1 copy.39
  1.8 0.2 copy.40.refs_2_
  1.9 0.0 copy-start.3
  1.9 1.0 copy-done.3
  3.0 0.0 copy-start.7
  3.0 0.8 copy-done.7
  3.8 58.0 %enter.1 = (bf16[1024,2048]{1,0:T(8,128)(2,1)S(1)}, s32[64,128]{1,0:T(8,128)S(1)}, bf16[2048,768]{1,0:T(8,128)(2,1)S(1)}, bf16[256,2048]{1,0:T(8,128)(2,1)S(1)}) custom-call(bf16[128,2048]{1,0:T(8,128)(2,1)S(1)} %copy-done.3, s32[8,128]{1,0:T(8,128)S(1)} %broadcast_in_dim.8.refs_1_, bf16[128,768]{1,0:T(8,128)(2,1)S(1)} %copy.40.refs_2_, ...), custom_call_target="tpu_custom_call" | custom-call | tf_op jit(solution)/shard_map/enter/pallas_call | solution.py:361
  61.8 0.0 copy-start.10
  61.9 0.6 convert_reduce_fusion
  62.5 1.2 fusion.3
  63.7 0.0 copy-done.10
  63.7 3.9 %fusion.21 = bf16[1024,768]{0,1:T(8,128)(2,1)S(1)} fusion(bf16[2048,768]{1,0:T(8,128)(2,1)S(1)} %get-tuple-element.19, bf16[1024,2048]{1,0:T(8,128)(2,1)S(1)} %get-tuple-element.18, f32[2048]{0:T(1024)S(1)} %copy-done.10, f32[1024]{0:T(1024)S(1)} %add_rsqrt_fusion, f32[1024]{0:T(1024)S(1)} %broadcast_multiply_fusion.1), kind=kOutput, calls=%fused_computation.25 | convolution fusion | flops 3232497664 | bytes 8929280 | tf_op jit(solution)/shard_map/dot_general | solution.py:546
  67.7 0.1 copy.45
  67.8 2.5 select_reduce_fusion
  70.3 0.1 fusion.57
  70.4 5.1 %fusion.68 = (f32[2,1024]{1,0:T(2,128)S(1)}, f32[2,1024,1024]{1,2,0:T(8,128)}) fusion(bf16[1024,2,3,128]{0,3,2,1:T(8,128)(2,1)S(1)} %bitcast.90), kind=kOutput, calls=%fused_computation.117 | convolution fusion | flops 543163392 | bytes 9445376 | tf_op jit(solution)/shard_map/sub | solution.py:585
  75.6 4.2 %fusion.27 = bf16[2,128,1024]{2,1,0:T(8,128)(2,1)S(1)} fusion(f32[2,1024,1024]{1,2,0:T(8,128)} %get-tuple-element.38, f32[2,1024]{1,0:T(2,128)S(1)} %get-tuple-element.37, bf16[1024,2,3,128]{0,3,2,1:T(8,128)(2,1)S(1)} %bitcast.91), kind=kOutput, calls=%fused_computation.33 | convolution fusion | flops 541327360 | bytes 9445376 | tf_op jit(solution)/shard_map/hqk,khd->qhd/dot_general | solution.py:587
  79.7 0.0 copy-start.5
  79.8 1.3 convolution_convert_fusion.refs_0_
  81.1 0.0 copy-done.5
  81.1 0.0 copy-start.4
  81.1 0.0 copy-start.9
  81.1 0.0 copy-start.6
  81.1 43.1 %heads.1 = (f32[128,2048]{1,0:T(8,128)S(1)}, bf16[2048,1024]{1,0:T(8,128)(2,1)S(1)}) custom-call(bf16[1024,2048]{1,0:T(8,128)(2,1)S(1)} %convolution_convert_fusion.refs_0_, bf16[128,1024]{1,0:T(8,128)(2,1)S(1)} %copy-done.5), custom_call_target="tpu_custom_call" | custom-call | tf_op jit(solution)/shard_map/heads/pallas_call | solution.py:361
  124.2 0.0 copy-start
  124.2 2.0 copy-done
  126.2 0.0 copy-done.4
  126.2 0.2 convert_reduce_fusion.1
  126.4 0.3 fusion.30
  126.7 0.0 copy-done.9
  126.7 0.4 fusion.32.refs_0_
  127.1 0.0 copy-done.6
  127.1 48.1 %norms.1 = (bf16[1024,2048]{1,0:T(8,128)(2,1)S(1)}, bf16[1024,2048]{1,0:T(8,128)(2,1)S(1)}) custom-call(bf16[128,2048]{1,0:T(8,128)(2,1)S(1)} %fusion.32.refs_0_, bf16[1024,128]{1,0:T(8,128)(2,1)S(1)} %copy-done.6), custom_call_target="tpu_custom_call" | custom-call | tf_op jit(solution)/shard_map/norms/pallas_call | solution.py:361
  175.2 0.0 copy-start.1
  175.3 0.0 copy-start.2
  175.3 3.9 %convolution_convert_fusion.1 = bf16[512,2048]{1,0:T(8,128)(2,1)} fusion(bf16[1024,2048]{1,0:T(8,128)(2,1)S(1)} %get-tuple-element.22.x_ref, s32[1024]{0:T(1024)S(1)} %get-tuple-element.36), kind=kOutput, calls=%fused_computation.22 | convolution fusion | flops 2149056512 | bytes 6295552 | tf_op jit(solution)/shard_map/dot_general | solution.py:546
  179.2 0.0 copy-done.1
  179.2 0.0 copy-done.2
  179.2 32.4 %dispatch.1 = (bf16[1024,1024]{1,0:T(8,128)(2,1)S(1)}, bf16[2,4,2,32,2048]{4,3,2,1,0:T(8,128)(2,1)S(1)}) custom-call(bf16[1024,2048]{1,0:T(8,128)(2,1)} %copy-done.2, bf16[2048,1024]{1,0:T(8,128)(2,1)} %copy-done, bf16[2,4,2,32,2048]{4,3,2,1,0:T(8,128)(2,1)} %bitcast.84), custom_call_target="tpu_custom_call" | custom-call | tf_op jit(solution)/shard_map/dispatch/pallas_call | solution.py:496
  211.7 0.0 copy-start.8
  211.7 3.4 %copy-done.8 = bf16[1,2048,2048]{2,1,0:T(8,128)(2,1)S(1)} copy-done((bf16[1,2048,2048]{2,1,0:T(8,128)(2,1)S(1)}, bf16[1,2048,2048]{2,1,0:T(8,128)(2,1)}, u32[]{:S(2)}) %copy-start.8) | copy-done | bytes 8388632
  215.0 7.2 %up_gelu.1 = bf16[512,2048]{1,0:T(8,128)(2,1)S(1)} custom-call(bf16[512,2048]{1,0:T(8,128)(2,1)S(1)} %bitcast.81, bf16[2048,2048]{1,0:T(8,128)(2,1)S(1)} %bitcast.80), custom_call_target="tpu_custom_call" | custom-call | flops 4294967296 | bytes 12582912 | tf_op jit(solution)/shard_map/up_gelu/pallas_call | solution.py:519
  222.3 8.3 %fusion.18 = bf16[512,2048]{1,0:T(8,128)(2,1)S(1)} fusion(bf16[512,2048]{1,0:T(8,128)(2,1)S(1)} %up_gelu.1, bf16[1,2048,2048]{2,1,0:T(8,128)(2,1)} %param.19), kind=kOutput, calls=%fused_computation.23 | convolution fusion | flops 4296015872 | bytes 12582912 | tf_op jit(solution)/shard_map/dot_general | solution.py:546
  230.6 41.7 %collect.1 = (bf16[1024,2048]{1,0:T(8,128)(2,1)}, bf16[4,2,32,2048]{3,2,1,0:T(8,128)(2,1)S(1)}, bf16[4,2,16,2048]{3,2,1,0:T(8,128)(2,1)S(1)}) custom-call(bf16[1024,1024]{1,0:T(8,128)(2,1)S(1)} %get-tuple-element.25.x_ref, bf16[1024,2048]{1,0:T(8,128)(2,1)} %copy-done.1, bf16[2,4,2,32,2048]{4,3,2,1,0:T(8,128)(2,1)S(1)} %bitcast.78), custom_call_target="tpu_custom_call" | custom-call | tf_op jit(solution)/shard_map/collect/pallas_call | solution.py:496
  272.3 4.3 %add_convert_fusion.refs_0_ = bf16[1024,2048]{1,0:T(8,128)(2,1)S(1)} fusion(bf16[1024,2048]{1,0:T(8,128)(2,1)} %get-tuple-element.28, bf16[128,2048]{1,0:T(8,128)(2,1)S(1)} %bitcast.83, bf16[256,2048]{1,0:T(8,128)(2,1)S(1)} %bitcast.82, s32[1024]{0:T(1024)S(1)} %get-tuple-element.35), kind=kOutput, calls=%fused_computation.10 | convolution fusion | flops 1620443136 | bytes 9965568 | tf_op jit(solution)/shard_map/dot_general | solution.py:546
  276.6 37.0 %leave.1 = f32[128,2048]{1,0:T(8,128)S(1)} custom-call(bf16[1024,2048]{1,0:T(8,128)(2,1)S(1)} %add_convert_fusion.refs_0_), custom_call_target="tpu_custom_call" | custom-call | tf_op jit(solution)/shard_map/leave/pallas_call | solution.py:361
  313.6 0.9 fusion.33
  (7 shorter events, 0.1 us)
Async XLA Ops:
  1.9 1.0 copy-start.3
  3.0 0.8 copy-start.7
  61.8 1.9 copy-start.10
  79.7 1.3 copy-start.5
  81.1 45.1 %copy-start.4 = (bf16[128,2048]{1,0:T(8,128)(2,1)S(1)}, bf16[128,2048]{1,0:T(8,128)(2,1)}, u32[]{:S(2)}) copy-start(bf16[128,2048]{1,0:T(8,128)(2,1)} %refs_0_.1) | copy-start | bytes 1572868
  81.1 45.7 %copy-start.9 = (f32[2048]{0:T(1024)S(1)}, f32[2048]{0:T(1024)}, u32[]{:S(2)}) copy-start(f32[2048]{0:T(1024)} %param.14) | copy-start | bytes 24580
  81.1 46.0 %copy-start.6 = (bf16[1024,128]{1,0:T(8,128)(2,1)S(1)}, bf16[1024,128]{1,0:T(8,128)(2,1)}, u32[]{:S(2)}) copy-start(bf16[1024,128]{1,0:T(8,128)(2,1)} %refs_1_.3) | copy-start | bytes 786436
  124.2 2.0 copy-start
  175.2 4.0 %copy-start.1 = (bf16[1024,2048]{1,0:T(8,128)(2,1)}, bf16[1024,2048]{1,0:T(8,128)(2,1)S(1)}, u32[]{:S(2)}) copy-start(bf16[1024,2048]{1,0:T(8,128)(2,1)S(1)} %get-tuple-element.26.w_ref) | copy-start | bytes 12582916
  175.3 4.0 %copy-start.2 = (bf16[1024,2048]{1,0:T(8,128)(2,1)}, bf16[1024,2048]{1,0:T(8,128)(2,1)S(1)}, u32[]{:S(2)}) copy-start(bf16[1024,2048]{1,0:T(8,128)(2,1)S(1)} %get-tuple-element.22.x_ref) | copy-start | bytes 12582916
  211.7 3.4 %copy-start.8 = (bf16[1,2048,2048]{2,1,0:T(8,128)(2,1)S(1)}, bf16[1,2048,2048]{2,1,0:T(8,128)(2,1)}, u32[]{:S(2)}) copy-start(bf16[1,2048,2048]{2,1,0:T(8,128)(2,1)} %param.18) | copy-start | bytes 25165828

commit v3 on v2

--- a/solution.py
+++ b/solution.py
@@ -1,5 +1,6 @@
 import functools
 import heapq
+import math
 import jax
 import jax.numpy as jnp
 from jax import lax
@@ -22,6 +23,9 @@
         self.finish = []
         self.queue = []
         self.serial = 0
+        self.now = 0.0
+        self.free = {}
+        self.spare = []
 
     def row_of(self, high, y, core):
         return high * 8 + lax.rem(y + 8, 4) * 2 + core
@@ -59,23 +63,38 @@
         out, arrival = make(dst), make(arriving)
         out.start()
         self.finish.append(out)
-        return arrival
-
-    def at(self, time, action):
-        heapq.heappush(self.queue, (time, self.serial, action))
-        self.serial += 1
-
-    def when(self, time, arrival, action=None):
+        rate, delay = (600e3, 1.0) if name == "c" else (46e3, 2.0)
+        begin = max(self.now, self.free.get(name[:2], 0.0))
+        self.free[name[:2]] = begin + math.prod(arriving.shape) * arriving.dtype.itemsize / rate
+        return arrival, self.free[name[:2]] + delay
+
+    def when(self, pending, action=None):
+        arrival, time = pending
+
         def run():
             arrival.wait_recv()
             if action is not None:
                 action()
 
-        self.at(time, run)
+        heapq.heappush(self.queue, (time, self.serial, run))
+        self.serial += 1
+
+    def work(self, time, action):
+        self.spare.append((time, action))
+
+    def spend(self, time):
+        self.now += time
 
     def run(self):
-        while self.queue:
-            heapq.heappop(self.queue)[2]()
+        while self.queue or self.spare:
+            if self.spare and (not self.queue or self.queue[0][0] > self.now + 0.5 * self.spare[0][0]):
+                time, action = self.spare.pop(0)
+                action()
+                self.now += time
+                continue
+            time, _, action = heapq.heappop(self.queue)
+            self.now = max(self.now, time) + 0.02
+            action()
         for out in self.finish:
             out.wait_send()
 
@@ -104,38 +123,38 @@
         start = 0 if step > 0 else half_a
         got = part(at, 0, start, half_a)
         far = net.copy(got, got, part(at - step, 0, start, half_a), forward)
-        net.when(6.0, far, lambda: to_z(part(2, 0, start, half_a), part(2, 1, start, half_a)))
+        net.when(far, lambda: to_z(part(2, 0, start, half_a), part(2, 1, start, half_a)))
         to_z(part(at, 0, 0, a), part(at, 1, 0, a))
 
     def to_z(got, arriving):
-        net.when(27.0, net.copy(got, got, arriving, "z"))
+        net.when(net.copy(got, got, arriving, "z"))
 
     def from_b(side, other):
         step = 1 if side == "x-" else -1
         start = a if step > 0 else a + half_b
         got = part(-step, other, start, half_b)
         forward = "x+" if step > 0 else "x-"
-        net.when(27.0, net.copy(got, got, part(-2 * step, other, start, half_b), forward))
+        net.when(net.copy(got, got, part(-2 * step, other, start, half_b), forward))
 
     def from_z():
         got = part(0, 1, a, b)
         for side, forward in (("x-", "x+"), ("x+", "x-")):
             dx = -1 if side == "x-" else 1
             arrival = net.copy(got, got, part(dx, 1, a, b), forward)
-            net.when(20.0, arrival, lambda side=side: from_b(side, 1))
+            net.when(arrival, lambda side=side: from_b(side, 1))
 
     arrival = net.copy(own(a, b), part(0, 0, a, b), part(0, 1, a, b), "z")
-    net.when(9.0, arrival, from_z)
+    net.when(arrival, from_z)
     for side, forward in (("x-", "x+"), ("x+", "x-")):
         dx = -1 if side == "x-" else 1
         arrival = net.copy(own(0, a), part(0, 0, 0, a), part(dx, 0, 0, a), forward)
-        net.when(4.0, arrival, lambda side=side: from_a(side))
+        net.when(arrival, lambda side=side: from_a(side))
     for side, forward in (("x-", "x+"), ("x+", "x-")):
         dx = -1 if side == "x-" else 1
         arrival = net.copy(own(a, b), part(0, 0, a, b), part(dx, 0, a, b), forward)
-        net.when(12.0, arrival, lambda side=side: from_b(side, 0))
+        net.when(arrival, lambda side=side: from_b(side, 0))
     to_z_own = net.copy(own(0, a), part(0, 0, 0, a), part(0, 1, 0, a), "z")
-    net.when(27.0, to_z_own)
+    net.when(to_z_own)
     out[pl.ds(pl.multiple_of(net.col * size, size), size), :] = src[...]
 
 
@@ -149,20 +168,20 @@
 
     def onward(other):
         got = part(-1, other)
-        net.when(27.0, net.copy(got, got, part(-2, other), "x+"))
+        net.when(net.copy(got, got, part(-2, other), "x+"))
 
     def around(other, got):
         arrival = net.copy(got, part(0, other), part(-1, other), "x+")
-        net.when(5.0 + other, arrival, lambda: onward(other))
-        net.when(27.0, net.copy(got, part(0, other), part(1, other), "x-"))
+        net.when(arrival, lambda: onward(other))
+        net.when(net.copy(got, part(0, other), part(1, other), "x-"))
 
     around(0, src)
     arrival = net.copy(src, part(0, 0), part(0, 1), "z")
-    net.when(3.0, arrival, lambda: around(1, part(0, 1)))
+    net.when(arrival, lambda: around(1, part(0, 1)))
     out[pl.ds(pl.multiple_of(net.col * size, size), size), :] = src[...]
 
 
-def gather(net, src, out, relay, axis, early, late):
+def gather(net, src, out, relay, axis):
     depth, width = src.shape
     high, y, core = net.high, net.y, net.core
     middle = depth // 2
@@ -176,29 +195,28 @@
 
     def to_core(dy, other, half=None):
         got = part(dy, other, core, half)
-        net.when(late, net.copy(got, got, part(dy, other, 1 - core, half), "c"))
+        net.when(net.copy(got, got, part(dy, other, 1 - core, half), "c"))
 
     def from_y(dy, other):
         got = part(dy, other, core, 0 if dy < 0 else 1)
         forward = "y+" if dy < 0 else "y-"
         half = 0 if dy < 0 else 1
         arrival = net.copy(got, got, part(2, other, core, half), forward)
-        net.when(late - 1, arrival, lambda: to_core(2, other, half))
+        net.when(arrival, lambda: to_core(2, other, half))
         to_core(dy, other)
 
-    def around(other, got, time):
+    def around(other, got):
         for dy, forward in ((-1, "y+"), (1, "y-")):
             arrival = net.copy(got, part(0, other, core), part(dy, other, core), forward)
-            net.when(time, arrival, lambda dy=dy: from_y(dy, other))
-
-    around(0, src, early + 0.5)
-    span = late - early
+            net.when(arrival, lambda dy=dy: from_y(dy, other))
+
+    around(0, src)
     waiting = [2]
 
     def arrived():
         waiting[0] -= 1
         if waiting[0] == 0:
-            around(1, part(0, 1, core), early + 0.6 * span)
+            around(1, part(0, 1, core))
             to_core(0, 1)
 
     for half, first, second in ((0, "z", "w"), (1, "w", "z")):
@@ -207,11 +225,11 @@
         def onward(half=half, second=second):
             got = relay.at[half]
             arrival = net.copy(got, part(0, half, core, half), part(0, 1, core, half), second)
-            net.when(early + 0.45 * span, arrival, arrived)
-
-        net.when(early + 0.2 * span, arrival, onward)
+            net.when(arrival, arrived)
+
+        net.when(arrival, onward)
     mine = part(0, 0, core)
-    net.when(late, net.copy(src, mine, part(0, 0, 1 - core), "c"))
+    net.when(net.copy(src, mine, part(0, 0, 1 - core), "c"))
     index = net.row
     if axis == 0:
         out[pl.ds(pl.multiple_of(index * depth, depth), depth), :] = src[...]
@@ -230,7 +248,7 @@
         index = net.col_of(x + dx, 1 - low if other else low)
         return pl.ds(pl.multiple_of(index * size + start, 16), count)
 
-    def ring(block, start, count, far, near, acc, times, done):
+    def ring(block, count, far, near, acc, done):
         half = count // 2
         halves = {"x+": (0, half), "x-": (half, half)}
         waiting = [4]
@@ -247,15 +265,16 @@
             def add(index=index, forward=forward, first=first):
                 term = block(1 if forward == "x+" else -1, first, half)
                 acc[index] = far[index] + term[...]
+                net.spend(0.1)
                 dst = near.at[index, pl.ds(first, half)]
-                net.when(times[2], net.copy(acc.at[index], dst, dst, forward), arrived)
-
-            net.when(times[0], arrival, add)
+                net.when(net.copy(acc.at[index], dst, dst, forward), arrived)
+
+            net.when(arrival, add)
         for index, forward in ((0, "x+"), (1, "x-")):
             first = half - halves[forward][0]
             dst = near.at[index, pl.ds(first, half)]
             term = block(1 if forward == "x+" else -1, first, half)
-            net.when(times[1], net.copy(term, dst, dst, forward), arrived)
+            net.when(net.copy(term, dst, dst, forward), arrived)
 
     def block_b(other):
         return lambda dx, first, count: src.at[rows(dx, other, a + first, count)]
@@ -263,38 +282,40 @@
     def block_a(dx, first, count):
         return sums.at[pl.ds((dx % 4) * a + first, count)]
 
-    arrivals = []
+    left = [4]
+
+    def from_partner(k):
+        sums[pl.ds(k * a, a), :] = from_z[pl.ds(k * a, a), :] + src[rows(k, 0, 0, a), :]
+        net.spend(0.1)
+        left[0] -= 1
+        if left[0] == 0:
+            ring(block_a, a, far_a, near_a, acc_a, a_done)
+
     for k in (2, 1, 3, 0):
-        arrivals.append((k, net.copy(
-            src.at[rows(k, 1, 0, a)], from_z.at[pl.ds(k * a, a)], from_z.at[pl.ds(k * a, a)], "z"
-        )))
+        landing = from_z.at[pl.ds(k * a, a)]
+        net.when(net.copy(src.at[rows(k, 1, 0, a)], landing, landing, "z"), lambda k=k: from_partner(k))
 
     def plane_done():
         index = rows(0, 1, a, b)
         total = near_b[0, 0].astype(jnp.float32) + near_b[0, 1].astype(jnp.float32)
         plane[...] = (total + src[index, :].astype(jnp.float32)).astype(plane.dtype)
-        net.when(31.0, net.copy(plane, last, last, "z"), finish_b)
+        net.when(net.copy(plane, last, last, "z"), finish_b)
+
+    both = [2]
 
     def finish_b():
-        out[pl.ds(a, b), :] = out[pl.ds(a, b), :] + last[...].astype(jnp.float32)
-
-    def own_done():
+        both[0] -= 1
+        if both[0]:
+            return
         total = near_b[1, 0].astype(jnp.float32) + near_b[1, 1].astype(jnp.float32)
-        out[pl.ds(a, b), :] = total + src[rows(0, 0, a, b), :].astype(jnp.float32)
+        out[pl.ds(a, b), :] = total + src[rows(0, 0, a, b), :].astype(jnp.float32) + last[...].astype(jnp.float32)
 
     def a_done():
         total = near_a[0].astype(jnp.float32) + near_a[1].astype(jnp.float32)
         out[pl.ds(0, a), :] = total + sums[pl.ds(0, a), :].astype(jnp.float32)
 
-    def start_a():
-        for k, arrival in arrivals:
-            arrival.wait_recv()
-            sums[pl.ds(k * a, a), :] = from_z[pl.ds(k * a, a), :] + src[rows(k, 0, 0, a), :]
-        ring(block_a, 0, a, far_a, near_a, acc_a, (26.0, 29.0, 29.5), a_done)
-
-    ring(block_b(1), a, b, far_b.at[0], near_b.at[0], acc_b.at[0], (5.0, 18.0, 18.5), plane_done)
-    ring(block_b(0), a, b, far_b.at[1], near_b.at[1], acc_b.at[1], (9.0, 27.0, 27.5), own_done)
-    net.at(13.0, start_a)
+    ring(block_b(1), b, far_b.at[0], near_b.at[0], acc_b.at[0], plane_done)
+    ring(block_b(0), b, far_b.at[1], near_b.at[1], acc_b.at[1], finish_b)
 
 
 def scatter_scratch(size, width, dtype):
@@ -327,8 +348,8 @@
     for _ in range(smalls):
         spread_small(net, ins[k], outs[k])
         k += 1
-    for axis, early, late in gathers:
-        gather(net, ins[k], outs[k], relays.pop(0), axis, early, late)
+    for axis in gathers:
+        gather(net, ins[k], outs[k], relays.pop(0), axis)
         k += 1
     net.run()
 
@@ -351,7 +372,7 @@
         arrays.append(array)
         shapes.append(jax.ShapeDtypeStruct((array.shape[0] * col_total, array.shape[1]), array.dtype))
         copies += 8
-    for array, axis, _, _ in gathers:
+    for array, axis in gathers:
         depth, width = array.shape
         arrays.append(array)
         shape = (depth * row_total, width) if axis == 0 else (depth, width * row_total)
@@ -359,7 +380,7 @@
         scratch.append(pltpu.VMEM((2, depth // 2, width), array.dtype))
         copies += 22
     return pl.pallas_call(
-        functools.partial(comm_body, len(spreads), len(smalls), [g[1:] for g in gathers], len(sums)),
+        functools.partial(comm_body, len(spreads), len(smalls), [axis for _, axis in gathers], len(sums)),
         out_shape=shapes,
         in_specs=[pl.BlockSpec(memory_space=pltpu.VMEM)] * len(arrays),
         out_specs=[pl.BlockSpec(memory_space=pltpu.VMEM)] * len(arrays),
@@ -371,7 +392,7 @@
     )(*arrays)
 
 
-def y_exchange(net, src, dst, relay, times, ready=None, arrived=None):
+def y_exchange(net, src, dst, relay, ready=None, arrived=None):
     core = net.core
     half = src.shape[2] // 2
     tell = arrived or (lambda d: None)
@@ -384,18 +405,18 @@
             def onward(index=index, forward=forward, rows=rows):
                 for c, name in ((core, forward), (1 - core, forward + "c")):
                     arrival = net.copy(relay.at[index, c], dst.at[2, core, rows], dst.at[2, c, rows], name)
-                    net.when(times[3], arrival, lambda: tell(2))
-
-            net.when(times[1], arrival, onward)
+                    net.when(arrival, lambda: tell(2))
+
+            net.when(arrival, onward)
 
     def beside(d):
         forward = "y+" if d == 1 else "y-"
         for c, name in ((core, forward), (1 - core, forward + "c")):
             arrival = net.copy(src.at[d, c], dst.at[4 - d, core], dst.at[4 - d, c], name)
-            net.when(times[2], arrival, lambda: tell(4 - d))
+            net.when(arrival, lambda: tell(4 - d))
 
     def here():
-        net.when(times[2], net.copy(src.at[0, 1 - core], dst.at[0, core], dst.at[0, 1 - core], "c"), lambda: tell(0))
+        net.when(net.copy(src.at[0, 1 - core], dst.at[0, core], dst.at[0, 1 - core], "c"), lambda: tell(0))
         dst[0, core] = src[0, core]
 
     steps = {2: opposite, 1: lambda: beside(1), 3: lambda: beside(3), 0: here}
@@ -414,22 +435,22 @@
     mine, theirs = pl.ds(pl.multiple_of(low * half, half), half), pl.ds(pl.multiple_of((1 - low) * half, half), half)
 
     def ready(steps):
-        for k, d in enumerate((2, 1, 3, 0)):
+        for d in (2, 1, 3, 0):
             arrival = net.copy(table.at[1, d, :, mine], far.at[d, :, mine], far.at[d, :, theirs], "w")
 
-            def onward(k=k, d=d):
+            def onward(d=d):
                 arrival = net.copy(far.at[d, :, theirs], far.at[d, :, theirs], far.at[d, :, mine], "z")
-                net.when(7.0 + 2.5 * k, arrival, steps[d])
-
-            net.when(3.5 + 2.5 * k, arrival, onward)
-
-    y_exchange(net, table.at[0], out.at[0], relay.at[0], (0.0, 5.0, 12.0, 16.0))
-    y_exchange(net, far, out.at[1], relay.at[1], (0.0, 17.0, 24.0, 25.0), ready)
-    up_tasks(net, x_ref, w_ref, hidden, 1.0, 1.2)
+                net.when(arrival, steps[d])
+
+            net.when(arrival, onward)
+
+    y_exchange(net, table.at[0], out.at[0], relay.at[0])
+    y_exchange(net, far, out.at[1], relay.at[1], ready)
+    up_tasks(net, x_ref, w_ref, hidden)
     net.run()
 
 
-def up_tasks(net, x_ref, w_ref, out, start, every):
+def up_tasks(net, x_ref, w_ref, out):
     rows, width = out.shape
     tile = min(256, rows)
     span = min(256, width)
@@ -444,10 +465,10 @@
             out[at, columns] = (inner * (1.0 + lax.erf(inner * (0.5**0.5))) * 0.5).astype(out.dtype)
 
     for j in range(width // span):
-        net.at(start + every * j, lambda j=j: piece(j))
-
-
-def down_tasks(net, x_ref, w_ref, out, start, every):
+        net.work(1.2, lambda j=j: piece(j))
+
+
+def down_tasks(net, x_ref, w_ref, out):
     rows, width = out.shape
     tile = min(256, rows)
     span = min(512, width)
@@ -462,7 +483,7 @@
             out[at, columns] = product.astype(out.dtype)
 
     for j in range(width // span):
-        net.at(start + every * j, lambda j=j: piece(j))
+        net.work(1.2, lambda j=j: piece(j))
 
 
 def collect_body(x_ref, w_ref, parts, dense, near, across, far, other, total, relay, send, recv):
@@ -472,7 +493,6 @@
     half = parts.shape[3] // 2
     mine, theirs = pl.ds(pl.multiple_of(low * half, half), half), pl.ds(pl.multiple_of((1 - low) * half, half), half)
     left = {0: 1, 1: 2, 2: 4, 3: 2}
-    after = {0: 9.0, 1: 13.0, 3: 15.0, 2: 18.0}
 
     def arrived(d):
         left[d] -= 1
@@ -481,13 +501,14 @@
 
         def add():
             total[d] = far[d, :, theirs] + other[d]
-            net.when(27.0, net.copy(total.at[d], across.at[d], across.at[d], "w"))
-
-        net.when(after[d], net.copy(far.at[d, :, mine], other.at[d], other.at[d], "z"), add)
-
-    y_exchange(net, parts.at[1], far, relay.at[1], (0.0, 5.0, 9.0, 14.0), None, arrived)
-    y_exchange(net, parts.at[0], near, relay.at[0], (0.0, 14.5, 22.0, 25.0))
-    down_tasks(net, x_ref, w_ref, dense, 0.5, 2.0)
+            net.spend(0.2)
+            net.when(net.copy(total.at[d], across.at[d], across.at[d], "w"))
+
+        net.when(net.copy(far.at[d, :, mine], other.at[d], other.at[d], "z"), add)
+
+    y_exchange(net, parts.at[1], far, relay.at[1], None, arrived)
+    y_exchange(net, parts.at[0], near, relay.at[0])
+    down_tasks(net, x_ref, w_ref, dense)
     net.run()
 
 
@@ -574,7 +595,7 @@
         0,
         spreads=(tokens,),
         smalls=(ids_block,),
-        gathers=((qkv_weight.reshape(qkv_weight.shape[0], -1), 0, 3.0, 14.0), (out_weight, 1, 13.0, 19.0)),
+        gathers=((qkv_weight.reshape(qkv_weight.shape[0], -1), 0), (out_weight, 1)),
     )
     normed = layer_norm(image_rows, ln1_gain).astype(jnp.bfloat16)
     projected = matmul(normed, qkv_whole).astype(jnp.bfloat16)
@@ -587,12 +608,12 @@
     attended = jnp.einsum("hqk,khd->qhd", probabilities, values, preferred_element_type=jnp.float32)
     attended = attended.astype(jnp.bfloat16).reshape(seq_len, head_count * head_dim)
     head_terms = matmul(attended, out_whole).astype(jnp.bfloat16)
-    mixed_heads, up_whole = exchange("heads", 1, sums=(head_terms,), gathers=((ffn_in, 0, 5.0, 19.0),))
+    mixed_heads, up_whole = exchange("heads", 1, sums=(head_terms,), gathers=((ffn_in, 0),))
     hidden_mine = (tokens.astype(jnp.float32) + mixed_heads).astype(jnp.bfloat16)
     normed_mine = layer_norm(hidden_mine, ln2_gain).astype(jnp.bfloat16)
 
     normed_image, down_whole = exchange(
-        "norms", 2, spreads=(normed_mine,), gathers=((ffn_out, 1, 5.0, 19.0),)
+        "norms", 2, spreads=(normed_mine,), gathers=((ffn_out, 1),)
     )
 
     ids_rows = ids_all.reshape(col_total, 8, tok_count)[:, 0]

time: 315 us -> 279 us (0.89)
  Pallas kernels: 268 us -> 230 us
    pallas_call x4, Pallas kernels: 186 us -> 150 us  [exchange(): pl.pallas_call(functools.partial(comm_body, len(spreads), len(smalls), [a...]
where the time goes in v3:
time: 279 us; the launch traced here: 277 us
  Pallas kernels  230 us (82%)
  matrix products  31.1 us (11%)
  local copies, waits for them, and re-layouts  9.32 us (3%)
  other arithmetic  6.28 us (2%)
    pallas_call x4, Pallas kernels, exchange(): pl.pallas_call(functools.partial(comm_body, len(spreads), len(smalls), [a...  150 us
    pallas_call x2, Pallas kernels, expert_call(): pl.pallas_call(body, out_shape=[jax.ShapeDtypeStruct(shape, jnp.bfloat16)...  72.6 us
    dot_general x5, matrix products, matmul(): return jnp.dot(a, b, preferred_element_type=jnp.float32)  21.8 us
    unnamed x23, local copies, waits for them, and re-layouts  8.36 us
    pallas_call x1, Pallas kernels, up_gelu(): pl.pallas_call(up_body, grid=(width // tile,), out_shape=jax.ShapeDtypeSt...  7.24 us

profile of v3, /device:TPU:2, one launch (start us, length us, event | category | flops | bytes accessed | tf_op | source)
XLA Modules:
  0.0 277.0 jit_solution(6029689095484282456)
XLA Ops:
  0.0 0.7 broadcast_in_dim.8.refs_1_
  0.7 1.1 copy.39
  1.8 0.2 copy.40.refs_2_
  1.9 0.0 copy-start.3
  1.9 1.0 copy-done.3
  3.0 0.0 copy-start.7
  3.0 0.8 copy-done.7
  3.8 39.6 %enter.1 = (bf16[1024,2048]{1,0:T(8,128)(2,1)S(1)}, s32[64,128]{1,0:T(8,128)S(1)}, bf16[2048,768]{1,0:T(8,128)(2,1)S(1)}, bf16[256,2048]{1,0:T(8,128)(2,1)S(1)}) custom-call(bf16[128,2048]{1,0:T(8,128)(2,1)S(1)} %copy-done.3, s32[8,128]{1,0:T(8,128)S(1)} %broadcast_in_dim.8.refs_1_, bf16[128,768]{1,0:T(8,128)(2,1)S(1)} %copy.40.refs_2_, ...), custom_call_target="tpu_custom_call" | custom-call | tf_op jit(solution)/shard_map/enter/pallas_call | solution.py:382
  43.4 0.0 copy-start.10
  43.5 0.6 convert_reduce_fusion
  44.1 1.2 fusion.3
  45.3 0.0 copy-done.10
  45.3 3.9 %fusion.21 = bf16[1024,768]{0,1:T(8,128)(2,1)S(1)} fusion(bf16[2048,768]{1,0:T(8,128)(2,1)S(1)} %get-tuple-element.19, bf16[1024,2048]{1,0:T(8,128)(2,1)S(1)} %get-tuple-element.18, f32[2048]{0:T(1024)S(1)} %copy-done.10, f32[1024]{0:T(1024)S(1)} %add_rsqrt_fusion, f32[1024]{0:T(1024)S(1)} %broadcast_multiply_fusion.1), kind=kOutput, calls=%fused_computation.25 | convolution fusion | flops 3232497664 | bytes 8929280 | tf_op jit(solution)/shard_map/dot_general | solution.py:567
  49.3 0.1 copy.45
  49.4 2.5 select_reduce_fusion
  51.9 0.1 fusion.57
  52.0 5.1 %fusion.68 = (f32[2,1024]{1,0:T(2,128)S(1)}, f32[2,1024,1024]{1,2,0:T(8,128)}) fusion(bf16[1024,2,3,128]{0,3,2,1:T(8,128)(2,1)S(1)} %bitcast.90), kind=kOutput, calls=%fused_computation.117 | convolution fusion | flops 543163392 | bytes 9445376 | tf_op jit(solution)/shard_map/sub | solution.py:606
  57.2 4.2 %fusion.27 = bf16[2,128,1024]{2,1,0:T(8,128)(2,1)S(1)} fusion(f32[2,1024,1024]{1,2,0:T(8,128)} %get-tuple-element.38, f32[2,1024]{1,0:T(2,128)S(1)} %get-tuple-element.37, bf16[1024,2,3,128]{0,3,2,1:T(8,128)(2,1)S(1)} %bitcast.91), kind=kOutput, calls=%fused_computation.33 | convolution fusion | flops 541327360 | bytes 9445376 | tf_op jit(solution)/shard_map/hqk,khd->qhd/dot_general | solution.py:608
  61.3 0.0 copy-start.5
  61.4 1.3 convolution_convert_fusion.refs_0_
  62.6 0.0 copy-done.5
  62.7 0.0 copy-start.4
  62.7 0.0 copy-start.9
  62.7 0.0 copy-start.6
  62.7 37.0 %heads.1 = (f32[128,2048]{1,0:T(8,128)S(1)}, bf16[2048,1024]{1,0:T(8,128)(2,1)S(1)}) custom-call(bf16[1024,2048]{1,0:T(8,128)(2,1)S(1)} %convolution_convert_fusion.refs_0_, bf16[128,1024]{1,0:T(8,128)(2,1)S(1)} %copy-done.5), custom_call_target="tpu_custom_call" | custom-call | tf_op jit(solution)/shard_map/heads/pallas_call | solution.py:382
  99.7 0.0 copy-start
  99.7 2.0 copy-done
  101.7 0.0 copy-done.4
  101.7 0.2 convert_reduce_fusion.1
  101.9 0.3 fusion.30
  102.2 0.0 copy-done.9
  102.2 0.4 fusion.32.refs_0_
  102.6 0.0 copy-done.6
  102.6 39.8 %norms.1 = (bf16[1024,2048]{1,0:T(8,128)(2,1)S(1)}, bf16[1024,2048]{1,0:T(8,128)(2,1)S(1)}) custom-call(bf16[128,2048]{1,0:T(8,128)(2,1)S(1)} %fusion.32.refs_0_, bf16[1024,128]{1,0:T(8,128)(2,1)S(1)} %copy-done.6), custom_call_target="tpu_custom_call" | custom-call | tf_op jit(solution)/shard_map/norms/pallas_call | solution.py:382
  142.4 0.0 copy-start.1
  142.4 0.0 copy-start.2
  142.5 3.9 %convolution_convert_fusion.1 = bf16[512,2048]{1,0:T(8,128)(2,1)} fusion(bf16[1024,2048]{1,0:T(8,128)(2,1)S(1)} %get-tuple-element.22.x_ref, s32[1024]{0:T(1024)S(1)} %get-tuple-element.36), kind=kOutput, calls=%fused_computation.22 | convolution fusion | flops 2149056512 | bytes 6295552 | tf_op jit(solution)/shard_map/dot_general | solution.py:567
  146.4 0.0 copy-done.1
  146.4 0.0 copy-done.2
  146.4 33.0 %dispatch.1 = (bf16[1024,1024]{1,0:T(8,128)(2,1)S(1)}, bf16[2,4,2,32,2048]{4,3,2,1,0:T(8,128)(2,1)S(1)}) custom-call(bf16[1024,2048]{1,0:T(8,128)(2,1)} %copy-done.2, bf16[2048,1024]{1,0:T(8,128)(2,1)} %copy-done, bf16[2,4,2,32,2048]{4,3,2,1,0:T(8,128)(2,1)} %bitcast.84), custom_call_target="tpu_custom_call" | custom-call | tf_op jit(solution)/shard_map/dispatch/pallas_call | solution.py:517
  179.4 0.0 copy-start.8
  179.4 3.4 %copy-done.8 = bf16[1,2048,2048]{2,1,0:T(8,128)(2,1)S(1)} copy-done((bf16[1,2048,2048]{2,1,0:T(8,128)(2,1)S(1)}, bf16[1,2048,2048]{2,1,0:T(8,128)(2,1)}, u32[]{:S(2)}) %copy-start.8) | copy-done | bytes 8388632
  182.8 7.2 %up_gelu.1 = bf16[512,2048]{1,0:T(8,128)(2,1)S(1)} custom-call(bf16[512,2048]{1,0:T(8,128)(2,1)S(1)} %bitcast.81, bf16[2048,2048]{1,0:T(8,128)(2,1)S(1)} %bitcast.80), custom_call_target="tpu_custom_call" | custom-call | flops 4294967296 | bytes 12582912 | tf_op jit(solution)/shard_map/up_gelu/pallas_call | solution.py:540
  190.0 8.3 %fusion.18 = bf16[512,2048]{1,0:T(8,128)(2,1)S(1)} fusion(bf16[512,2048]{1,0:T(8,128)(2,1)S(1)} %up_gelu.1, bf16[1,2048,2048]{2,1,0:T(8,128)(2,1)} %param.19), kind=kOutput, calls=%fused_computation.23 | convolution fusion | flops 4296015872 | bytes 12582912 | tf_op jit(solution)/shard_map/dot_general | solution.py:567
  198.3 39.6 %collect.1 = (bf16[1024,2048]{1,0:T(8,128)(2,1)}, bf16[4,2,32,2048]{3,2,1,0:T(8,128)(2,1)S(1)}, bf16[4,2,16,2048]{3,2,1,0:T(8,128)(2,1)S(1)}) custom-call(bf16[1024,1024]{1,0:T(8,128)(2,1)S(1)} %get-tuple-element.25.x_ref, bf16[1024,2048]{1,0:T(8,128)(2,1)} %copy-done.1, bf16[2,4,2,32,2048]{4,3,2,1,0:T(8,128)(2,1)S(1)} %bitcast.78), custom_call_target="tpu_custom_call" | custom-call | tf_op jit(solution)/shard_map/collect/pallas_call | solution.py:517
  238.0 4.3 %add_convert_fusion.refs_0_ = bf16[1024,2048]{1,0:T(8,128)(2,1)S(1)} fusion(bf16[1024,2048]{1,0:T(8,128)(2,1)} %get-tuple-element.28, bf16[128,2048]{1,0:T(8,128)(2,1)S(1)} %bitcast.83, bf16[256,2048]{1,0:T(8,128)(2,1)S(1)} %bitcast.82, s32[1024]{0:T(1024)S(1)} %get-tuple-element.35), kind=kOutput, calls=%fused_computation.10 | convolution fusion | flops 1620443136 | bytes 9965568 | tf_op jit(solution)/shard_map/dot_general | solution.py:567
  242.3 33.8 %leave.1 = f32[128,2048]{1,0:T(8,128)S(1)} custom-call(bf16[1024,2048]{1,0:T(8,128)(2,1)S(1)} %add_convert_fusion.refs_0_), custom_call_target="tpu_custom_call" | custom-call | tf_op jit(solution)/shard_map/leave/pallas_call | solution.py:382
  276.1 0.9 fusion.33
  (7 shorter events, 0.1 us)
Async XLA Ops:
  1.9 1.0 copy-start.3
  3.0 0.8 copy-start.7
  43.4 1.9 copy-start.10
  61.3 1.3 copy-start.5
  62.7 39.0 %copy-start.4 = (bf16[128,2048]{1,0:T(8,128)(2,1)S(1)}, bf16[128,2048]{1,0:T(8,128)(2,1)}, u32[]{:S(2)}) copy-start(bf16[128,2048]{1,0:T(8,128)(2,1)} %refs_0_.1) | copy-start | bytes 1572868
  62.7 39.6 %copy-start.9 = (f32[2048]{0:T(1024)S(1)}, f32[2048]{0:T(1024)}, u32[]{:S(2)}) copy-start(f32[2048]{0:T(1024)} %param.14) | copy-start | bytes 24580
  62.7 39.9 %copy-start.6 = (bf16[1024,128]{1,0:T(8,128)(2,1)S(1)}, bf16[1024,128]{1,0:T(8,128)(2,1)}, u32[]{:S(2)}) copy-start(bf16[1024,128]{1,0:T(8,128)(2,1)} %refs_1_.3) | copy-start | bytes 786436
  99.7 2.0 copy-start
  142.4 4.0 %copy-start.1 = (bf16[1024,2048]{1,0:T(8,128)(2,1)}, bf16[1024,2048]{1,0:T(8,128)(2,1)S(1)}, u32[]{:S(2)}) copy-start(bf16[1024,2048]{1,0:T(8,128)(2,1)S(1)} %get-tuple-element.26.w_ref) | copy-start | bytes 12582916
  142.4 4.0 %copy-start.2 = (bf16[1024,2048]{1,0:T(8,128)(2,1)}, bf16[1024,2048]{1,0:T(8,128)(2,1)S(1)}, u32[]{:S(2)}) copy-start(bf16[1024,2048]{1,0:T(8,128)(2,1)S(1)} %get-tuple-element.22.x_ref) | copy-start | bytes 12582916
  179.4 3.4 %copy-start.8 = (bf16[1,2048,2048]{2,1,0:T(8,128)(2,1)S(1)}, bf16[1,2048,2048]{2,1,0:T(8,128)(2,1)}, u32[]{:S(2)}) copy-start(bf16[1,2048,2048]{2,1,0:T(8,128)(2,1)} %param.18) | copy-start | bytes 25165828

commit v4 on v3

--- a/solution.py
+++ b/solution.py
@@ -237,9 +237,9 @@
         out[:, pl.ds(pl.multiple_of(index * width, width), width)] = src[...]
 
 
-def reduce_scatter(net, src, out, scratch):
+def reduce_scatter(net, fill, src, scratch, finish):
     from_z, sums, far_a, near_a, acc_a, far_b, near_b, acc_b, plane, last = scratch
-    size = out.shape[0]
+    size = src.shape[0] // 8
     a = SPLIT
     b = size - a
     x, low = net.x, net.low
@@ -258,23 +258,28 @@
             if waiting[0] == 0:
                 done()
 
-        for index, forward in ((0, "x+"), (1, "x-")):
-            first = halves[forward][0]
-            arrival = net.copy(block(2, first, half), far.at[index], far.at[index], forward)
-
-            def add(index=index, forward=forward, first=first):
+        def start_far():
+            for index, forward in ((0, "x+"), (1, "x-")):
+                first = halves[forward][0]
+                arrival = net.copy(block(2, first, half), far.at[index], far.at[index], forward)
+
+                def add(index=index, forward=forward, first=first):
+                    term = block(1 if forward == "x+" else -1, first, half)
+                    acc[index] = far[index] + term[...]
+                    net.spend(0.1)
+                    dst = near.at[index, pl.ds(first, half)]
+                    net.when(net.copy(acc.at[index], dst, dst, forward), arrived)
+
+                net.when(arrival, add)
+
+        def start_direct():
+            for index, forward in ((0, "x+"), (1, "x-")):
+                first = half - halves[forward][0]
+                dst = near.at[index, pl.ds(first, half)]
                 term = block(1 if forward == "x+" else -1, first, half)
-                acc[index] = far[index] + term[...]
-                net.spend(0.1)
-                dst = near.at[index, pl.ds(first, half)]
-                net.when(net.copy(acc.at[index], dst, dst, forward), arrived)
-
-            net.when(arrival, add)
-        for index, forward in ((0, "x+"), (1, "x-")):
-            first = half - halves[forward][0]
-            dst = near.at[index, pl.ds(first, half)]
-            term = block(1 if forward == "x+" else -1, first, half)
-            net.when(net.copy(term, dst, dst, forward), arrived)
+                net.when(net.copy(term, dst, dst, forward), arrived)
+
+        return start_far, start_direct
 
     def block_b(other):
         return lambda dx, first, count: src.at[rows(dx, other, a + first, count)]
@@ -283,39 +288,50 @@
         return sums.at[pl.ds((dx % 4) * a + first, count)]
 
     left = [4]
+    both = [3]
+    wide = lambda value: value.astype(jnp.float32)
 
     def from_partner(k):
         sums[pl.ds(k * a, a), :] = from_z[pl.ds(k * a, a), :] + src[rows(k, 0, 0, a), :]
         net.spend(0.1)
         left[0] -= 1
         if left[0] == 0:
-            ring(block_a, a, far_a, near_a, acc_a, a_done)
-
-    for k in (2, 1, 3, 0):
+            for start in ring(block_a, a, far_a, near_a, acc_a, arrived):
+                start()
+
+    def to_partner(k):
         landing = from_z.at[pl.ds(k * a, a)]
-        net.when(net.copy(src.at[rows(k, 1, 0, a)], landing, landing, "z"), lambda k=k: from_partner(k))
+        net.when(net.copy(src.at[rows(k, 1, 0, a)], landing, landing, "z"), lambda: from_partner(k))
 
     def plane_done():
-        index = rows(0, 1, a, b)
-        total = near_b[0, 0].astype(jnp.float32) + near_b[0, 1].astype(jnp.float32)
-        plane[...] = (total + src[index, :].astype(jnp.float32)).astype(plane.dtype)
-        net.when(net.copy(plane, last, last, "z"), finish_b)
-
-    both = [2]
-
-    def finish_b():
+        total = wide(near_b[0, 0]) + wide(near_b[0, 1]) + wide(src[rows(0, 1, a, b), :])
+        plane[...] = total.astype(plane.dtype)
+        net.spend(0.3)
+        net.when(net.copy(plane, last, last, "z"), arrived)
+
+    def arrived():
         both[0] -= 1
         if both[0]:
             return
-        total = near_b[1, 0].astype(jnp.float32) + near_b[1, 1].astype(jnp.float32)
-        out[pl.ds(a, b), :] = total + src[rows(0, 0, a, b), :].astype(jnp.float32) + last[...].astype(jnp.float32)
-
-    def a_done():
-        total = near_a[0].astype(jnp.float32) + near_a[1].astype(jnp.float32)
-        out[pl.ds(0, a), :] = total + sums[pl.ds(0, a), :].astype(jnp.float32)
-
-    ring(block_b(1), b, far_b.at[0], near_b.at[0], acc_b.at[0], plane_done)
-    ring(block_b(0), b, far_b.at[1], near_b.at[1], acc_b.at[1], finish_b)
+        first = wide(near_a[0]) + wide(near_a[1]) + wide(sums[pl.ds(0, a), :])
+        second = wide(near_b[1, 0]) + wide(near_b[1, 1]) + wide(src[rows(0, 0, a, b), :]) + wide(last[...])
+        net.spend(0.5)
+        finish(first, second)
+
+    far_other, direct_other = ring(block_b(1), b, far_b.at[0], near_b.at[0], acc_b.at[0], plane_done)
+    far_own, direct_own = ring(block_b(0), b, far_b.at[1], near_b.at[1], acc_b.at[1], arrived)
+    fill(lambda i: net.col_of(x + 2, lax.rem(low + 1 + i, 2)))
+    far_other()
+    far_own()
+    to_partner(2)
+    fill(lambda i: net.col_of(x + 1 - 2 * i, 1 - low))
+    direct_other()
+    to_partner(1)
+    to_partner(3)
+    fill(lambda i: net.col_of(x + 1 - 2 * i, low))
+    direct_own()
+    fill(lambda i: net.col_of(x, lax.rem(low + 1 + i, 2)))
+    to_partner(0)
 
 
 def scatter_scratch(size, width, dtype):
@@ -326,76 +342,168 @@
     return [pltpu.VMEM(shape, dtype) for shape in shapes]
 
 
-def comm_body(spreads, smalls, gathers, sums, *refs):
-    count = spreads + smalls + len(gathers) + sums
-    ins, outs, rest = refs[:count], refs[count : 2 * count], refs[2 * count :]
-    scratch, (send, recv) = rest[:-2], rest[-2:]
-    net = Net(send, recv)
-    names = []
-    if spreads or smalls or sums:
-        names += ["x+", "x-", "z"]
-    if gathers:
-        names += ["y+", "y-", "w", "c"] + ([] if names else ["z"])
-    net.greet(names)
-    relays = list(scratch[10 * sums :])
-    k = 0
-    for _ in range(sums):
-        reduce_scatter(net, ins[k], outs[k], scratch[:10])
-        k += 1
-    for _ in range(spreads):
+def comm_body(spreads, smalls, gathers, *refs):
+    count = spreads + smalls + len(gathers)
+    ins, outs, relays = refs[:count], refs[count : 2 * count], refs[2 * count : -2]
+    net = Net(*refs[-2:])
+    net.greet(["x+", "x-", "z", "y+", "y-", "w", "c"])
+    for k in range(spreads):
         spread(net, ins[k], outs[k])
-        k += 1
-    for _ in range(smalls):
+    for k in range(spreads, spreads + smalls):
         spread_small(net, ins[k], outs[k])
-        k += 1
-    for axis in gathers:
-        gather(net, ins[k], outs[k], relays.pop(0), axis)
-        k += 1
+    for i, axis in enumerate(gathers):
+        k = spreads + smalls + i
+        gather(net, ins[k], outs[k], relays[i], axis)
     net.run()
 
 
-def exchange(name, collective_id, sums=(), spreads=(), smalls=(), gathers=()):
-    row_total = lax.axis_size("row")
-    col_total = lax.axis_size("col")
-    arrays, shapes, scratch, copies = [], [], [], 0
-    for array in sums:
-        size = array.shape[0] // col_total
-        arrays.append(array)
-        shapes.append(jax.ShapeDtypeStruct((size, array.shape[1]), jnp.float32))
-        scratch += scatter_scratch(size, array.shape[1], array.dtype)
-        copies += 24
-    for array in spreads:
-        arrays.append(array)
-        shapes.append(jax.ShapeDtypeStruct((array.shape[0] * col_total, array.shape[1]), array.dtype))
-        copies += 20
-    for array in smalls:
-        arrays.append(array)
-        shapes.append(jax.ShapeDtypeStruct((array.shape[0] * col_total, array.shape[1]), array.dtype))
-        copies += 8
-    for array, axis in gathers:
-        depth, width = array.shape
-        arrays.append(array)
-        shape = (depth * row_total, width) if axis == 0 else (depth, width * row_total)
-        shapes.append(jax.ShapeDtypeStruct(shape, array.dtype))
-        scratch.append(pltpu.VMEM((2, depth // 2, width), array.dtype))
-        copies += 22
+def communicate(name, body, collective_id, arrays, shapes, scratch, copies):
     return pl.pallas_call(
-        functools.partial(comm_body, len(spreads), len(smalls), [axis for _, axis in gathers], len(sums)),
+        body,
         out_shape=shapes,
         in_specs=[pl.BlockSpec(memory_space=pltpu.VMEM)] * len(arrays),
-        out_specs=[pl.BlockSpec(memory_space=pltpu.VMEM)] * len(arrays),
+        out_specs=[pl.BlockSpec(memory_space=pltpu.VMEM)] * len(shapes),
         scratch_shapes=scratch + [pltpu.SemaphoreType.DMA((copies,)), pltpu.SemaphoreType.DMA((copies,))],
         compiler_params=pltpu.CompilerParams(
-            collective_id=collective_id, has_side_effects=True, vmem_limit_bytes=40 * 2**20
+            collective_id=collective_id, has_side_effects=True, vmem_limit_bytes=56 * 2**20
         ),
         name=name,
     )(*arrays)
 
 
-def y_exchange(net, src, dst, relay, ready=None, arrived=None):
+def gathered(array, axis):
+    depth, width = array.shape
+    total = lax.axis_size("row")
+    shape = (depth * total, width) if axis == 0 else (depth, width * total)
+    return jax.ShapeDtypeStruct(shape, array.dtype)
+
+
+def relay_of(array):
+    return pltpu.VMEM((2, array.shape[0] // 2, array.shape[1]), array.dtype)
+
+
+def exchange(name, collective_id, spreads=(), smalls=(), gathers=()):
+    whole = [jax.ShapeDtypeStruct((8 * a.shape[0], a.shape[1]), a.dtype) for a in (*spreads, *smalls)]
+    return communicate(
+        name,
+        functools.partial(comm_body, len(spreads), len(smalls), [axis for _, axis in gathers]),
+        collective_id,
+        [*spreads, *smalls, *(array for array, _ in gathers)],
+        whole + [gathered(*pair) for pair in gathers],
+        [relay_of(array) for array, _ in gathers],
+        20 * len(spreads) + 8 * len(smalls) + 22 * len(gathers),
+    )
+
+
+def middle_body(heads, qkv, weight, tokens, gain, up, down, hidden, normed_image, up_whole, down_whole, terms, mixed, normed, up_relay, down_relay, *rest):
+    net = Net(*rest[-2:])
+    net.greet(["x+", "x-", "z", "y+", "y-", "w", "c"])
+    size = tokens.shape[0]
+    dim = qkv.shape[1] // (3 * heads)
+
+    def fill(column):
+        @pl.loop(0, 2)
+        def _(i):
+            at = pl.ds(pl.multiple_of(column(i) * size, size), size)
+
+            @pl.loop(0, heads)
+            def _(h):
+                part = lambda k: pl.ds(pl.multiple_of((3 * h + k) * dim, dim), dim)
+                scores = lax.dot_general(
+                    qkv[at, part(0)], qkv[:, part(1)], (((1,), (1,)), ((), ())), preferred_element_type=jnp.float32
+                )
+                scores = scores * (dim ** (-0.5))
+                weights = jnp.exp(scores - jnp.max(scores, axis=-1, keepdims=True))
+                chances = (weights / jnp.sum(weights, axis=-1, keepdims=True)).astype(jnp.bfloat16)
+                mixed[:, pl.ds(pl.multiple_of(h * dim, dim), dim)] = matmul(chances, qkv[:, part(2)]).astype(jnp.bfloat16)
+
+            @pl.loop(0, weight.shape[1] // 512)
+            def _(j):
+                columns = pl.ds(pl.multiple_of(j * 512, 512), 512)
+                terms[at, columns] = matmul(mixed[...], weight[:, columns]).astype(jnp.bfloat16)
+
+        net.spend(2.6)
+
+    def finish(first, second):
+        for start, total in ((0, first), (SPLIT, second)):
+            at = pl.ds(start, total.shape[0])
+            state = (tokens[at, :].astype(jnp.float32) + total).astype(jnp.bfloat16)
+            hidden[at, :] = state
+            normed[at, :] = layer_norm(state, gain[...]).astype(jnp.bfloat16)
+        net.spend(0.5)
+        spread(net, normed, normed_image)
+
+    gather(net, up, up_whole, up_relay, 0)
+    gather(net, down, down_whole, down_relay, 1)
+    reduce_scatter(net, fill, terms, rest[:-2], finish)
+    net.run()
+
+
+def middle(collective_id, heads, qkv, weight, tokens, gain, up, down):
+    size, width = tokens.shape
+    image = jax.ShapeDtypeStruct((8 * size, width), tokens.dtype)
+    scratch = [
+        pltpu.VMEM(image.shape, image.dtype),
+        pltpu.VMEM((size, weight.shape[0]), image.dtype),
+        pltpu.VMEM(tokens.shape, image.dtype),
+        relay_of(up),
+        relay_of(down),
+    ]
+    return communicate(
+        "middle",
+        functools.partial(middle_body, heads),
+        collective_id,
+        (qkv, weight, tokens, gain, up, down),
+        [jax.ShapeDtypeStruct(tokens.shape, tokens.dtype), image, gathered(up, 0), gathered(down, 1)],
+        scratch + scatter_scratch(size, width, tokens.dtype),
+        24 + 20 + 2 * 22,
+    )
+
+
+def leave_body(dense, picking, returned, hidden, out, terms, *rest):
+    net = Net(*rest[-2:])
+    net.greet(["x+", "x-", "z"])
+    size = hidden.shape[0]
+
+    def fill(column):
+        @pl.loop(0, 2)
+        def _(i):
+            at = pl.ds(pl.multiple_of(column(i) * size, size), size)
+
+            @pl.loop(0, dense.shape[1] // 512)
+            def _(j):
+                columns = pl.ds(pl.multiple_of(j * 512, 512), 512)
+                total = dense[at, columns].astype(jnp.float32) + matmul(picking[at, :], returned[:, columns])
+                terms[at, columns] = total.astype(jnp.bfloat16)
+
+        net.spend(0.8)
+
+    def finish(first, second):
+        for start, total in ((0, first), (SPLIT, second)):
+            at = pl.ds(start, total.shape[0])
+            out[at, :] = (hidden[at, :].astype(jnp.float32) + total).astype(jnp.bfloat16)
+
+    reduce_scatter(net, fill, terms, rest[:-2], finish)
+    net.run()
+
+
+def leave(collective_id, dense, picking, returned, hidden):
+    return communicate(
+        "leave",
+        leave_body,
+        collective_id,
+        (dense, picking, returned, hidden),
+        [jax.ShapeDtypeStruct(hidden.shape, hidden.dtype)],
+        [pltpu.VMEM(dense.shape, dense.dtype)] + scatter_scratch(*hidden.shape, hidden.dtype),
+        24,
+    )
+
+
+def y_exchange(net, src, dst, relay, ready=None, arrived=None, then=None):
     core = net.core
     half = src.shape[2] // 2
     tell = arrived or (lambda d: None)
+    forwarded = [2]
 
     def opposite():
         for index, forward in ((0, "y+"), (1, "y-")):
@@ -406,6 +514,9 @@
                 for c, name in ((core, forward), (1 - core, forward + "c")):
                     arrival = net.copy(relay.at[index, c], dst.at[2, core, rows], dst.at[2, c, rows], name)
                     net.when(arrival, lambda: tell(2))
+                forwarded[0] -= 1
+                if then is not None and forwarded[0] == 0:
+                    then()
 
             net.when(arrival, onward)
 
@@ -506,26 +617,15 @@
 
         net.when(net.copy(far.at[d, :, mine], other.at[d], other.at[d], "z"), add)
 
-    y_exchange(net, parts.at[1], far, relay.at[1], None, arrived)
-    y_exchange(net, parts.at[0], near, relay.at[0])
+    second = lambda: y_exchange(net, parts.at[0], near, relay.at[0])
+    y_exchange(net, parts.at[1], far, relay.at[1], None, arrived, second)
     down_tasks(net, x_ref, w_ref, dense)
     net.run()
 
 
 def expert_call(name, body, collective_id, arrays, shapes, scratch):
-    copies = 40
-    return pl.pallas_call(
-        body,
-        out_shape=[jax.ShapeDtypeStruct(shape, jnp.bfloat16) for shape in shapes],
-        in_specs=[pl.BlockSpec(memory_space=pltpu.VMEM)] * len(arrays),
-        out_specs=[pl.BlockSpec(memory_space=pltpu.VMEM)] * len(shapes),
-        scratch_shapes=[pltpu.VMEM(shape, jnp.bfloat16) for shape in scratch]
-        + [pltpu.SemaphoreType.DMA((copies,)), pltpu.SemaphoreType.DMA((copies,))],
-        compiler_params=pltpu.CompilerParams(
-            collective_id=collective_id, has_side_effects=True, vmem_limit_bytes=48 * 2**20
-        ),
-        name=name,
-    )(*arrays)
+    shapes = [jax.ShapeDtypeStruct(shape, jnp.bfloat16) for shape in shapes]
+    return communicate(name, body, collective_id, arrays, shapes, [pltpu.VMEM(shape, jnp.bfloat16) for shape in scratch], 40)
 
 
 def up_body(x_ref, w_ref, o_ref):
@@ -599,21 +699,8 @@
     )
     normed = layer_norm(image_rows, ln1_gain).astype(jnp.bfloat16)
     projected = matmul(normed, qkv_whole).astype(jnp.bfloat16)
-    projected = projected.reshape(seq_len, head_count, 3, head_dim)
-    queries, keys, values = projected[:, :, 0], projected[:, :, 1], projected[:, :, 2]
-    scores = jnp.einsum("qhd,khd->hqk", queries, keys, preferred_element_type=jnp.float32)
-    scores = scores * (head_dim ** (-0.5))
-    weights = jnp.exp(scores - jnp.max(scores, axis=-1, keepdims=True))
-    probabilities = (weights / jnp.sum(weights, axis=-1, keepdims=True)).astype(jnp.bfloat16)
-    attended = jnp.einsum("hqk,khd->qhd", probabilities, values, preferred_element_type=jnp.float32)
-    attended = attended.astype(jnp.bfloat16).reshape(seq_len, head_count * head_dim)
-    head_terms = matmul(attended, out_whole).astype(jnp.bfloat16)
-    mixed_heads, up_whole = exchange("heads", 1, sums=(head_terms,), gathers=((ffn_in, 0),))
-    hidden_mine = (tokens.astype(jnp.float32) + mixed_heads).astype(jnp.bfloat16)
-    normed_mine = layer_norm(hidden_mine, ln2_gain).astype(jnp.bfloat16)
-
-    normed_image, down_whole = exchange(
-        "norms", 2, spreads=(normed_mine,), gathers=((ffn_out, 1),)
+    hidden_mine, normed_image, up_whole, down_whole = middle(
+        1, head_count, projected, out_whole, tokens, ln2_gain[None, :], ffn_in, ffn_out
     )
 
     ids_rows = ids_all.reshape(col_total, 8, tok_count)[:, 0]
@@ -662,9 +749,8 @@
         (full, part, part, relays),
     )
     rows_two = jnp.concatenate((near.reshape(-1, model_width), across.reshape(-1, model_width)))
-    partial = dense.astype(jnp.float32) + matmul(picking, rows_two)
-    (total,) = exchange("leave", 5, sums=(partial.astype(jnp.bfloat16),))
-    return (hidden_mine.astype(jnp.float32) + total).astype(jnp.bfloat16)
+    (out,) = leave(5, dense, picking, rows_two, hidden_mine)
+    return out
 
 
 def solution(mesh):

time: 279 us -> 291 us (1.043)
  Pallas kernels: 230 us -> 248 us
  matrix products: 31.1 us -> 20.3 us
  other arithmetic: 6.28 us -> 11.4 us
    pallas_call x6 -> x5, Pallas kernels: 223 us -> 240 us  [communicate(): pl.pallas_call(body, out_shape=shapes, in_specs=[pl.BlockSpec(memory_spac...]
    sub x1 -> x0, matrix products: 5.14 us -> none  [shards(): weights = jnp.exp(scores - jnp.max(scores, axis=-1, keepdims=True))]
    dot_general x1 -> x0, matrix products: 4.15 us -> none  [shards(): jnp.einsum('hqk,khd->qhd', probabilities, values, preferred_element_type=...]
    dot_general x5 -> x3, matrix products: 21.8 us -> 20.3 us  [matmul(): return jnp.dot(a, b, preferred_element_type=jnp.float32)]
    unnamed x23 -> x12, local copies, waits for them, and re-layouts: 8.36 us -> 8.33 us
where the time goes in v4:
time: 291 us; the launch traced here: 290 us
  Pallas kernels  248 us (85%)
  matrix products  20.3 us (7%)
  other arithmetic  11.4 us (4%)
  local copies, waits for them, and re-layouts  10.6 us (4%)
    pallas_call x5, Pallas kernels, communicate(): pl.pallas_call(body, out_shape=shapes, in_specs=[pl.BlockSpec(memory_spac...  240 us
    dot_general x3, matrix products, matmul(): return jnp.dot(a, b, preferred_element_type=jnp.float32)  20.3 us
    unnamed x12, local copies, waits for them, and re-layouts  8.33 us
    pallas_call x1, Pallas kernels, up_gelu(): pl.pallas_call(up_body, grid=(width // tile,), out_shape=jax.ShapeDtypeSt...  7.24 us

profile of v4, /device:TPU:2, one launch (start us, length us, event | category | flops | bytes accessed | tf_op | source)
XLA Modules:
  0.0 290.1 jit_solution(5222357936378761029)
XLA Ops:
  0.0 1.1 copy.23
  1.1 0.8 copy.24.refs_2_
  1.9 1.2 broadcast_in_dim.11.refs_1_
  3.2 44.0 %enter.1 = (bf16[1024,2048]{1,0:T(8,128)(2,1)}, s32[64,128]{1,0:T(8,128)}, bf16[2048,768]{1,0:T(8,128)(2,1)}, bf16[256,2048]{1,0:T(8,128)(2,1)}) custom-call(bf16[128,2048]{1,0:T(8,128)(2,1)} %tokens.1, s32[8,128]{1,0:T(8,128)} %broadcast_in_dim.11.refs_1_, bf16[128,768]{1,0:T(8,128)(2,1)} %copy.24.refs_2_, bf16[256,128]{1,0:T(8,128)(2,1)} %refs_3_.1), custom_call_target="tpu_custom_call" | custom-call | tf_op jit(solution)/shard_map/enter/pallas_call | solution.py:361
  47.2 0.8 broadcast_multiply_fusion
  48.0 0.1 copy.25
  48.1 2.5 select_reduce_fusion
  50.6 0.0 copy-start.2
  50.6 0.1 fusion.38
  50.8 0.0 copy-start.3
  50.8 0.0 copy-start.4
  50.8 3.0 %convert_reduce_fusion = f32[1024]{0:T(1024)S(1)} fusion(bf16[1024,2048]{1,0:T(8,128)(2,1)} %get-tuple-element.18), kind=kLoop, calls=%fused_computation.1 | loop fusion | flops 4193280 | bytes 4198400 | tf_op jit(solution)/shard_map/reduce_sum | solution.py:661
  53.7 0.4 copy-done.2
  54.1 1.2 fusion.2
  55.3 0.0 copy-done.3
  55.4 0.0 copy-done.4
  55.4 5.1 %fusion.15.qkv = bf16[1024,768]{1,0:T(8,128)(2,1)} fusion(bf16[2048,768]{1,0:T(8,128)(2,1)S(1)} %copy-done.3, bf16[1024,2048]{1,0:T(8,128)(2,1)S(1)} %copy-done.2, f32[2048]{0:T(1024)S(1)} %copy-done.4, f32[1024]{0:T(1024)S(1)} %add_rsqrt_fusion, f32[1024]{0:T(1024)S(1)} %broadcast_multiply_fusion.1), kind=kOutput, calls=%fused_computation.16 | convolution fusion | flops 3232497664 | bytes 8929280 | tf_op jit(solution)/shard_map/dot_general | solution.py:667
  60.5 84.2 %middle.1 = (bf16[128,2048]{1,0:T(8,128)(2,1)}, bf16[1024,2048]{1,0:T(8,128)(2,1)}, bf16[2048,1024]{1,0:T(8,128)(2,1)}, bf16[1024,2048]{1,0:T(8,128)(2,1)}) custom-call(bf16[1024,768]{1,0:T(8,128)(2,1)} %fusion.15.qkv, bf16[256,2048]{1,0:T(8,128)(2,1)} %get-tuple-element.20.weight, bf16[128,2048]{1,0:T(8,128)(2,1)} %tokens.1, f32[1,2048]{1,0:T(1,128)} %bitcast.53, ...), custom_call_target="tpu_custom_call" | custom-call | tf_op jit(solution)/shard_map/middle/pallas_call | solution.py:361
  144.7 5.9 %convolution_convert_fusion = bf16[512,2048]{1,0:T(8,128)(2,1)} fusion(bf16[1024,2048]{1,0:T(8,128)(2,1)} %get-tuple-element.21.x_ref, s32[1024]{0:T(1024)S(1)} %get-tuple-element.34), kind=kOutput, calls=%fused_computation.13 | convolution fusion | flops 2149056512 | bytes 6295552 | tf_op jit(solution)/shard_map/dot_general | solution.py:667
  150.5 34.7 %dispatch.1 = (bf16[1024,1024]{1,0:T(8,128)(2,1)}, bf16[2,4,2,32,2048]{4,3,2,1,0:T(8,128)(2,1)}) custom-call(bf16[1024,2048]{1,0:T(8,128)(2,1)} %get-tuple-element.21.x_ref, bf16[2048,1024]{1,0:T(8,128)(2,1)} %get-tuple-element.22.w_ref, bf16[2,4,2,32,2048]{4,3,2,1,0:T(8,128)(2,1)} %bitcast.46), custom_call_target="tpu_custom_call" | custom-call | tf_op jit(solution)/shard_map/dispatch/pallas_call | solution.py:361
  185.2 0.0 copy-start
  185.2 3.4 %copy-done = bf16[1,2048,2048]{2,1,0:T(8,128)(2,1)S(1)} copy-done((bf16[1,2048,2048]{2,1,0:T(8,128)(2,1)S(1)}, bf16[1,2048,2048]{2,1,0:T(8,128)(2,1)}, u32[]{:S(2)}) %copy-start) | copy-done | bytes 8388632
  188.6 0.0 copy-start.1
  188.6 1.6 copy-done.1
  190.2 7.2 %up_gelu.1 = bf16[512,2048]{1,0:T(8,128)(2,1)S(1)} custom-call(bf16[512,2048]{1,0:T(8,128)(2,1)S(1)} %bitcast.45, bf16[2048,2048]{1,0:T(8,128)(2,1)S(1)} %bitcast.44), custom_call_target="tpu_custom_call" | custom-call | flops 4294967296 | bytes 12582912 | tf_op jit(solution)/shard_map/up_gelu/pallas_call | solution.py:640
  197.4 9.3 %fusion.12 = bf16[512,2048]{1,0:T(8,128)(2,1)} fusion(bf16[512,2048]{1,0:T(8,128)(2,1)S(1)} %up_gelu.1, bf16[1,2048,2048]{2,1,0:T(8,128)(2,1)} %param.19), kind=kOutput, calls=%fused_computation.14 | convolution fusion | flops 4296015872 | bytes 12582912 | tf_op jit(solution)/shard_map/dot_general | solution.py:667
  206.7 35.6 %collect.1 = (bf16[1024,2048]{1,0:T(8,128)(2,1)}, bf16[4,2,32,2048]{3,2,1,0:T(8,128)(2,1)}, bf16[4,2,16,2048]{3,2,1,0:T(8,128)(2,1)}) custom-call(bf16[1024,1024]{1,0:T(8,128)(2,1)} %get-tuple-element.24.x_ref, bf16[1024,2048]{1,0:T(8,128)(2,1)} %get-tuple-element.25.w_ref, bf16[2,4,2,32,2048]{4,3,2,1,0:T(8,128)(2,1)} %bitcast.47), custom_call_target="tpu_custom_call" | custom-call | tf_op jit(solution)/shard_map/collect/pallas_call | solution.py:361
  242.3 2.7 pad_maximum_fusion.returned
  245.1 1.1 fusion.18.picking
  246.1 42.0 %leave.1 = bf16[128,2048]{1,0:T(8,128)(2,1)} custom-call(bf16[1024,2048]{1,0:T(8,128)(2,1)} %get-tuple-element.27.dense, bf16[1024,384]{1,0:T(8,128)(2,1)} %fusion.18.picking, bf16[384,2048]{1,0:T(8,128)(2,1)} %pad_maximum_fusion.returned, bf16[128,2048]{1,0:T(8,128)(2,1)} %get-tuple-element.30.hidden), custom_call_target="tpu_custom_call" | custom-call | tf_op jit(solution)/shard_map/leave/pallas_call | solution.py:361
  288.2 1.9 copy.28
  (4 shorter events, 0.1 us)
Async XLA Ops:
  50.6 3.5 %copy-start.2 = (bf16[1024,2048]{1,0:T(8,128)(2,1)S(1)}, bf16[1024,2048]{1,0:T(8,128)(2,1)}, u32[]{:S(2)}) copy-start(bf16[1024,2048]{1,0:T(8,128)(2,1)} %get-tuple-element.18) | copy-start | bytes 12582916
  50.8 4.6 %copy-start.3 = (bf16[2048,768]{1,0:T(8,128)(2,1)S(1)}, bf16[2048,768]{1,0:T(8,128)(2,1)}, u32[]{:S(2)}) copy-start(bf16[2048,768]{1,0:T(8,128)(2,1)} %get-tuple-element.19) | copy-start | bytes 9437188
  50.8 4.6 %copy-start.4 = (f32[2048]{0:T(1024)S(1)}, f32[2048]{0:T(1024)}, u32[]{:S(2)}) copy-start(f32[2048]{0:T(1024)} %param.11) | copy-start | bytes 24580
  185.2 3.4 %copy-start = (bf16[1,2048,2048]{2,1,0:T(8,128)(2,1)S(1)}, bf16[1,2048,2048]{2,1,0:T(8,128)(2,1)}, u32[]{:S(2)}) copy-start(bf16[1,2048,2048]{2,1,0:T(8,128)(2,1)} %param.18) | copy-start | bytes 25165828
  188.6 1.6 copy-start.1

commit v5 on v4

--- a/solution.py
+++ b/solution.py
@@ -33,6 +33,9 @@
     def col_of(self, x, low):
         return lax.rem(x + 8, 4) * 2 + low
 
+    def block_of(self, x, low):
+        return low * 4 + lax.rem(x + 8, 4)
+
     def peer(self, name):
         high, y, core, x, low = self.high, self.y, self.core, self.x, self.low
         at = {
@@ -103,59 +106,84 @@
     return ref.at[pl.ds(pl.multiple_of(start, step), size)]
 
 
-def spread(net, src, out):
+def counted(count, action):
+    left = [count]
+
+    def step():
+        left[0] -= 1
+        if left[0] == 0:
+            action()
+
+    return step
+
+
+def spread(net, src, out, plane_done=lambda: None, done=lambda: None):
     size = src.shape[0]
     a, half_a, half_b = SPLIT, SPLIT // 2, (size - SPLIT) // 2
     b = size - a
     x, low = net.x, net.low
+    mine = counted(8, plane_done)
+    theirs = counted(12, done)
+    sides = ((-1, "x+", 0), (1, "x-", 1))
 
     def part(dx, other, start, rows):
         plane = 1 - low if other else low
-        return rows_of(out, net.col_of(x + dx, plane) * size + start, rows)
+        return rows_of(out, net.block_of(x + dx, plane) * size + start, rows)
 
     def own(start, rows):
         return src.at[pl.ds(start, rows)]
 
-    def from_a(side):
-        step = 1 if side == "x-" else -1
-        at = -step
-        forward = "x+" if step > 0 else "x-"
-        start = 0 if step > 0 else half_a
-        got = part(at, 0, start, half_a)
-        far = net.copy(got, got, part(at - step, 0, start, half_a), forward)
-        net.when(far, lambda: to_z(part(2, 0, start, half_a), part(2, 1, start, half_a)))
-        to_z(part(at, 0, 0, a), part(at, 1, 0, a))
-
-    def to_z(got, arriving):
-        net.when(net.copy(got, got, arriving, "z"))
-
-    def from_b(side, other):
-        step = 1 if side == "x-" else -1
-        start = a if step > 0 else a + half_b
-        got = part(-step, other, start, half_b)
-        forward = "x+" if step > 0 else "x-"
-        net.when(net.copy(got, got, part(-2 * step, other, start, half_b), forward))
+    def to_z(dx, start, rows):
+        got = part(dx, 0, start, rows)
+        net.when(net.copy(got, got, part(dx, 1, start, rows), "z"), theirs)
+
+    def onward(dx, forward, other, start, rows, then):
+        got = part(dx, other, start, rows)
+        net.when(net.copy(got, got, part(2, other, start, rows), forward), then)
+
+    def from_a(dx, forward, index):
+        mine()
+
+        def far():
+            mine()
+            to_z(2, index * half_a, half_a)
+
+        onward(dx, forward, 0, index * half_a, half_a, far)
+        to_z(dx, 0, a)
+
+    def from_b(dx, forward, index):
+        mine()
+        onward(dx, forward, 0, a + index * half_b, half_b, mine)
+        later()
+
+    def partner(index, half, then):
+        dx, forward, _ = sides[index]
+        got = part(0, 1, a + half * half_b, half_b)
+        net.when(net.copy(got, got, part(dx, 1, a + half * half_b, half_b), forward), then)
 
     def from_z():
-        got = part(0, 1, a, b)
-        for side, forward in (("x-", "x+"), ("x+", "x-")):
-            dx = -1 if side == "x-" else 1
-            arrival = net.copy(got, got, part(dx, 1, a, b), forward)
-            net.when(arrival, lambda side=side: from_b(side, 1))
-
-    arrival = net.copy(own(a, b), part(0, 0, a, b), part(0, 1, a, b), "z")
-    net.when(arrival, from_z)
-    for side, forward in (("x-", "x+"), ("x+", "x-")):
-        dx = -1 if side == "x-" else 1
-        arrival = net.copy(own(0, a), part(0, 0, 0, a), part(dx, 0, 0, a), forward)
-        net.when(arrival, lambda side=side: from_a(side))
-    for side, forward in (("x-", "x+"), ("x+", "x-")):
-        dx = -1 if side == "x-" else 1
-        arrival = net.copy(own(a, b), part(0, 0, a, b), part(dx, 0, a, b), forward)
-        net.when(arrival, lambda side=side: from_b(side, 0))
-    to_z_own = net.copy(own(0, a), part(0, 0, 0, a), part(0, 1, 0, a), "z")
-    net.when(to_z_own)
-    out[pl.ds(pl.multiple_of(net.col * size, size), size), :] = src[...]
+        theirs()
+        for dx, forward, index in sides:
+
+            def first(dx=dx, forward=forward, index=index):
+                theirs()
+                onward(dx, forward, 1, a + index * half_b, half_b, theirs)
+
+            partner(index, index, first)
+        later()
+
+    def second():
+        for _, _, index in sides:
+            partner(index, 1 - index, theirs)
+
+    later = counted(3, second)
+    net.when(net.copy(own(a, b), part(0, 0, a, b), part(0, 1, a, b), "z"), from_z)
+    for start, rows, action in ((0, a, from_a), (a, b, from_b)):
+        for dx, forward, index in sides:
+            arrival = net.copy(own(start, rows), part(0, 0, start, rows), part(dx, 0, start, rows), forward)
+            net.when(arrival, functools.partial(action, dx, forward, index))
+    net.when(net.copy(own(0, a), part(0, 0, 0, a), part(0, 1, 0, a), "z"), theirs)
+    out[pl.ds(pl.multiple_of(net.block_of(x, low) * size, size), size), :] = src[...]
 
 
 def spread_small(net, src, out):
@@ -164,7 +192,7 @@
 
     def part(dx, other):
         plane = 1 - low if other else low
-        return rows_of(out, net.col_of(x + dx, plane) * size, size, 8)
+        return rows_of(out, net.block_of(x + dx, plane) * size, size, 8)
 
     def onward(other):
         got = part(-1, other)
@@ -178,13 +206,14 @@
     around(0, src)
     arrival = net.copy(src, part(0, 0), part(0, 1), "z")
     net.when(arrival, lambda: around(1, part(0, 1)))
-    out[pl.ds(pl.multiple_of(net.col * size, size), size), :] = src[...]
-
-
-def gather(net, src, out, relay, axis):
+    out[pl.ds(pl.multiple_of(net.block_of(x, net.low) * size, size), size), :] = src[...]
+
+
+def gather(net, src, out, relay, axis, done=lambda: None):
     depth, width = src.shape
     high, y, core = net.high, net.y, net.core
     middle = depth // 2
+    landed = counted(10, done)
 
     def part(dy, other, core, half=None):
         index = net.row_of(1 - high if other else high, y + dy, core)
@@ -195,7 +224,7 @@
 
     def to_core(dy, other, half=None):
         got = part(dy, other, core, half)
-        net.when(net.copy(got, got, part(dy, other, 1 - core, half), "c"))
+        net.when(net.copy(got, got, part(dy, other, 1 - core, half), "c"), landed)
 
     def from_y(dy, other):
         got = part(dy, other, core, 0 if dy < 0 else 1)
@@ -229,7 +258,7 @@
 
         net.when(arrival, onward)
     mine = part(0, 0, core)
-    net.when(net.copy(src, mine, part(0, 0, 1 - core), "c"))
+    net.when(net.copy(src, mine, part(0, 0, 1 - core), "c"), landed)
     index = net.row
     if axis == 0:
         out[pl.ds(pl.multiple_of(index * depth, depth), depth), :] = src[...]
@@ -245,7 +274,7 @@
     x, low = net.x, net.low
 
     def rows(dx, other, start, count):
-        index = net.col_of(x + dx, 1 - low if other else low)
+        index = net.block_of(x + dx, 1 - low if other else low)
         return pl.ds(pl.multiple_of(index * size + start, 16), count)
 
     def ring(block, count, far, near, acc, done):
@@ -320,17 +349,17 @@
 
     far_other, direct_other = ring(block_b(1), b, far_b.at[0], near_b.at[0], acc_b.at[0], plane_done)
     far_own, direct_own = ring(block_b(0), b, far_b.at[1], near_b.at[1], acc_b.at[1], arrived)
-    fill(lambda i: net.col_of(x + 2, lax.rem(low + 1 + i, 2)))
+    fill(lambda i: net.block_of(x + 2, lax.rem(low + 1 + i, 2)))
     far_other()
     far_own()
     to_partner(2)
-    fill(lambda i: net.col_of(x + 1 - 2 * i, 1 - low))
+    fill(lambda i: net.block_of(x + 1 - 2 * i, 1 - low))
     direct_other()
     to_partner(1)
     to_partner(3)
-    fill(lambda i: net.col_of(x + 1 - 2 * i, low))
+    fill(lambda i: net.block_of(x + 1 - 2 * i, low))
     direct_own()
-    fill(lambda i: net.col_of(x, lax.rem(low + 1 + i, 2)))
+    fill(lambda i: net.block_of(x, lax.rem(low + 1 + i, 2)))
     to_partner(0)
 
 
@@ -358,6 +387,7 @@
 
 
 def communicate(name, body, collective_id, arrays, shapes, scratch, copies):
+    used = sum(math.prod(ref.shape) * jnp.dtype(ref.dtype).itemsize for ref in scratch)
     return pl.pallas_call(
         body,
         out_shape=shapes,
@@ -365,7 +395,7 @@
         out_specs=[pl.BlockSpec(memory_space=pltpu.VMEM)] * len(shapes),
         scratch_shapes=scratch + [pltpu.SemaphoreType.DMA((copies,)), pltpu.SemaphoreType.DMA((copies,))],
         compiler_params=pltpu.CompilerParams(
-            collective_id=collective_id, has_side_effects=True, vmem_limit_bytes=56 * 2**20
+            collective_id=collective_id, has_side_effects=True, vmem_limit_bytes=used + 6 * 2**20
         ),
         name=name,
     )(*arrays)
@@ -391,15 +421,20 @@
         [*spreads, *smalls, *(array for array, _ in gathers)],
         whole + [gathered(*pair) for pair in gathers],
         [relay_of(array) for array, _ in gathers],
-        20 * len(spreads) + 8 * len(smalls) + 22 * len(gathers),
+        22 * len(spreads) + 8 * len(smalls) + 22 * len(gathers),
     )
 
 
-def middle_body(heads, qkv, weight, tokens, gain, up, down, hidden, normed_image, up_whole, down_whole, terms, mixed, normed, up_relay, down_relay, *rest):
+def middle_body(heads, qkv, weight, tokens, gain, up, down, position, hidden, down_whole, units, out, *rest):
+    terms, mixed, normed, image, up_whole, table, far, y_relay, up_relay, down_relay = rest[:10]
     net = Net(*rest[-2:])
-    net.greet(["x+", "x-", "z", "y+", "y-", "w", "c"])
+    net.greet(["x+", "x-", "z", "y+", "y-", "w", "c", "y+c", "y-c"])
     size = tokens.shape[0]
     dim = qkv.shape[1] // (3 * heads)
+    low = net.low
+    slots = out.shape[3] // 2
+    mine = pl.ds(pl.multiple_of(low * slots, slots), slots)
+    theirs = pl.ds(pl.multiple_of((1 - low) * slots, slots), slots)
 
     def fill(column):
         @pl.loop(0, 2)
@@ -424,46 +459,95 @@
 
         net.spend(2.6)
 
-    def finish(first, second):
-        for start, total in ((0, first), (SPLIT, second)):
+    def place(index, plane):
+        rows = pl.ds(pl.multiple_of(plane * 4 * size, 4 * size), 4 * size)
+        flat = math.prod(table.shape[1:5])
+        here = lax.broadcasted_iota(jnp.int32, (flat, 4 * size), 0) == position[pl.ds(0, 1), rows]
+        placing = jnp.where(here, 1.0, 0.0).astype(jnp.bfloat16)
+        span = 512
+
+        @pl.loop(0, image.shape[1] // span)
+        def _(j):
+            columns = pl.ds(pl.multiple_of(j * span, span), span)
+            put = matmul(placing, image[rows, columns]).astype(jnp.bfloat16)
+            table[index, :, :, :, :, columns] = put.reshape(table.shape[1:5] + (span,))
+
+        net.spend(1.2)
+
+    def plane_done():
+        place(0, low)
+
+        def from_w(d):
+            got = far.at[d, :, theirs]
+            arrival = net.copy(got, got, far.at[d, :, mine], "z")
+            net.when(arrival, last[d])
+            first[d]()
+
+        for d in (2, 1, 3, 0):
+            arrival = net.copy(table.at[0, 1, d], far.at[d, :, mine], far.at[d, :, theirs], "w")
+            net.when(arrival, functools.partial(from_w, d))
+        start_all(own)
+        ready()
+
+    def image_done():
+        place(1, 1 - low)
+        start_all(other)
+        ready()
+
+    own = y_exchange(net, chunks(table.at[0, 0]), chunks(out.at[0], mine), y_relay.at[0])
+    first = y_exchange(net, chunks(far, theirs), chunks(out.at[1], theirs), y_relay.at[1])
+    last = y_exchange(net, chunks(far, mine), chunks(out.at[1], mine), y_relay.at[2])
+    other = y_exchange(net, chunks(table.at[1, 0]), chunks(out.at[0], theirs), y_relay.at[3])
+    ready = counted(3, lambda: up_tasks(net, image, up_whole, units))
+
+    def finish(first_rows, second_rows):
+        for start, total in ((0, first_rows), (SPLIT, second_rows)):
             at = pl.ds(start, total.shape[0])
             state = (tokens[at, :].astype(jnp.float32) + total).astype(jnp.bfloat16)
             hidden[at, :] = state
             normed[at, :] = layer_norm(state, gain[...]).astype(jnp.bfloat16)
         net.spend(0.5)
-        spread(net, normed, normed_image)
-
-    gather(net, up, up_whole, up_relay, 0)
+        spread(net, normed, image, plane_done, image_done)
+
+    gather(net, up, up_whole, up_relay, 0, ready)
     gather(net, down, down_whole, down_relay, 1)
-    reduce_scatter(net, fill, terms, rest[:-2], finish)
+    reduce_scatter(net, fill, terms, rest[10:-2], finish)
     net.run()
 
 
-def middle(collective_id, heads, qkv, weight, tokens, gain, up, down):
+def middle(collective_id, heads, qkv, weight, tokens, gain, up, down, position, slots):
     size, width = tokens.shape
-    image = jax.ShapeDtypeStruct((8 * size, width), tokens.dtype)
+    image = (8 * size, width)
+    sixteen = lambda *shape: pltpu.VMEM(shape, tokens.dtype)
     scratch = [
-        pltpu.VMEM(image.shape, image.dtype),
-        pltpu.VMEM((size, weight.shape[0]), image.dtype),
-        pltpu.VMEM(tokens.shape, image.dtype),
+        sixteen(*image),
+        sixteen(size, weight.shape[0]),
+        sixteen(size, width),
+        sixteen(*image),
+        sixteen(*gathered(up, 0).shape),
+        sixteen(2, 2, 4, 2, slots // 2, width),
+        sixteen(4, 2, slots, width),
+        sixteen(4, 2, slots // 2, width),
         relay_of(up),
         relay_of(down),
     ]
+    made = lambda *shape: jax.ShapeDtypeStruct(shape, tokens.dtype)
     return communicate(
         "middle",
         functools.partial(middle_body, heads),
         collective_id,
-        (qkv, weight, tokens, gain, up, down),
-        [jax.ShapeDtypeStruct(tokens.shape, tokens.dtype), image, gathered(up, 0), gathered(down, 1)],
+        (qkv, weight, tokens, gain, up, down, position),
+        [made(size, width), gathered(down, 1), made(8 * size, up.shape[1]), made(2, 4, 2, slots, width)],
         scratch + scatter_scratch(size, width, tokens.dtype),
-        24 + 20 + 2 * 22,
+        24 + 22 + 2 * 22 + 8 + 4 * 10,
     )
 
 
-def leave_body(dense, picking, returned, hidden, out, terms, *rest):
+def leave_body(dense, picking, near, across, hidden, out, terms, *rest):
     net = Net(*rest[-2:])
     net.greet(["x+", "x-", "z"])
     size = hidden.shape[0]
+    count = near.shape[0]
 
     def fill(column):
         @pl.loop(0, 2)
@@ -473,7 +557,9 @@
             @pl.loop(0, dense.shape[1] // 512)
             def _(j):
                 columns = pl.ds(pl.multiple_of(j * 512, 512), 512)
-                total = dense[at, columns].astype(jnp.float32) + matmul(picking[at, :], returned[:, columns])
+                total = dense[at, columns].astype(jnp.float32)
+                total += matmul(picking[at, pl.ds(0, count)], near[:, columns])
+                total += matmul(picking[at, pl.ds(count, across.shape[0])], across[:, columns])
                 terms[at, columns] = total.astype(jnp.bfloat16)
 
         net.spend(0.8)
@@ -487,78 +573,51 @@
     net.run()
 
 
-def leave(collective_id, dense, picking, returned, hidden):
+def leave(collective_id, dense, picking, near, across, hidden):
     return communicate(
         "leave",
         leave_body,
         collective_id,
-        (dense, picking, returned, hidden),
+        (dense, picking, near, across, hidden),
         [jax.ShapeDtypeStruct(hidden.shape, hidden.dtype)],
         [pltpu.VMEM(dense.shape, dense.dtype)] + scatter_scratch(*hidden.shape, hidden.dtype),
         24,
     )
 
 
-def y_exchange(net, src, dst, relay, ready=None, arrived=None, then=None):
+def y_exchange(net, src, dst, relay, arrived=lambda d: None, then=lambda: None):
     core = net.core
-    half = src.shape[2] // 2
-    tell = arrived or (lambda d: None)
-    forwarded = [2]
+    forwarded = counted(2, then)
 
     def opposite():
-        for index, forward in ((0, "y+"), (1, "y-")):
-            rows = pl.ds(index * half, half)
-            arrival = net.copy(src.at[2, :, rows], relay.at[index], relay.at[index], forward)
-
-            def onward(index=index, forward=forward, rows=rows):
-                for c, name in ((core, forward), (1 - core, forward + "c")):
-                    arrival = net.copy(relay.at[index, c], dst.at[2, core, rows], dst.at[2, c, rows], name)
-                    net.when(arrival, lambda: tell(2))
-                forwarded[0] -= 1
-                if then is not None and forwarded[0] == 0:
-                    then()
-
-            net.when(arrival, onward)
+        for index, c, forward, last in ((0, core, "y+", "y+"), (1, 1 - core, "y-", "y-c")):
+
+            def onward(index=index, c=c, last=last):
+                arrival = net.copy(relay.at[index], dst(2, core), dst(2, c), last)
+                net.when(arrival, lambda: arrived(2))
+                forwarded()
+
+            net.when(net.copy(src(2, c), relay.at[index], relay.at[index], forward), onward)
 
     def beside(d):
         forward = "y+" if d == 1 else "y-"
         for c, name in ((core, forward), (1 - core, forward + "c")):
-            arrival = net.copy(src.at[d, c], dst.at[4 - d, core], dst.at[4 - d, c], name)
-            net.when(arrival, lambda: tell(4 - d))
+            net.when(net.copy(src(d, c), dst(4 - d, core), dst(4 - d, c), name), lambda: arrived(4 - d))
 
     def here():
-        net.when(net.copy(src.at[0, 1 - core], dst.at[0, core], dst.at[0, 1 - core], "c"), lambda: tell(0))
-        dst[0, core] = src[0, core]
-
-    steps = {2: opposite, 1: lambda: beside(1), 3: lambda: beside(3), 0: here}
-    if ready is None:
-        for d in (2, 1, 3, 0):
-            steps[d]()
-    else:
-        ready(steps)
-
-
-def dispatch_body(x_ref, w_ref, table, hidden, out, far, relay, send, recv):
-    net = Net(send, recv)
-    net.greet(["y+", "y-", "y+c", "y-c", "c", "z", "w"])
-    low = net.low
-    half = table.shape[3] // 2
-    mine, theirs = pl.ds(pl.multiple_of(low * half, half), half), pl.ds(pl.multiple_of((1 - low) * half, half), half)
-
-    def ready(steps):
-        for d in (2, 1, 3, 0):
-            arrival = net.copy(table.at[1, d, :, mine], far.at[d, :, mine], far.at[d, :, theirs], "w")
-
-            def onward(d=d):
-                arrival = net.copy(far.at[d, :, theirs], far.at[d, :, theirs], far.at[d, :, mine], "z")
-                net.when(arrival, steps[d])
-
-            net.when(arrival, onward)
-
-    y_exchange(net, table.at[0], out.at[0], relay.at[0])
-    y_exchange(net, far, out.at[1], relay.at[1], ready)
-    up_tasks(net, x_ref, w_ref, hidden)
-    net.run()
+        net.when(net.copy(src(0, 1 - core), dst(0, core), dst(0, 1 - core), "c"), lambda: arrived(0))
+        dst(0, core)[...] = src(0, core)[...]
+
+    return {2: opposite, 1: lambda: beside(1), 3: lambda: beside(3), 0: here}
+
+
+def chunks(ref, *rest):
+    return lambda d, c: ref.at[(d, c, *rest)]
+
+
+def start_all(steps):
+    for d in (2, 1, 3, 0):
+        steps[d]()
 
 
 def up_tasks(net, x_ref, w_ref, out):
@@ -576,7 +635,7 @@
             out[at, columns] = (inner * (1.0 + lax.erf(inner * (0.5**0.5))) * 0.5).astype(out.dtype)
 
     for j in range(width // span):
-        net.work(1.2, lambda j=j: piece(j))
+        net.work(1.6, lambda j=j: piece(j))
 
 
 def down_tasks(net, x_ref, w_ref, out):
@@ -603,13 +662,8 @@
     low = net.low
     half = parts.shape[3] // 2
     mine, theirs = pl.ds(pl.multiple_of(low * half, half), half), pl.ds(pl.multiple_of((1 - low) * half, half), half)
-    left = {0: 1, 1: 2, 2: 4, 3: 2}
-
-    def arrived(d):
-        left[d] -= 1
-        if left[d]:
-            return
-
+
+    def landed(d):
         def add():
             total[d] = far[d, :, theirs] + other[d]
             net.spend(0.2)
@@ -617,8 +671,10 @@
 
         net.when(net.copy(far.at[d, :, mine], other.at[d], other.at[d], "z"), add)
 
-    second = lambda: y_exchange(net, parts.at[0], near, relay.at[0])
-    y_exchange(net, parts.at[1], far, relay.at[1], None, arrived, second)
+    counts = {d: counted(1 if d == 0 else 2, functools.partial(landed, d)) for d in range(4)}
+    second = y_exchange(net, chunks(parts.at[0]), chunks(near), relay.at[0])
+    first = y_exchange(net, chunks(parts.at[1]), chunks(far), relay.at[1], lambda d: counts[d](), lambda: start_all(second))
+    start_all(first)
     down_tasks(net, x_ref, w_ref, dense)
     net.run()
 
@@ -689,67 +745,53 @@
     head_count, head_dim = qkv_weight.shape[1], qkv_weight.shape[3]
     seq_len = tok_count * col_total
 
-    ids_block = jnp.broadcast_to(expert_ids[:, 0][None, :], (8, tok_count))
-    image_rows, ids_all, qkv_whole, out_whole = exchange(
+    ids = expert_ids[:, 0]
+    token = jnp.arange(tok_count, dtype=jnp.int32)
+    same = (expert_ids == ids[None, :]) & (token[:, None] < token[None, :])
+    codes = ids * capacity + jnp.sum(same.astype(jnp.int32), axis=0)
+    image_rows, codes_all, qkv_whole, out_whole = exchange(
         "enter",
         0,
         spreads=(tokens,),
-        smalls=(ids_block,),
+        smalls=(jnp.broadcast_to(codes[None, :], (8, tok_count)),),
         gathers=((qkv_weight.reshape(qkv_weight.shape[0], -1), 0), (out_weight, 1)),
     )
     normed = layer_norm(image_rows, ln1_gain).astype(jnp.bfloat16)
     projected = matmul(normed, qkv_whole).astype(jnp.bfloat16)
-    hidden_mine, normed_image, up_whole, down_whole = middle(
-        1, head_count, projected, out_whole, tokens, ln2_gain[None, :], ffn_in, ffn_out
-    )
-
-    ids_rows = ids_all.reshape(col_total, 8, tok_count)[:, 0]
-    expert_range = jnp.arange(expert_count, dtype=jnp.int32)
-    one_hot = (ids_rows[:, :, None] == expert_range).astype(jnp.int32)
-    earlier = jnp.cumsum(one_hot, axis=1) - one_hot
-    slot_index = jnp.sum(earlier * one_hot, axis=2)
-    block_index = jnp.arange(col_total, dtype=jnp.int32)[:, None]
+    codes_all = codes_all.reshape(col_total, 8, tok_count)[:, 0]
+    ids_rows, slot_index = codes_all // capacity, codes_all % capacity
+    block = jnp.arange(col_total, dtype=jnp.int32)[:, None]
+    plane, place = block // 4, block % 4 * capacity + slot_index
     home_row = 2 * ids_rows // col_total
     mine = (2 * ids_rows % col_total) // 2 == col_index // 2
     other = (home_row // 8 != row_index // 8).astype(jnp.int32)
-    step = (home_row // 2 - row_index // 2 + 8) % 4
-    chunk = step * 2 + home_row % 2
-    place = block_index * capacity + slot_index
-    rows = col_total * capacity
-    position = jnp.where(mine, (other * 8 + chunk) * rows + place, -1).reshape(seq_len)
+    chunk = (home_row // 2 - row_index // 2 + 8) % 4 * 2 + home_row % 2
+    half = 4 * capacity
+    rows = 2 * half
     slot_count = row_total * rows
-    slots = jnp.arange(slot_count, dtype=jnp.int32)
-    placing = (slots[:, None] == position[None, :]).astype(jnp.bfloat16)
-    half = rows // 2
-    crossed = jnp.where(place // half == col_index % 2, 8 * rows + chunk * half + place % half, -1)
-    source = jnp.where(mine, jnp.where(other == 1, crossed, chunk * rows + place), -1).reshape(seq_len)
+    position = jnp.where(mine, (other * 8 + chunk) * half + place, -1).reshape(1, seq_len)
+    position = jnp.broadcast_to(position, (8, seq_len))
+    crossed = jnp.where(plane == col_index % 2, (8 * rows) + chunk * half + place, -1)
+    source = jnp.where(mine, jnp.where(other == 1, crossed, chunk * rows + plane * half + place), -1).reshape(seq_len)
     returned_slots = jnp.arange(8 * (rows + half), dtype=jnp.int32)
     picking = (source[:, None] == returned_slots[None, :]).astype(jnp.bfloat16)
 
-    table = matmul(placing, normed_image).astype(jnp.bfloat16)
-    table = table.reshape(2, 4, 2, rows, model_width)
+    hidden_mine, down_whole, hidden_units, expert_rows = middle(
+        1, head_count, projected, out_whole, tokens, ln2_gain[None, :], ffn_in, ffn_out, position, rows
+    )
     full, part = (4, 2, rows, model_width), (4, 2, half, model_width)
-    relays = (2, 2, 2, half, model_width)
-    hidden_units, expert_rows = expert_call(
-        "dispatch",
-        dispatch_body,
-        3,
-        (normed_image, up_whole, table),
-        ((seq_len, up_whole.shape[1]), table.shape),
-        (full, relays),
-    )
     expert_units = up_gelu(expert_rows.reshape(slot_count, model_width), expert_in[0])
-    partial_out = matmul(expert_units, expert_out[0]).astype(jnp.bfloat16).reshape(table.shape)
+    partial_out = matmul(expert_units, expert_out[0]).astype(jnp.bfloat16).reshape(expert_rows.shape)
     dense, near, across = expert_call(
         "collect",
         collect_body,
         4,
         (hidden_units, down_whole, partial_out),
         ((seq_len, model_width), full, part),
-        (full, part, part, relays),
+        (full, part, part, (2, 2, rows, model_width)),
     )
-    rows_two = jnp.concatenate((near.reshape(-1, model_width), across.reshape(-1, model_width)))
-    (out,) = leave(5, dense, picking, rows_two, hidden_mine)
+    flat = lambda array: array.reshape(-1, model_width)
+    (out,) = leave(5, dense, picking, flat(near), flat(across), hidden_mine)
     return out
 
 

time: 291 us -> 229 us (0.79)
  Pallas kernels: 248 us -> 213 us
  matrix products: 20.3 us -> 8.38 us
  other arithmetic: 11.4 us -> 3.64 us
  local copies, waits for them, and re-layouts: 10.6 us -> 4.01 us
    pallas_call x5 -> x4, Pallas kernels: 240 us -> 205 us  [communicate(): pl.pallas_call(body, out_shape=shapes, in_specs=[pl.BlockSpec(memory_spac...]
    dot_general x3 -> x2, matrix products: 20.3 us -> 8.38 us  [matmul(): return jnp.dot(a, b, preferred_element_type=jnp.float32)]
    unnamed x12 -> x24, local copies, waits for them, and re-layouts: 8.33 us -> 3.84 us
where the time goes in v5:
time: 229 us
  Pallas kernels  213 us (93%)
  matrix products  8.38 us (4%)
  local copies, waits for them, and re-layouts  4.01 us (2%)
  other arithmetic  3.64 us (2%)
    pallas_call x4, Pallas kernels, communicate(): pl.pallas_call(body, out_shape=shapes, in_specs=[pl.BlockSpec(memory_spac...  205 us
    dot_general x2, matrix products, matmul(): return jnp.dot(a, b, preferred_element_type=jnp.float32)  8.38 us
    pallas_call x1, Pallas kernels, up_gelu(): pl.pallas_call(up_body, grid=(width // tile,), out_shape=jax.ShapeDtypeSt...  7.29 us

profile of v5, /device:TPU:2, one launch (start us, length us, event | category | flops | bytes accessed | tf_op | source)
XLA Modules:
  0.0 229.1 jit_solution(4458766339774965266)
XLA Ops:
  0.0 1.1 copy.14
  1.1 0.2 copy.15.refs_2_
  1.3 0.8 convert_reduce_fusion.1
  2.1 0.7 multiply_add_fusion
  2.8 0.0 copy-start
  2.8 1.0 copy-done
  3.8 0.0 copy-start.4
  3.8 0.8 copy-done.4
  4.7 39.7 %enter.1 = (bf16[1024,2048]{1,0:T(8,128)(2,1)S(1)}, s32[64,128]{1,0:T(8,128)S(1)}, bf16[2048,768]{1,0:T(8,128)(2,1)S(1)}, bf16[256,2048]{1,0:T(8,128)(2,1)S(1)}) custom-call(bf16[128,2048]{1,0:T(8,128)(2,1)S(1)} %copy-done, s32[8,128]{1,0:T(8,128)S(1)} %broadcast_in_dim.17.refs_1_, bf16[128,768]{1,0:T(8,128)(2,1)S(1)} %copy.15.refs_2_, ...), custom_call_target="tpu_custom_call" | custom-call | tf_op jit(solution)/shard_map/enter/pallas_call | solution.py:391
  44.3 0.1 fusion.33
  44.4 0.0 copy-start.6
  44.4 0.6 convert_reduce_fusion
  45.1 0.0 slice-start
  45.1 1.2 fusion.2
  46.3 0.0 copy-done.6
  46.3 0.0 copy-start.1
  46.3 0.0 copy-start.2
  46.3 0.0 copy-start.3
  46.4 0.0 copy-start.5
  46.4 0.0 slice-start.1
  46.4 3.7 %fusion.15.qkv = bf16[1024,768]{1,0:T(8,128)(2,1)S(1)} fusion(bf16[2048,768]{1,0:T(8,128)(2,1)S(1)} %get-tuple-element.17, bf16[1024,2048]{1,0:T(8,128)(2,1)S(1)} %get-tuple-element.16, f32[2048]{0:T(1024)S(1)} %copy-done.6, f32[1024]{0:T(1024)S(1)} %add_rsqrt_fusion, f32[1024]{0:T(1024)S(1)} %broadcast_multiply_fusion), kind=kOutput, calls=%fused_computation.14 | convolution fusion | flops 3232497664 | bytes 8929280 | tf_op jit(solution)/shard_map/dot_general | solution.py:723
  50.1 0.0 copy-done.1
  50.1 0.0 copy-done.2
  50.1 0.0 copy-done.3
  50.1 0.0 copy-done.5
  50.1 0.0 slice-start.2
  50.1 97.7 %middle.1 = (bf16[128,2048]{1,0:T(8,128)(2,1)S(1)}, bf16[1024,2048]{1,0:T(8,128)(2,1)S(1)}, bf16[1024,1024]{1,0:T(8,128)(2,1)S(1)}, bf16[2,4,2,32,2048]{4,3,2,1,0:T(8,128)(2,1)S(1)}) custom-call(bf16[1024,768]{1,0:T(8,128)(2,1)S(1)} %fusion.15.qkv, bf16[256,2048]{1,0:T(8,128)(2,1)S(1)} %get-tuple-element.18.weight, bf16[128,2048]{1,0:T(8,128)(2,1)S(1)} %copy-done.1, ...), custom_call_target="tpu_custom_call" | custom-call | tf_op jit(solution)/shard_map/middle/pallas_call | solution.py:391
  147.8 0.0 slice-done
  147.8 0.0 slice-done.1
  147.8 0.0 slice-start.3
  147.8 7.3 %up_gelu.1 = bf16[512,2048]{1,0:T(8,128)(2,1)S(1)} custom-call(bf16[512,2048]{1,0:T(8,128)(2,1)S(1)} %bitcast.42, bf16[2048,2048]{1,0:T(8,128)(2,1)S(1)} %bitcast.41), custom_call_target="tpu_custom_call" | custom-call | flops 4294967296 | bytes 12582912 | tf_op jit(solution)/shard_map/up_gelu/pallas_call | solution.py:696
  155.1 0.0 slice-done.2
  155.1 0.0 slice-done.3
  155.1 4.7 %fusion.12 = bf16[512,2048]{1,0:T(8,128)(2,1)S(1)} fusion(bf16[512,2048]{1,0:T(8,128)(2,1)S(1)} %up_gelu.1, bf16[1,2048,2048]{2,1,0:T(8,128)(2,1)S(1)} %bitcast.46), kind=kOutput, calls=%fused_computation.13 | convolution fusion | flops 4296015872 | bytes 12582912 | tf_op jit(solution)/shard_map/dot_general | solution.py:723
  159.9 29.7 %collect.1 = (bf16[1024,2048]{1,0:T(8,128)(2,1)S(1)}, bf16[4,2,32,2048]{3,2,1,0:T(8,128)(2,1)S(1)}, bf16[4,2,16,2048]{3,2,1,0:T(8,128)(2,1)S(1)}) custom-call(bf16[1024,1024]{1,0:T(8,128)(2,1)S(1)} %get-tuple-element.20.x_ref, bf16[1024,2048]{1,0:T(8,128)(2,1)S(1)} %get-tuple-element.21.w_ref, bf16[2,4,2,32,2048]{4,3,2,1,0:T(8,128)(2,1)S(1)} %bitcast.34), custom_call_target="tpu_custom_call" | custom-call | tf_op jit(solution)/shard_map/collect/pallas_call | solution.py:391
  189.5 0.2 fusion.18.picking
  189.7 38.5 %leave.1 = bf16[128,2048]{1,0:T(8,128)(2,1)S(1)} custom-call(bf16[1024,2048]{1,0:T(8,128)(2,1)S(1)} %get-tuple-element.23.dense, bf16[1024,384]{1,0:T(8,128)(2,1)S(1)} %fusion.18.picking, bf16[256,2048]{1,0:T(8,128)(2,1)S(1)} %bitcast.35, bf16[128,2048]{1,0:T(8,128)(2,1)S(1)} %bitcast.36, bf16[128,2048]{1,0:T(8,128)(2,1)S(1)} %get-tuple-element.26.hidden), custom_call_target="tpu_custom_call" | custom-call | tf_op jit(solution)/shard_map/leave/pallas_call | solution.py:391
  228.3 0.8 copy.17
  (9 shorter events, 0.0 us)
Async XLA Ops:
  2.8 1.0 copy-start
  3.8 0.8 copy-start.4
  44.4 1.9 copy-start.6
  45.1 102.7 %slice-start = ((s8[8388608]{0:T(1024)(128)(4,1)}), s8[4194304]{0:T(1024)(128)(4,1)S(1)}, s32[]{:S(2)}) async-start(s8[8388608]{0:T(1024)(128)(4,1)} %bitcast.39), calls=%async_computation | async-start | bytes 8388608
  46.3 3.7 %copy-start.1 = (bf16[128,2048]{1,0:T(8,128)(2,1)S(1)}, bf16[128,2048]{1,0:T(8,128)(2,1)}, u32[]{:S(2)}) copy-start(bf16[128,2048]{1,0:T(8,128)(2,1)} %tokens.1) | copy-start | bytes 1572868
  46.3 3.7 %copy-start.2 = (bf16[128,1024]{1,0:T(8,128)(2,1)S(1)}, bf16[128,1024]{1,0:T(8,128)(2,1)}, u32[]{:S(2)}) copy-start(bf16[128,1024]{1,0:T(8,128)(2,1)} %up.1) | copy-start | bytes 786436
  46.3 3.7 %copy-start.3 = (bf16[1024,128]{1,0:T(8,128)(2,1)S(1)}, bf16[1024,128]{1,0:T(8,128)(2,1)}, u32[]{:S(2)}) copy-start(bf16[1024,128]{1,0:T(8,128)(2,1)} %down.1) | copy-start | bytes 786436
  46.4 3.7 %copy-start.5 = (f32[2048]{0:T(1024)S(1)}, f32[2048]{0:T(1024)}, u32[]{:S(2)}) copy-start(f32[2048]{0:T(1024)} %param.14) | copy-start | bytes 24580
  46.4 101.4 %slice-start.1 = ((s8[8388608]{0:T(1024)(128)(4,1)}), s8[4194304]{0:T(1024)(128)(4,1)S(1)}, s32[]{:S(2)}) async-start(s8[8388608]{0:T(1024)(128)(4,1)} %bitcast.39), calls=%async_computation.1 | async-start | bytes 8388608
  50.1 105.0 %slice-start.2 = ((s8[8388608]{0:T(1024)(128)(4,1)}), s8[4194304]{0:T(1024)(128)(4,1)S(1)}, s32[]{:S(2)}) async-start(s8[8388608]{0:T(1024)(128)(4,1)} %bitcast.45), calls=%async_computation.2 | async-start | bytes 8388608
  147.8 7.3 %slice-start.3 = ((s8[8388608]{0:T(1024)(128)(4,1)}), s8[4194304]{0:T(1024)(128)(4,1)S(1)}, s32[]{:S(2)}) async-start(s8[8388608]{0:T(1024)(128)(4,1)} %bitcast.45), calls=%async_computation.3 | async-start | bytes 8388608

commit v6 on v5

--- a/solution.py
+++ b/solution.py
@@ -266,10 +266,12 @@
         out[:, pl.ds(pl.multiple_of(index * width, width), width)] = src[...]
 
 
-def reduce_scatter(net, fill, src, scratch, finish):
-    from_z, sums, far_a, near_a, acc_a, far_b, near_b, acc_b, plane, last = scratch
+def reduce_scatter(net, fill, src, scratch, finish, split, step=lambda action: action()):
+    far_b, near_b, acc_b, plane, last = scratch[:5]
+    if split:
+        from_z, sums, far_a, near_a, acc_a = scratch[5:]
     size = src.shape[0] // 8
-    a = SPLIT
+    a = split
     b = size - a
     x, low = net.x, net.low
 
@@ -293,6 +295,7 @@
                 arrival = net.copy(block(2, first, half), far.at[index], far.at[index], forward)
 
                 def add(index=index, forward=forward, first=first):
+                    need(3)
                     term = block(1 if forward == "x+" else -1, first, half)
                     acc[index] = far[index] + term[...]
                     net.spend(0.1)
@@ -317,10 +320,11 @@
         return sums.at[pl.ds((dx % 4) * a + first, count)]
 
     left = [4]
-    both = [3]
+    both = [3 if a else 2]
     wide = lambda value: value.astype(jnp.float32)
 
     def from_partner(k):
+        need(4)
         sums[pl.ds(k * a, a), :] = from_z[pl.ds(k * a, a), :] + src[rows(k, 0, 0, a), :]
         net.spend(0.1)
         left[0] -= 1
@@ -329,10 +333,13 @@
                 start()
 
     def to_partner(k):
+        if a == 0:
+            return
         landing = from_z.at[pl.ds(k * a, a)]
         net.when(net.copy(src.at[rows(k, 1, 0, a)], landing, landing, "z"), lambda: from_partner(k))
 
     def plane_done():
+        need(4)
         total = wide(near_b[0, 0]) + wide(near_b[0, 1]) + wide(src[rows(0, 1, a, b), :])
         plane[...] = total.astype(plane.dtype)
         net.spend(0.3)
@@ -342,32 +349,49 @@
         both[0] -= 1
         if both[0]:
             return
-        first = wide(near_a[0]) + wide(near_a[1]) + wide(sums[pl.ds(0, a), :])
-        second = wide(near_b[1, 0]) + wide(near_b[1, 1]) + wide(src[rows(0, 0, a, b), :]) + wide(last[...])
+        if a:
+            finish(0, wide(near_a[0]) + wide(near_a[1]) + wide(sums[pl.ds(0, a), :]))
+        total = wide(near_b[1, 0]) + wide(near_b[1, 1]) + wide(src[rows(0, 0, a, b), :]) + wide(last[...])
         net.spend(0.5)
-        finish(first, second)
+        finish(a, total)
 
     far_other, direct_other = ring(block_b(1), b, far_b.at[0], near_b.at[0], acc_b.at[0], plane_done)
     far_own, direct_own = ring(block_b(0), b, far_b.at[1], near_b.at[1], acc_b.at[1], arrived)
-    fill(lambda i: net.block_of(x + 2, lax.rem(low + 1 + i, 2)))
-    far_other()
-    far_own()
-    to_partner(2)
-    fill(lambda i: net.block_of(x + 1 - 2 * i, 1 - low))
-    direct_other()
-    to_partner(1)
-    to_partner(3)
-    fill(lambda i: net.block_of(x + 1 - 2 * i, low))
-    direct_own()
-    fill(lambda i: net.block_of(x, lax.rem(low + 1 + i, 2)))
-    to_partner(0)
-
-
-def scatter_scratch(size, width, dtype):
-    a = SPLIT
-    b = size - a
-    shapes = [(4 * a, width), (4 * a, width), (2, a // 2, width), (2, a, width), (2, a // 2, width)]
-    shapes += [(2, 2, b // 2, width), (2, 2, b, width), (2, 2, b // 2, width), (b, width), (b, width)]
+    def first():
+        fill(lambda i: net.block_of(x + 2, lax.rem(low + 1 + i, 2)))
+        far_other()
+        far_own()
+        to_partner(2)
+
+    def second():
+        fill(lambda i: net.block_of(x + 1 - 2 * i, 1 - low))
+        direct_other()
+        to_partner(1)
+        to_partner(3)
+
+    def third():
+        fill(lambda i: net.block_of(x + 1 - 2 * i, low))
+        direct_own()
+
+    def fourth():
+        fill(lambda i: net.block_of(x, lax.rem(low + 1 + i, 2)))
+        to_partner(0)
+
+    actions = [first, second, third, fourth]
+
+    def need(number):
+        while len(actions) > 4 - number:
+            actions.pop(0)()
+
+    for number in range(1, 5):
+        step(lambda number=number: need(number))
+
+
+def scatter_scratch(size, width, dtype, split):
+    a, b = split, size - split
+    shapes = [(2, 2, b // 2, width), (2, 2, b, width), (2, 2, b // 2, width), (b, width), (b, width)]
+    if a:
+        shapes += [(4 * a, width), (4 * a, width), (2, a // 2, width), (2, a, width), (2, a // 2, width)]
     return [pltpu.VMEM(shape, dtype) for shape in shapes]
 
 
@@ -500,18 +524,19 @@
     other = y_exchange(net, chunks(table.at[1, 0]), chunks(out.at[0], theirs), y_relay.at[3])
     ready = counted(3, lambda: up_tasks(net, image, up_whole, units))
 
-    def finish(first_rows, second_rows):
-        for start, total in ((0, first_rows), (SPLIT, second_rows)):
-            at = pl.ds(start, total.shape[0])
-            state = (tokens[at, :].astype(jnp.float32) + total).astype(jnp.bfloat16)
-            hidden[at, :] = state
-            normed[at, :] = layer_norm(state, gain[...]).astype(jnp.bfloat16)
+    def finish(start, total):
+        at = pl.ds(start, total.shape[0])
+        state = (tokens[at, :].astype(jnp.float32) + total).astype(jnp.bfloat16)
+        hidden[at, :] = state
+        normed[at, :] = layer_norm(state, gain[...]).astype(jnp.bfloat16)
+        if start == 0:
+            return
         net.spend(0.5)
         spread(net, normed, image, plane_done, image_done)
 
     gather(net, up, up_whole, up_relay, 0, ready)
     gather(net, down, down_whole, down_relay, 1)
-    reduce_scatter(net, fill, terms, rest[10:-2], finish)
+    reduce_scatter(net, fill, terms, rest[10:-2], finish, SPLIT)
     net.run()
 
 
@@ -538,50 +563,8 @@
         collective_id,
         (qkv, weight, tokens, gain, up, down, position),
         [made(size, width), gathered(down, 1), made(8 * size, up.shape[1]), made(2, 4, 2, slots, width)],
-        scratch + scatter_scratch(size, width, tokens.dtype),
+        scratch + scatter_scratch(size, width, tokens.dtype, SPLIT),
         24 + 22 + 2 * 22 + 8 + 4 * 10,
-    )
-
-
-def leave_body(dense, picking, near, across, hidden, out, terms, *rest):
-    net = Net(*rest[-2:])
-    net.greet(["x+", "x-", "z"])
-    size = hidden.shape[0]
-    count = near.shape[0]
-
-    def fill(column):
-        @pl.loop(0, 2)
-        def _(i):
-            at = pl.ds(pl.multiple_of(column(i) * size, size), size)
-
-            @pl.loop(0, dense.shape[1] // 512)
-            def _(j):
-                columns = pl.ds(pl.multiple_of(j * 512, 512), 512)
-                total = dense[at, columns].astype(jnp.float32)
-                total += matmul(picking[at, pl.ds(0, count)], near[:, columns])
-                total += matmul(picking[at, pl.ds(count, across.shape[0])], across[:, columns])
-                terms[at, columns] = total.astype(jnp.bfloat16)
-
-        net.spend(0.8)
-
-    def finish(first, second):
-        for start, total in ((0, first), (SPLIT, second)):
-            at = pl.ds(start, total.shape[0])
-            out[at, :] = (hidden[at, :].astype(jnp.float32) + total).astype(jnp.bfloat16)
-
-    reduce_scatter(net, fill, terms, rest[:-2], finish)
-    net.run()
-
-
-def leave(collective_id, dense, picking, near, across, hidden):
-    return communicate(
-        "leave",
-        leave_body,
-        collective_id,
-        (dense, picking, near, across, hidden),
-        [jax.ShapeDtypeStruct(hidden.shape, hidden.dtype)],
-        [pltpu.VMEM(dense.shape, dense.dtype)] + scatter_scratch(*hidden.shape, hidden.dtype),
-        24,
     )
 
 
@@ -638,50 +621,141 @@
         net.work(1.6, lambda j=j: piece(j))
 
 
-def down_tasks(net, x_ref, w_ref, out):
-    rows, width = out.shape
-    tile = min(256, rows)
-    span = min(512, width)
-
-    def piece(j):
-        columns = pl.ds(j * span, span)
-
-        @pl.loop(0, rows // tile)
-        def _(i):
-            at = pl.ds(pl.multiple_of(i * tile, tile), tile)
-            product = jnp.dot(x_ref[at, :], w_ref[:, columns], preferred_element_type=jnp.float32)
-            out[at, columns] = product.astype(out.dtype)
-
-    for j in range(width // span):
-        net.work(1.2, lambda j=j: piece(j))
-
-
-def collect_body(x_ref, w_ref, parts, dense, near, across, far, other, total, relay, send, recv):
-    net = Net(send, recv)
-    net.greet(["y+", "y-", "y+c", "y-c", "c", "z", "w"])
+def tail_body(units, down, parts, pick, hidden, out, *rest):
+    terms, pair, far, other, total, near, partial, found, packed, relay, y_relay = rest[:11]
+    net = Net(*rest[-2:])
+    net.greet(["x+", "x-", "y+", "y-", "y+c", "y-c", "c", "z", "w"])
     low = net.low
     half = parts.shape[3] // 2
+    size = hidden.shape[0]
     mine, theirs = pl.ds(pl.multiple_of(low * half, half), half), pl.ds(pl.multiple_of((1 - low) * half, half), half)
-
-    def landed(d):
+    count = packed.shape[1] // 4
+
+    def fill(column):
+        at = [pl.ds(pl.multiple_of(column(i) * size, size), size) for i in range(2)]
+        for i in range(2):
+            pair[pl.ds(i * size, size), :] = units[at[i], :]
+
+        @pl.loop(0, down.shape[1] // 256)
+        def _(j):
+            columns = pl.ds(pl.multiple_of(j * 256, 256), 256)
+            product = matmul(pair[...], down[:, columns]).astype(jnp.bfloat16)
+            for i in range(2):
+                terms[at[i], columns] = product[i * size : (i + 1) * size]
+
+    def pack(index):
+        flat = math.prod(found.shape[1:4])
+        row = lax.broadcasted_iota(jnp.int32, (count, flat), 0)
+        slot = lax.broadcasted_iota(jnp.int32, (count, flat), 1)
+        each = half // 4
+        same = (row // each == slot // half) & (row % each == slot % each)
+        for k in range(4):
+            chosen = same & (slot % half // each == lax.rem(net.x + k, 4))
+            chosen = jnp.where(chosen, 1.0, 0.0).astype(jnp.bfloat16)
+
+            @pl.loop(0, found.shape[4] // 512)
+            def _(j):
+                columns = pl.ds(pl.multiple_of(j * 512, 512), 512)
+                rows = found[index, :, :, :, columns].reshape(flat, 512)
+                value = matmul(chosen, rows).astype(jnp.bfloat16)
+                packed[index, k * count : (k + 1) * count, columns] = value
+
+        net.spend(0.6)
+
+    def send(index):
+        pack(index)
+        at = lambda k, first=0, rows=count: packed.at[index, pl.ds(k * count + first, rows)]
+        place = lambda k, first=0, rows=count: arrived_rows.at[index, pl.ds(k * count + first, rows)]
+        middle = count // 2
+        for i, forward in ((0, "x+"), (1, "x-")):
+
+            def onward(i=i, forward=forward):
+                dst = place(2, i * middle, middle)
+                net.when(net.copy(relay.at[index, i], dst, dst, forward), landed)
+
+            net.when(net.copy(at(2, i * middle, middle), relay.at[index, i], relay.at[index, i], forward), onward)
+        for k, forward in ((1, "x+"), (3, "x-")):
+            net.when(net.copy(at(k), place(k), place(k), forward), landed)
+
+    arrived_rows, dense = rest[11:13]
+
+    def finish_dense(start, total):
+        dense[pl.ds(start, total.shape[0]), :] = total
+        ready()
+
+    def combine():
+        flat = 4 * count
+        for index in range(2):
+            arrived_rows[index, pl.ds(0, count), :] = packed[index, pl.ds(0, count), :]
+
+        @pl.loop(0, out.shape[1] // 512)
+        def _(j):
+            columns = pl.ds(pl.multiple_of(j * 512, 512), 512)
+            value = hidden[:, columns].astype(jnp.float32) + dense[:, columns]
+            for index in range(2):
+                value += matmul(pick[:, pl.ds(index * flat, flat)], arrived_rows[index, :, columns])
+            out[:, columns] = value.astype(jnp.bfloat16)
+
+    ready = counted(9, combine)
+    landed = ready
+
+    def far_landed(d):
         def add():
             total[d] = far[d, :, theirs] + other[d]
             net.spend(0.2)
-            net.when(net.copy(total.at[d], across.at[d], across.at[d], "w"))
+            arrival = net.copy(total.at[d], found.at[1, d], found.at[1, d], "w")
+            net.when(arrival, complete[1])
 
         net.when(net.copy(far.at[d, :, mine], other.at[d], other.at[d], "z"), add)
 
-    counts = {d: counted(1 if d == 0 else 2, functools.partial(landed, d)) for d in range(4)}
-    second = y_exchange(net, chunks(parts.at[0]), chunks(near), relay.at[0])
-    first = y_exchange(net, chunks(parts.at[1]), chunks(far), relay.at[1], lambda d: counts[d](), lambda: start_all(second))
+    def near_landed(d):
+        def add():
+            found[0, d] = near[d, :, mine] + partial[d]
+            net.spend(0.2)
+            complete[0]()
+
+        net.when(net.copy(near.at[d, :, theirs], partial.at[d], partial.at[d], "z"), add)
+
+    complete = [counted(4, functools.partial(send, index)) for index in range(2)]
+    far_counts = {d: counted(1 if d == 0 else 2, functools.partial(far_landed, d)) for d in range(4)}
+    near_counts = {d: counted(1 if d == 0 else 2, functools.partial(near_landed, d)) for d in range(4)}
+    second = y_exchange(net, chunks(parts.at[0]), chunks(near), y_relay.at[0], lambda d: near_counts[d]())
+    first = y_exchange(net, chunks(parts.at[1]), chunks(far), y_relay.at[1], lambda d: far_counts[d](), lambda: start_all(second))
     start_all(first)
-    down_tasks(net, x_ref, w_ref, dense)
+    reduce_scatter(net, fill, terms, rest[13:-2], finish_dense, 0, lambda action: net.work(1.6, action))
     net.run()
 
 
-def expert_call(name, body, collective_id, arrays, shapes, scratch):
-    shapes = [jax.ShapeDtypeStruct(shape, jnp.bfloat16) for shape in shapes]
-    return communicate(name, body, collective_id, arrays, shapes, [pltpu.VMEM(shape, jnp.bfloat16) for shape in scratch], 40)
+def tail(collective_id, units, down, parts, pick, hidden):
+    size, width = hidden.shape
+    rows = parts.shape[3]
+    full, part = (4, 2, rows, width), (4, 2, rows // 2, width)
+    sixteen = lambda *shape: pltpu.VMEM(shape, hidden.dtype)
+    count = rows
+    scratch = [
+        sixteen(8 * size, width),
+        sixteen(2 * size, units.shape[1]),
+        sixteen(*full),
+        sixteen(*part),
+        sixteen(*part),
+        sixteen(*full),
+        sixteen(*part),
+        sixteen(2, *part),
+        sixteen(2, 4 * count, width),
+        sixteen(2, 2, count // 2, width),
+        sixteen(2, 2, rows, width),
+        sixteen(2, 4 * count, width),
+        pltpu.VMEM((size, width), jnp.float32),
+    ]
+    return communicate(
+        "tail",
+        tail_body,
+        collective_id,
+        (units, down, parts, pick, hidden),
+        [jax.ShapeDtypeStruct(hidden.shape, hidden.dtype)],
+        scratch + scatter_scratch(size, width, hidden.dtype, 0),
+        24 + 2 * 10 + 12 + 12,
+    )
 
 
 def up_body(x_ref, w_ref, o_ref):
@@ -771,27 +845,18 @@
     slot_count = row_total * rows
     position = jnp.where(mine, (other * 8 + chunk) * half + place, -1).reshape(1, seq_len)
     position = jnp.broadcast_to(position, (8, seq_len))
-    crossed = jnp.where(plane == col_index % 2, (8 * rows) + chunk * half + place, -1)
-    source = jnp.where(mine, jnp.where(other == 1, crossed, chunk * rows + plane * half + place), -1).reshape(seq_len)
-    returned_slots = jnp.arange(8 * (rows + half), dtype=jnp.int32)
-    picking = (source[:, None] == returned_slots[None, :]).astype(jnp.bfloat16)
+    home = ids // 4
+    turn = (home // 2 - row_index // 2 + 8) % 4 * 2 + home % 2
+    found = (col_index // 2 - ids % 4 + 4) % 4 * rows + turn * capacity + codes % capacity
+    found = jnp.where(home // 8 != row_index // 8, found + 4 * rows, found)
+    pick = (found[:, None] == jnp.arange(8 * rows, dtype=jnp.int32)[None, :]).astype(jnp.bfloat16)
 
     hidden_mine, down_whole, hidden_units, expert_rows = middle(
         1, head_count, projected, out_whole, tokens, ln2_gain[None, :], ffn_in, ffn_out, position, rows
     )
-    full, part = (4, 2, rows, model_width), (4, 2, half, model_width)
     expert_units = up_gelu(expert_rows.reshape(slot_count, model_width), expert_in[0])
     partial_out = matmul(expert_units, expert_out[0]).astype(jnp.bfloat16).reshape(expert_rows.shape)
-    dense, near, across = expert_call(
-        "collect",
-        collect_body,
-        4,
-        (hidden_units, down_whole, partial_out),
-        ((seq_len, model_width), full, part),
-        (full, part, part, (2, 2, rows, model_width)),
-    )
-    flat = lambda array: array.reshape(-1, model_width)
-    (out,) = leave(5, dense, picking, flat(near), flat(across), hidden_mine)
+    (out,) = tail(2, hidden_units, down_whole, partial_out, pick, hidden_mine)
     return out
 
 

time: 229 us -> 216 us (0.943)
  Pallas kernels: 213 us -> 198 us
    pallas_call x4 -> x3, Pallas kernels: 205 us -> 191 us  [communicate(): pl.pallas_call(body, out_shape=shapes, in_specs=[pl.BlockSpec(memory_spac...]
where the time goes in v6:
time: 216 us; the launch traced here: 215 us
  Pallas kernels  198 us (92%)
  matrix products  8.33 us (4%)
  local copies, waits for them, and re-layouts  4.01 us (2%)
  other arithmetic  3.54 us (2%)
    pallas_call x3, Pallas kernels, communicate(): pl.pallas_call(body, out_shape=shapes, in_specs=[pl.BlockSpec(memory_spac...  191 us
    dot_general x2, matrix products, matmul(): return jnp.dot(a, b, preferred_element_type=jnp.float32)  8.33 us
    pallas_call x1, Pallas kernels, up_gelu(): pl.pallas_call(up_body, grid=(width // tile,), out_shape=jax.ShapeDtypeSt...  7.25 us

profile of v6, /device:TPU:2, one launch (start us, length us, event | category | flops | bytes accessed | tf_op | source)
XLA Modules:
  0.0 214.5 jit_solution(17132527459877898464)
XLA Ops:
  0.0 0.8 convert_reduce_fusion.1
  0.8 0.7 multiply_add_fusion
  1.5 1.1 copy.14
  2.6 0.2 copy.15.refs_2_
  2.8 0.0 copy-start
  2.8 1.0 copy-done
  3.8 0.0 copy-start.4
  3.8 0.8 copy-done.4
  4.6 39.7 %enter.1 = (bf16[1024,2048]{1,0:T(8,128)(2,1)S(1)}, s32[64,128]{1,0:T(8,128)S(1)}, bf16[2048,768]{1,0:T(8,128)(2,1)S(1)}, bf16[256,2048]{1,0:T(8,128)(2,1)S(1)}) custom-call(bf16[128,2048]{1,0:T(8,128)(2,1)S(1)} %copy-done, s32[8,128]{1,0:T(8,128)S(1)} %broadcast_in_dim.7.refs_1_, bf16[128,768]{1,0:T(8,128)(2,1)S(1)} %copy.15.refs_2_, ...), custom_call_target="tpu_custom_call" | custom-call | tf_op jit(solution)/shard_map/enter/pallas_call | solution.py:415
  44.3 0.1 fusion.33
  44.4 0.0 copy-start.7
  44.4 0.6 convert_reduce_fusion
  45.0 0.0 slice-start
  45.0 1.2 fusion.2
  46.3 0.0 copy-done.7
  46.3 0.0 copy-start.1
  46.3 0.0 copy-start.2
  46.3 0.0 copy-start.3
  46.3 0.0 copy-start.5
  46.3 0.0 slice-start.1
  46.4 3.6 %fusion.15.qkv = bf16[1024,768]{1,0:T(8,128)(2,1)S(1)} fusion(bf16[2048,768]{1,0:T(8,128)(2,1)S(1)} %get-tuple-element.14, bf16[1024,2048]{1,0:T(8,128)(2,1)S(1)} %get-tuple-element.13, f32[2048]{0:T(1024)S(1)} %copy-done.7, f32[1024]{0:T(1024)S(1)} %add_rsqrt_fusion, f32[1024]{0:T(1024)S(1)} %broadcast_multiply_fusion), kind=kOutput, calls=%fused_computation.14 | convolution fusion | flops 3232497664 | bytes 8929280 | tf_op jit(solution)/shard_map/dot_general | solution.py:797
  50.0 0.0 copy-done.1
  50.0 0.0 copy-done.2
  50.0 0.0 copy-done.3
  50.0 0.0 copy-done.5
  50.0 0.0 slice-start.2
  50.0 97.6 %middle.1 = (bf16[128,2048]{1,0:T(8,128)(2,1)S(1)}, bf16[1024,2048]{1,0:T(8,128)(2,1)S(1)}, bf16[1024,1024]{1,0:T(8,128)(2,1)S(1)}, bf16[2,4,2,32,2048]{4,3,2,1,0:T(8,128)(2,1)S(1)}) custom-call(bf16[1024,768]{1,0:T(8,128)(2,1)S(1)} %fusion.15.qkv, bf16[256,2048]{1,0:T(8,128)(2,1)S(1)} %get-tuple-element.15.weight, bf16[128,2048]{1,0:T(8,128)(2,1)S(1)} %copy-done.1, ...), custom_call_target="tpu_custom_call" | custom-call | tf_op jit(solution)/shard_map/middle/pallas_call | solution.py:415
  147.7 0.0 slice-done
  147.7 0.0 slice-done.1
  147.7 0.0 slice-start.3
  147.7 7.3 %up_gelu.1 = bf16[512,2048]{1,0:T(8,128)(2,1)S(1)} custom-call(bf16[512,2048]{1,0:T(8,128)(2,1)S(1)} %bitcast.32, bf16[2048,2048]{1,0:T(8,128)(2,1)S(1)} %bitcast.31), custom_call_target="tpu_custom_call" | custom-call | flops 4294967296 | bytes 12582912 | tf_op jit(solution)/shard_map/up_gelu/pallas_call | solution.py:770
  155.0 0.0 slice-done.2
  155.0 0.0 slice-done.3
  155.0 0.0 copy-start.6
  155.0 4.7 %fusion.12 = bf16[512,2048]{1,0:T(8,128)(2,1)S(1)} fusion(bf16[512,2048]{1,0:T(8,128)(2,1)S(1)} %up_gelu.1, bf16[1,2048,2048]{2,1,0:T(8,128)(2,1)S(1)} %bitcast.37), kind=kOutput, calls=%fused_computation.13 | convolution fusion | flops 4296015872 | bytes 12582912 | tf_op jit(solution)/shard_map/dot_general | solution.py:797
  159.7 0.0 copy-done.6
  159.8 0.1 fusion.18.pick
  159.9 53.9 %tail.1 = bf16[128,2048]{1,0:T(8,128)(2,1)S(1)} custom-call(bf16[1024,1024]{1,0:T(8,128)(2,1)S(1)} %get-tuple-element.17.units, bf16[1024,2048]{1,0:T(8,128)(2,1)S(1)} %get-tuple-element.18.down, bf16[2,4,2,32,2048]{4,3,2,1,0:T(8,128)(2,1)S(1)} %bitcast.26, bf16[128,256]{1,0:T(8,128)(2,1)S(1)} %fusion.18.pick, bf16[128,2048]{1,0:T(8,128)(2,1)S(1)} %get-tuple-element.20.hidden), custom_call_target="tpu_custom_call" | custom-call | tf_op jit(solution)/shard_map/tail/pallas_call | solution.py:415
  213.8 0.8 copy.17
  (9 shorter events, 0.1 us)
Async XLA Ops:
  2.8 1.0 copy-start
  3.8 0.8 copy-start.4
  44.4 1.9 copy-start.7
  45.0 102.7 %slice-start = ((s8[8388608]{0:T(1024)(128)(4,1)}), s8[4194304]{0:T(1024)(128)(4,1)S(1)}, s32[]{:S(2)}) async-start(s8[8388608]{0:T(1024)(128)(4,1)} %bitcast.29), calls=%async_computation | async-start | bytes 8388608
  46.3 3.7 %copy-start.1 = (bf16[128,2048]{1,0:T(8,128)(2,1)S(1)}, bf16[128,2048]{1,0:T(8,128)(2,1)}, u32[]{:S(2)}) copy-start(bf16[128,2048]{1,0:T(8,128)(2,1)} %tokens.1) | copy-start | bytes 1572868
  46.3 3.7 %copy-start.2 = (bf16[128,1024]{1,0:T(8,128)(2,1)S(1)}, bf16[128,1024]{1,0:T(8,128)(2,1)}, u32[]{:S(2)}) copy-start(bf16[128,1024]{1,0:T(8,128)(2,1)} %up.1) | copy-start | bytes 786436
  46.3 3.7 %copy-start.3 = (bf16[1024,128]{1,0:T(8,128)(2,1)S(1)}, bf16[1024,128]{1,0:T(8,128)(2,1)}, u32[]{:S(2)}) copy-start(bf16[1024,128]{1,0:T(8,128)(2,1)} %down.1) | copy-start | bytes 786436
  46.3 3.7 %copy-start.5 = (f32[2048]{0:T(1024)S(1)}, f32[2048]{0:T(1024)}, u32[]{:S(2)}) copy-start(f32[2048]{0:T(1024)} %param.14) | copy-start | bytes 24580
  46.3 101.4 %slice-start.1 = ((s8[8388608]{0:T(1024)(128)(4,1)}), s8[4194304]{0:T(1024)(128)(4,1)S(1)}, s32[]{:S(2)}) async-start(s8[8388608]{0:T(1024)(128)(4,1)} %bitcast.29), calls=%async_computation.1 | async-start | bytes 8388608
  50.0 105.0 %slice-start.2 = ((s8[8388608]{0:T(1024)(128)(4,1)}), s8[4194304]{0:T(1024)(128)(4,1)S(1)}, s32[]{:S(2)}) async-start(s8[8388608]{0:T(1024)(128)(4,1)} %bitcast.36), calls=%async_computation.2 | async-start | bytes 8388608
  147.7 7.3 %slice-start.3 = ((s8[8388608]{0:T(1024)(128)(4,1)}), s8[4194304]{0:T(1024)(128)(4,1)S(1)}, s32[]{:S(2)}) async-start(s8[8388608]{0:T(1024)(128)(4,1)} %bitcast.36), calls=%async_computation.3 | async-start | bytes 8388608
  155.0 4.7 %copy-start.6 = (s32[128,1]{0,1:T(1,128)S(1)}, s32[128,1]{0,1:T(1,128)}, u32[]{:S(2)}) copy-start(s32[128,1]{0,1:T(1,128)} %param.17) | copy-start | bytes 1540

commit v7 on v6

--- a/solution.py
+++ b/solution.py
@@ -410,12 +410,13 @@
     net.run()
 
 
-def communicate(name, body, collective_id, arrays, shapes, scratch, copies):
-    used = sum(math.prod(ref.shape) * jnp.dtype(ref.dtype).itemsize for ref in scratch)
+def communicate(name, body, collective_id, arrays, shapes, scratch, copies, outside=()):
+    used = sum(math.prod(r.shape) * jnp.dtype(r.dtype).itemsize for r in scratch if r.memory_space == pltpu.VMEM)
+    spaces = [pl.ANY if i in outside else pltpu.VMEM for i in range(len(arrays))]
     return pl.pallas_call(
         body,
         out_shape=shapes,
-        in_specs=[pl.BlockSpec(memory_space=pltpu.VMEM)] * len(arrays),
+        in_specs=[pl.BlockSpec(memory_space=space) for space in spaces],
         out_specs=[pl.BlockSpec(memory_space=pltpu.VMEM)] * len(shapes),
         scratch_shapes=scratch + [pltpu.SemaphoreType.DMA((copies,)), pltpu.SemaphoreType.DMA((copies,))],
         compiler_params=pltpu.CompilerParams(
@@ -621,8 +622,16 @@
         net.work(1.6, lambda j=j: piece(j))
 
 
-def tail_body(units, down, parts, pick, hidden, out, *rest):
+def tail_body(units, down, rows, expert_in, expert_out, pick, hidden, out, *rest):
     terms, pair, far, other, total, near, partial, found, packed, relay, y_relay = rest[:11]
+    arrived_rows, dense, parts, inner, weights, fetched = rest[11:17]
+    tiles, span = weights.shape[1], weights.shape[3]
+    fetches = []
+    for i, source in enumerate((expert_in, expert_out)):
+        for j in range(tiles):
+            fetch = pltpu.make_async_copy(source.at[:, pl.ds(j * span, span)], weights.at[i, j], fetched.at[i, j])
+            fetch.start()
+            fetches.append(fetch)
     net = Net(*rest[-2:])
     net.greet(["x+", "x-", "y+", "y-", "y+c", "y-c", "c", "z", "w"])
     low = net.low
@@ -677,7 +686,25 @@
         for k, forward in ((1, "x+"), (3, "x-")):
             net.when(net.copy(at(k), place(k), place(k), forward), landed)
 
-    arrived_rows, dense = rest[11:13]
+    flat_rows = math.prod(parts.shape[1:4])
+
+    def expert_up(j):
+        fetches[j].wait()
+
+        @pl.loop(0, 2)
+        def _(i):
+            value = matmul(rows[i].reshape(flat_rows, rows.shape[4]), weights[0, j])
+            value = value * (1.0 + lax.erf(value * (0.5**0.5))) * 0.5
+            inner[i, :, pl.ds(j * span, span)] = value.astype(inner.dtype)
+
+        net.spend(1.5)
+
+    def expert_down(i, j):
+        if i == 1:
+            fetches[tiles + j].wait()
+        value = matmul(inner[i], weights[1, j]).astype(parts.dtype)
+        parts[i, :, :, :, pl.ds(j * span, span)] = value.reshape(parts.shape[1:4] + (span,))
+        net.spend(0.7)
 
     def finish_dense(start, total):
         dense[pl.ds(start, total.shape[0]), :] = total
@@ -720,18 +747,33 @@
     far_counts = {d: counted(1 if d == 0 else 2, functools.partial(far_landed, d)) for d in range(4)}
     near_counts = {d: counted(1 if d == 0 else 2, functools.partial(near_landed, d)) for d in range(4)}
     second = y_exchange(net, chunks(parts.at[0]), chunks(near), y_relay.at[0], lambda d: near_counts[d]())
-    first = y_exchange(net, chunks(parts.at[1]), chunks(far), y_relay.at[1], lambda d: far_counts[d](), lambda: start_all(second))
+    go = counted(2, lambda: start_all(second))
+    first = y_exchange(net, chunks(parts.at[1]), chunks(far), y_relay.at[1], lambda d: far_counts[d](), go)
+    steps = []
+    reduce_scatter(net, fill, terms, rest[17:-2], finish_dense, 0, steps.append)
+    steps[0]()
+    net.spend(1.6)
+    for j in range(tiles):
+        expert_up(j)
+    for j in range(tiles):
+        expert_down(1, j)
     start_all(first)
-    reduce_scatter(net, fill, terms, rest[13:-2], finish_dense, 0, lambda action: net.work(1.6, action))
+    for j in range(tiles):
+        expert_down(0, j)
+    go()
+    for step in steps[1:]:
+        step()
+        net.spend(1.6)
     net.run()
 
 
-def tail(collective_id, units, down, parts, pick, hidden):
+def tail(collective_id, units, down, rows, expert_in, expert_out, pick, hidden):
     size, width = hidden.shape
-    rows = parts.shape[3]
-    full, part = (4, 2, rows, width), (4, 2, rows // 2, width)
+    count = rows.shape[3]
+    full, part = (4, 2, count, width), (4, 2, count // 2, width)
+    depth, inside = expert_in.shape
+    span = min(512, width)
     sixteen = lambda *shape: pltpu.VMEM(shape, hidden.dtype)
-    count = rows
     scratch = [
         sixteen(8 * size, width),
         sixteen(2 * size, units.shape[1]),
@@ -743,47 +785,24 @@
         sixteen(2, *part),
         sixteen(2, 4 * count, width),
         sixteen(2, 2, count // 2, width),
-        sixteen(2, 2, rows, width),
+        sixteen(2, 2, count, width),
         sixteen(2, 4 * count, width),
         pltpu.VMEM((size, width), jnp.float32),
+        sixteen(2, *full),
+        sixteen(2, 8 * count, inside),
+        sixteen(2, width // span, depth, span),
+        pltpu.SemaphoreType.DMA((2, width // span)),
     ]
     return communicate(
         "tail",
         tail_body,
         collective_id,
-        (units, down, parts, pick, hidden),
+        (units, down, rows, expert_in, expert_out, pick, hidden),
         [jax.ShapeDtypeStruct(hidden.shape, hidden.dtype)],
         scratch + scatter_scratch(size, width, hidden.dtype, 0),
         24 + 2 * 10 + 12 + 12,
+        outside=(3, 4),
     )
-
-
-def up_body(x_ref, w_ref, o_ref):
-    inner = jnp.dot(x_ref[...], w_ref[...], preferred_element_type=jnp.float32)
-    o_ref[...] = (inner * (1.0 + lax.erf(inner * (0.5**0.5))) * 0.5).astype(o_ref.dtype)
-
-
-def up_gelu(x, w):
-    rows, depth = x.shape
-    width = w.shape[1]
-    tile = min(width, 256)
-    return pl.pallas_call(
-        up_body,
-        grid=(width // tile,),
-        out_shape=jax.ShapeDtypeStruct((rows, width), jnp.bfloat16),
-        in_specs=[
-            pl.BlockSpec((rows, depth), lambda j: (0, 0)),
-            pl.BlockSpec((depth, tile), lambda j: (0, j)),
-        ],
-        out_specs=pl.BlockSpec((rows, tile), lambda j: (0, j)),
-        compiler_params=pltpu.CompilerParams(vmem_limit_bytes=32 * 2**20),
-        cost_estimate=pl.CostEstimate(
-            flops=2 * rows * depth * width,
-            bytes_accessed=2 * (rows * depth + depth * width + rows * width),
-            transcendentals=0,
-        ),
-        name="up_gelu",
-    )(x, w)
 
 
 def layer_norm(row_data, gain_vector):
@@ -854,9 +873,7 @@
     hidden_mine, down_whole, hidden_units, expert_rows = middle(
         1, head_count, projected, out_whole, tokens, ln2_gain[None, :], ffn_in, ffn_out, position, rows
     )
-    expert_units = up_gelu(expert_rows.reshape(slot_count, model_width), expert_in[0])
-    partial_out = matmul(expert_units, expert_out[0]).astype(jnp.bfloat16).reshape(expert_rows.shape)
-    (out,) = tail(2, hidden_units, down_whole, partial_out, pick, hidden_mine)
+    (out,) = tail(2, hidden_units, down_whole, expert_rows, expert_in[0], expert_out[0], pick, hidden_mine)
     return out
 
 

time: 216 us -> 221 us (1.023)
  Pallas kernels: 198 us -> 209 us
  matrix products: 8.33 us -> 3.7 us
    pallas_call x3, Pallas kernels: 191 us -> 209 us  [communicate(): pl.pallas_call(body, out_shape=shapes, in_specs=[pl.BlockSpec(memory_spac...]
    pallas_call x1 -> x0, Pallas kernels: 7.25 us -> none  [up_gelu(): pl.pallas_call(up_body, grid=(width // tile,), out_shape=jax.ShapeDtypeSt...]
    dot_general x2 -> x1, matrix products: 8.33 us -> 3.7 us  [matmul(): return jnp.dot(a, b, preferred_element_type=jnp.float32)]
where the time goes in v7:
time: 221 us
  Pallas kernels  209 us (95%)
  local copies, waits for them, and re-layouts  3.99 us (2%)
  matrix products  3.7 us (2%)
  other arithmetic  3.54 us (2%)
    pallas_call x3, Pallas kernels, communicate(): pl.pallas_call(body, out_shape=shapes, in_specs=[pl.BlockSpec(memory_spac...  209 us

profile of v7, /device:TPU:2, one launch (start us, length us, event | category | flops | bytes accessed | tf_op | source)
XLA Modules:
  0.0 220.8 jit_solution(12044199598196774989)
XLA Ops:
  0.0 0.8 convert_reduce_fusion.1
  0.8 0.7 multiply_add_fusion
  1.5 1.1 copy.14
  2.6 0.2 copy.15.refs_2_
  2.8 0.0 copy-start
  2.8 1.0 copy-done
  3.8 0.0 copy-start.4
  3.8 0.8 copy-done.4
  4.7 39.7 %enter.1 = (bf16[1024,2048]{1,0:T(8,128)(2,1)S(1)}, s32[64,128]{1,0:T(8,128)S(1)}, bf16[2048,768]{1,0:T(8,128)(2,1)S(1)}, bf16[256,2048]{1,0:T(8,128)(2,1)S(1)}) custom-call(bf16[128,2048]{1,0:T(8,128)(2,1)S(1)} %copy-done, s32[8,128]{1,0:T(8,128)S(1)} %broadcast_in_dim.7.refs_1_, bf16[128,768]{1,0:T(8,128)(2,1)S(1)} %copy.15.refs_2_, ...), custom_call_target="tpu_custom_call" | custom-call | tf_op jit(solution)/shard_map/enter/pallas_call | solution.py:416
  44.3 0.1 fusion.28
  44.4 0.0 copy-start.7
  44.4 0.6 convert_reduce_fusion
  45.0 1.2 fusion.2
  46.3 0.0 copy-done.7
  46.3 0.0 copy-start.1
  46.3 0.0 copy-start.2
  46.3 0.0 copy-start.3
  46.3 0.0 copy-start.5
  46.3 0.0 copy-start.6
  46.4 3.7 %fusion.10.qkv = bf16[1024,768]{1,0:T(8,128)(2,1)S(1)} fusion(bf16[2048,768]{1,0:T(8,128)(2,1)S(1)} %get-tuple-element.14, bf16[1024,2048]{1,0:T(8,128)(2,1)S(1)} %get-tuple-element.13, f32[2048]{0:T(1024)S(1)} %copy-done.7, f32[1024]{0:T(1024)S(1)} %add_rsqrt_fusion, f32[1024]{0:T(1024)S(1)} %broadcast_multiply_fusion), kind=kOutput, calls=%fused_computation.11 | convolution fusion | flops 3232497664 | bytes 8929280 | tf_op jit(solution)/shard_map/dot_general | solution.py:816
  50.1 0.0 copy-done.1
  50.1 0.0 copy-done.2
  50.1 0.0 copy-done.3
  50.1 0.0 copy-done.5
  50.1 97.6 %middle.1 = (bf16[128,2048]{1,0:T(8,128)(2,1)S(1)}, bf16[1024,2048]{1,0:T(8,128)(2,1)S(1)}, bf16[1024,1024]{1,0:T(8,128)(2,1)S(1)}, bf16[2,4,2,32,2048]{4,3,2,1,0:T(8,128)(2,1)S(1)}) custom-call(bf16[1024,768]{1,0:T(8,128)(2,1)S(1)} %fusion.10.qkv, bf16[256,2048]{1,0:T(8,128)(2,1)S(1)} %get-tuple-element.15.weight, bf16[128,2048]{1,0:T(8,128)(2,1)S(1)} %copy-done.1, ...), custom_call_target="tpu_custom_call" | custom-call | tf_op jit(solution)/shard_map/middle/pallas_call | solution.py:416
  147.8 0.0 copy-done.6
  147.8 0.1 fusion.13.pick
  147.9 72.1 %tail.1 = bf16[128,2048]{1,0:T(8,128)(2,1)S(1)} custom-call(bf16[1024,1024]{1,0:T(8,128)(2,1)S(1)} %get-tuple-element.17.units, bf16[1024,2048]{1,0:T(8,128)(2,1)S(1)} %get-tuple-element.18.down, bf16[2,4,2,32,2048]{4,3,2,1,0:T(8,128)(2,1)S(1)} %get-tuple-element.19.rows, bf16[2048,2048]{1,0:T(8,128)(2,1)} %bitcast.21, bf16[2048,2048]{1,0:T(8,128)(2,1)} %bitcast.22, ...), custom_call_target="tpu_custom_call" | custom-call | tf_op jit(solution)/shard_map/tail/pallas_call | solution.py:416
  220.0 0.8 copy.17
  (7 shorter events, 0.1 us)
Async XLA Ops:
  2.8 1.0 copy-start
  3.8 0.8 copy-start.4
  44.4 1.9 copy-start.7
  46.3 3.8 %copy-start.1 = (bf16[128,2048]{1,0:T(8,128)(2,1)S(1)}, bf16[128,2048]{1,0:T(8,128)(2,1)}, u32[]{:S(2)}) copy-start(bf16[128,2048]{1,0:T(8,128)(2,1)} %tokens.1) | copy-start | bytes 1572868
  46.3 3.8 %copy-start.2 = (bf16[128,1024]{1,0:T(8,128)(2,1)S(1)}, bf16[128,1024]{1,0:T(8,128)(2,1)}, u32[]{:S(2)}) copy-start(bf16[128,1024]{1,0:T(8,128)(2,1)} %up.1) | copy-start | bytes 786436
  46.3 3.8 %copy-start.3 = (bf16[1024,128]{1,0:T(8,128)(2,1)S(1)}, bf16[1024,128]{1,0:T(8,128)(2,1)}, u32[]{:S(2)}) copy-start(bf16[1024,128]{1,0:T(8,128)(2,1)} %down.1) | copy-start | bytes 786436
  46.3 3.8 %copy-start.5 = (f32[2048]{0:T(1024)S(1)}, f32[2048]{0:T(1024)}, u32[]{:S(2)}) copy-start(f32[2048]{0:T(1024)} %param.14) | copy-start | bytes 24580
  46.3 101.4 %copy-start.6 = (s32[128,1]{0,1:T(1,128)S(1)}, s32[128,1]{0,1:T(1,128)}, u32[]{:S(2)}) copy-start(s32[128,1]{0,1:T(1,128)} %param.17) | copy-start | bytes 1540

commit v8 on v7

--- a/solution.py
+++ b/solution.py
@@ -266,7 +266,7 @@
         out[:, pl.ds(pl.multiple_of(index * width, width), width)] = src[...]
 
 
-def reduce_scatter(net, fill, src, scratch, finish, split, step=lambda action: action()):
+def reduce_scatter(net, fill, src, scratch, finish, split, step=lambda action: action(), gate=lambda action: action()):
     far_b, near_b, acc_b, plane, last = scratch[:5]
     if split:
         from_z, sums, far_a, near_a, acc_a = scratch[5:]
@@ -343,7 +343,7 @@
         total = wide(near_b[0, 0]) + wide(near_b[0, 1]) + wide(src[rows(0, 1, a, b), :])
         plane[...] = total.astype(plane.dtype)
         net.spend(0.3)
-        net.when(net.copy(plane, last, last, "z"), arrived)
+        gate(lambda: net.when(net.copy(plane, last, last, "z"), arrived))
 
     def arrived():
         both[0] -= 1
@@ -410,7 +410,7 @@
     net.run()
 
 
-def communicate(name, body, collective_id, arrays, shapes, scratch, copies, outside=()):
+def communicate(name, body, collective_id, arrays, shapes, scratch, copies, outside=(), spare=6 * 2**20):
     used = sum(math.prod(r.shape) * jnp.dtype(r.dtype).itemsize for r in scratch if r.memory_space == pltpu.VMEM)
     spaces = [pl.ANY if i in outside else pltpu.VMEM for i in range(len(arrays))]
     return pl.pallas_call(
@@ -420,7 +420,7 @@
         out_specs=[pl.BlockSpec(memory_space=pltpu.VMEM)] * len(shapes),
         scratch_shapes=scratch + [pltpu.SemaphoreType.DMA((copies,)), pltpu.SemaphoreType.DMA((copies,))],
         compiler_params=pltpu.CompilerParams(
-            collective_id=collective_id, has_side_effects=True, vmem_limit_bytes=used + 6 * 2**20
+            collective_id=collective_id, has_side_effects=True, vmem_limit_bytes=min(used + spare, 62 * 2**20)
         ),
         name=name,
     )(*arrays)
@@ -450,8 +450,25 @@
     )
 
 
-def middle_body(heads, qkv, weight, tokens, gain, up, down, position, hidden, down_whole, units, out, *rest):
+def block_body(heads, qkv, weight, tokens, gain, up, down, position, expert_in, expert_out, pick, result, *rest):
     terms, mixed, normed, image, up_whole, table, far, y_relay, up_relay, down_relay = rest[:10]
+    hidden, down_whole, units, out, pair, weights, fetched = rest[10:17]
+    held, _, span = weights.shape
+    tiles = expert_in.shape[1] // span
+    fetches = []
+
+    def fetch():
+        t = len(fetches)
+        if t == 3 * tiles:
+            return
+        source = expert_in if t < tiles else expert_out
+        tile = source.at[:, pl.ds(t % tiles * span, span)]
+        copy = pltpu.make_async_copy(tile, weights.at[t % held], fetched.at[t])
+        copy.start()
+        fetches.append(copy)
+
+    for _ in range(held):
+        fetch()
     net = Net(*rest[-2:])
     net.greet(["x+", "x-", "z", "y+", "y-", "w", "c", "y+c", "y-c"])
     size = tokens.shape[0]
@@ -472,10 +489,11 @@
                 scores = lax.dot_general(
                     qkv[at, part(0)], qkv[:, part(1)], (((1,), (1,)), ((), ())), preferred_element_type=jnp.float32
                 )
-                scores = scores * (dim ** (-0.5))
-                weights = jnp.exp(scores - jnp.max(scores, axis=-1, keepdims=True))
-                chances = (weights / jnp.sum(weights, axis=-1, keepdims=True)).astype(jnp.bfloat16)
-                mixed[:, pl.ds(pl.multiple_of(h * dim, dim), dim)] = matmul(chances, qkv[:, part(2)]).astype(jnp.bfloat16)
+                scale = dim ** (-0.5) * math.log2(math.e)
+                chances = jnp.exp2((scores - jnp.max(scores, axis=-1, keepdims=True)) * scale)
+                total = jnp.sum(chances, axis=-1, keepdims=True)
+                value = matmul(chances.astype(jnp.bfloat16), qkv[:, part(2)]) / total
+                mixed[:, pl.ds(pl.multiple_of(h * dim, dim), dim)] = value.astype(jnp.bfloat16)
 
             @pl.loop(0, weight.shape[1] // 512)
             def _(j):
@@ -483,6 +501,20 @@
                 terms[at, columns] = matmul(mixed[...], weight[:, columns]).astype(jnp.bfloat16)
 
         net.spend(2.6)
+
+    def fill_dense(column):
+        while early:
+            early.pop().wait_send()
+        at = [pl.ds(pl.multiple_of(column(i) * size, size), size) for i in range(2)]
+        for i in range(2):
+            pair[pl.ds(i * size, size), :] = units[at[i], :]
+
+        @pl.loop(0, down_whole.shape[1] // 512)
+        def _(j):
+            columns = pl.ds(pl.multiple_of(j * 512, 512), 512)
+            product = matmul(pair[...], down_whole[:, columns]).astype(jnp.bfloat16)
+            for i in range(2):
+                terms[at[i], columns] = product[i * size : (i + 1) * size]
 
     def place(index, plane):
         rows = pl.ds(pl.multiple_of(plane * 4 * size, 4 * size), 4 * size)
@@ -519,11 +551,22 @@
         start_all(other)
         ready()
 
-    own = y_exchange(net, chunks(table.at[0, 0]), chunks(out.at[0], mine), y_relay.at[0])
-    first = y_exchange(net, chunks(far, theirs), chunks(out.at[1], theirs), y_relay.at[1])
-    last = y_exchange(net, chunks(far, mine), chunks(out.at[1], mine), y_relay.at[2])
-    other = y_exchange(net, chunks(table.at[1, 0]), chunks(out.at[0], theirs), y_relay.at[3])
-    ready = counted(3, lambda: up_tasks(net, image, up_whole, units))
+    finish_dense, start_expert, gate = returning(
+        net, out, pick, hidden, result, weights, fetches, fetch, *rest[17:30]
+    )
+    dispatched = counted(28, start_expert)
+    came = lambda d: dispatched()
+    own = y_exchange(net, chunks(table.at[0, 0]), chunks(out.at[0], mine), y_relay.at[0], came)
+    first = y_exchange(net, chunks(far, theirs), chunks(out.at[1], theirs), y_relay.at[1], came)
+    last = y_exchange(net, chunks(far, mine), chunks(out.at[1], mine), y_relay.at[2], came)
+    other = y_exchange(net, chunks(table.at[1, 0]), chunks(out.at[0], theirs), y_relay.at[3], came)
+    early = []
+
+    def dense():
+        up_tasks(net, image, up_whole, units)
+        reduce_scatter(net, fill_dense, terms, rest[30:40], finish_dense, 32, lambda action: net.work(1.4, action), gate)
+
+    ready = counted(4, dense)
 
     def finish(start, total):
         at = pl.ds(start, total.shape[0])
@@ -532,40 +575,66 @@
         normed[at, :] = layer_norm(state, gain[...]).astype(jnp.bfloat16)
         if start == 0:
             return
+        early.extend(net.finish)
+        net.finish.clear()
         net.spend(0.5)
         spread(net, normed, image, plane_done, image_done)
 
     gather(net, up, up_whole, up_relay, 0, ready)
-    gather(net, down, down_whole, down_relay, 1)
-    reduce_scatter(net, fill, terms, rest[10:-2], finish, SPLIT)
+    gather(net, down, down_whole, down_relay, 1, ready)
+    reduce_scatter(net, fill, terms, rest[40:-2], finish, SPLIT)
     net.run()
 
 
-def middle(collective_id, heads, qkv, weight, tokens, gain, up, down, position, slots):
+def whole_block(collective_id, heads, qkv, weight, tokens, gain, up, down, position, expert_in, expert_out, pick, slots):
     size, width = tokens.shape
-    image = (8 * size, width)
+    depth, inside = expert_in.shape
+    span = min(512, width)
+    full, part = (4, 2, slots, width), (4, 2, slots // 2, width)
     sixteen = lambda *shape: pltpu.VMEM(shape, tokens.dtype)
     scratch = [
-        sixteen(*image),
+        sixteen(8 * size, width),
         sixteen(size, weight.shape[0]),
         sixteen(size, width),
-        sixteen(*image),
+        sixteen(8 * size, width),
         sixteen(*gathered(up, 0).shape),
-        sixteen(2, 2, 4, 2, slots // 2, width),
-        sixteen(4, 2, slots, width),
+        sixteen(2, 2, *part),
+        sixteen(*full),
         sixteen(4, 2, slots // 2, width),
         relay_of(up),
         relay_of(down),
+        sixteen(size, width),
+        sixteen(*gathered(down, 1).shape),
+        sixteen(8 * size, up.shape[1]),
+        sixteen(2, *full),
+        sixteen(2 * size, up.shape[1]),
+        sixteen(3, depth, span),
+        pltpu.SemaphoreType.DMA((3 * (width // span),)),
+        sixteen(*full),
+        sixteen(*part),
+        sixteen(*part),
+        sixteen(*full),
+        sixteen(*part),
+        sixteen(2, *part),
+        sixteen(2, 4 * slots, width),
+        sixteen(2, 2, slots // 2, width),
+        sixteen(2, 2, slots, width),
+        sixteen(2, 4 * slots, width),
+        pltpu.VMEM((size, width), jnp.float32),
+        sixteen(2, *full),
+        sixteen(2, 8 * slots, inside),
     ]
-    made = lambda *shape: jax.ShapeDtypeStruct(shape, tokens.dtype)
+    scratch += scatter_scratch(size, width, tokens.dtype, 32) + scatter_scratch(size, width, tokens.dtype, SPLIT)
     return communicate(
-        "middle",
-        functools.partial(middle_body, heads),
+        "block",
+        functools.partial(block_body, heads),
         collective_id,
-        (qkv, weight, tokens, gain, up, down, position),
-        [made(size, width), gathered(down, 1), made(8 * size, up.shape[1]), made(2, 4, 2, slots, width)],
-        scratch + scatter_scratch(size, width, tokens.dtype, SPLIT),
-        24 + 22 + 2 * 22 + 8 + 4 * 10,
+        (qkv, weight, tokens, gain, up, down, position, expert_in, expert_out, pick),
+        [jax.ShapeDtypeStruct(tokens.shape, tokens.dtype)],
+        scratch,
+        24 + 22 + 2 * 22 + 8 + 4 * 10 + 24 + 2 * 10 + 12 + 12,
+        outside=(7, 8),
+        spare=7 * 2**20,
     )
 
 
@@ -622,35 +691,15 @@
         net.work(1.6, lambda j=j: piece(j))
 
 
-def tail_body(units, down, rows, expert_in, expert_out, pick, hidden, out, *rest):
-    terms, pair, far, other, total, near, partial, found, packed, relay, y_relay = rest[:11]
-    arrived_rows, dense, parts, inner, weights, fetched = rest[11:17]
-    tiles, span = weights.shape[1], weights.shape[3]
-    fetches = []
-    for i, source in enumerate((expert_in, expert_out)):
-        for j in range(tiles):
-            fetch = pltpu.make_async_copy(source.at[:, pl.ds(j * span, span)], weights.at[i, j], fetched.at[i, j])
-            fetch.start()
-            fetches.append(fetch)
-    net = Net(*rest[-2:])
-    net.greet(["x+", "x-", "y+", "y-", "y+c", "y-c", "c", "z", "w"])
+def returning(net, rows, pick, hidden, out, weights, fetches, fetch, *rest):
+    far, other, total, near, partial, found, packed, relay, y_relay = rest[:9]
+    arrived_rows, dense, parts, inner = rest[9:13]
+    held, _, span = weights.shape
+    tiles = inner.shape[2] // span
     low = net.low
     half = parts.shape[3] // 2
-    size = hidden.shape[0]
     mine, theirs = pl.ds(pl.multiple_of(low * half, half), half), pl.ds(pl.multiple_of((1 - low) * half, half), half)
     count = packed.shape[1] // 4
-
-    def fill(column):
-        at = [pl.ds(pl.multiple_of(column(i) * size, size), size) for i in range(2)]
-        for i in range(2):
-            pair[pl.ds(i * size, size), :] = units[at[i], :]
-
-        @pl.loop(0, down.shape[1] // 256)
-        def _(j):
-            columns = pl.ds(pl.multiple_of(j * 256, 256), 256)
-            product = matmul(pair[...], down[:, columns]).astype(jnp.bfloat16)
-            for i in range(2):
-                terms[at[i], columns] = product[i * size : (i + 1) * size]
 
     def pack(index):
         flat = math.prod(found.shape[1:4])
@@ -693,22 +742,23 @@
 
         @pl.loop(0, 2)
         def _(i):
-            value = matmul(rows[i].reshape(flat_rows, rows.shape[4]), weights[0, j])
+            value = matmul(rows[i].reshape(flat_rows, rows.shape[4]), weights[j % held])
             value = value * (1.0 + lax.erf(value * (0.5**0.5))) * 0.5
             inner[i, :, pl.ds(j * span, span)] = value.astype(inner.dtype)
 
-        net.spend(1.5)
+        fetch()
 
     def expert_down(i, j):
-        if i == 1:
-            fetches[tiles + j].wait()
-        value = matmul(inner[i], weights[1, j]).astype(parts.dtype)
+        t = (2 - i) * tiles + j
+        fetches[t].wait()
+        value = matmul(inner[i], weights[t % held]).astype(parts.dtype)
         parts[i, :, :, :, pl.ds(j * span, span)] = value.reshape(parts.shape[1:4] + (span,))
-        net.spend(0.7)
+        fetch()
 
     def finish_dense(start, total):
         dense[pl.ds(start, total.shape[0]), :] = total
-        ready()
+        if start:
+            ready()
 
     def combine():
         flat = 4 * count
@@ -735,6 +785,13 @@
 
         net.when(net.copy(far.at[d, :, mine], other.at[d], other.at[d], "z"), add)
 
+    pending = []
+    held_back = counted(5, lambda: pending.pop()())
+
+    def gate(action):
+        pending.append(action)
+        held_back()
+
     def near_landed(d):
         def add():
             found[0, d] = near[d, :, mine] + partial[d]
@@ -742,6 +799,7 @@
             complete[0]()
 
         net.when(net.copy(near.at[d, :, theirs], partial.at[d], partial.at[d], "z"), add)
+        held_back()
 
     complete = [counted(4, functools.partial(send, index)) for index in range(2)]
     far_counts = {d: counted(1 if d == 0 else 2, functools.partial(far_landed, d)) for d in range(4)}
@@ -749,60 +807,16 @@
     second = y_exchange(net, chunks(parts.at[0]), chunks(near), y_relay.at[0], lambda d: near_counts[d]())
     go = counted(2, lambda: start_all(second))
     first = y_exchange(net, chunks(parts.at[1]), chunks(far), y_relay.at[1], lambda d: far_counts[d](), go)
-    steps = []
-    reduce_scatter(net, fill, terms, rest[17:-2], finish_dense, 0, steps.append)
-    steps[0]()
-    net.spend(1.6)
-    for j in range(tiles):
-        expert_up(j)
-    for j in range(tiles):
-        expert_down(1, j)
-    start_all(first)
-    for j in range(tiles):
-        expert_down(0, j)
-    go()
-    for step in steps[1:]:
-        step()
-        net.spend(1.6)
-    net.run()
-
-
-def tail(collective_id, units, down, rows, expert_in, expert_out, pick, hidden):
-    size, width = hidden.shape
-    count = rows.shape[3]
-    full, part = (4, 2, count, width), (4, 2, count // 2, width)
-    depth, inside = expert_in.shape
-    span = min(512, width)
-    sixteen = lambda *shape: pltpu.VMEM(shape, hidden.dtype)
-    scratch = [
-        sixteen(8 * size, width),
-        sixteen(2 * size, units.shape[1]),
-        sixteen(*full),
-        sixteen(*part),
-        sixteen(*part),
-        sixteen(*full),
-        sixteen(*part),
-        sixteen(2, *part),
-        sixteen(2, 4 * count, width),
-        sixteen(2, 2, count // 2, width),
-        sixteen(2, 2, count, width),
-        sixteen(2, 4 * count, width),
-        pltpu.VMEM((size, width), jnp.float32),
-        sixteen(2, *full),
-        sixteen(2, 8 * count, inside),
-        sixteen(2, width // span, depth, span),
-        pltpu.SemaphoreType.DMA((2, width // span)),
-    ]
-    return communicate(
-        "tail",
-        tail_body,
-        collective_id,
-        (units, down, rows, expert_in, expert_out, pick, hidden),
-        [jax.ShapeDtypeStruct(hidden.shape, hidden.dtype)],
-        scratch + scatter_scratch(size, width, hidden.dtype, 0),
-        24 + 2 * 10 + 12 + 12,
-        outside=(3, 4),
-    )
+
+    def start():
+        for j in range(tiles):
+            net.work(1.2, functools.partial(expert_up, j))
+        for i, after in ((1, lambda: start_all(first)), (0, go)):
+            for j in range(tiles):
+                net.work(0.6, functools.partial(expert_down, i, j))
+            net.work(0.0, after)
+
+    return finish_dense, start, gate
 
 
 def layer_norm(row_data, gain_vector):
@@ -870,10 +884,10 @@
     found = jnp.where(home // 8 != row_index // 8, found + 4 * rows, found)
     pick = (found[:, None] == jnp.arange(8 * rows, dtype=jnp.int32)[None, :]).astype(jnp.bfloat16)
 
-    hidden_mine, down_whole, hidden_units, expert_rows = middle(
-        1, head_count, projected, out_whole, tokens, ln2_gain[None, :], ffn_in, ffn_out, position, rows
+    (out,) = whole_block(
+        1, head_count, projected, out_whole, tokens, ln2_gain[None, :], ffn_in, ffn_out, position,
+        expert_in[0], expert_out[0], pick, rows,
     )
-    (out,) = tail(2, hidden_units, down_whole, expert_rows, expert_in[0], expert_out[0], pick, hidden_mine)
     return out
 
 

time: 221 us -> 215 us (0.973)
  Pallas kernels: 209 us -> 199 us
  local copies, waits for them, and re-layouts: 3.99 us -> 6.6 us
    pallas_call x3 -> x2, Pallas kernels: 209 us -> 199 us  [communicate(): pl.pallas_call(body, out_shape=shapes, in_specs=[pl.BlockSpec(memory_spac...]
    unnamed x18 -> x12, local copies, waits for them, and re-layouts: 3.81 us -> 5.83 us
where the time goes in v8:
time: 215 us
  Pallas kernels  199 us (93%)
  local copies, waits for them, and re-layouts  6.6 us (3%)
  matrix products  5.12 us (2%)
  other arithmetic  4.17 us (2%)
    pallas_call x2, Pallas kernels, communicate(): pl.pallas_call(body, out_shape=shapes, in_specs=[pl.BlockSpec(memory_spac...  199 us
    unnamed x12, local copies, waits for them, and re-layouts  5.83 us
    dot_general x1, matrix products, matmul(): return jnp.dot(a, b, preferred_element_type=jnp.float32)  5.12 us

profile of v8, /device:TPU:2, one launch (start us, length us, event | category | flops | bytes accessed | tf_op | source)
XLA Modules:
  0.0 214.9 jit_solution(9399251342539191577)
XLA Ops:
  0.0 0.0 copy-start.4
  0.0 0.8 convert_reduce_fusion.1
  0.8 0.7 multiply_add_fusion
  1.5 1.1 copy.14
  2.6 0.2 copy.15.refs_2_
  2.8 0.0 copy-start
  2.8 1.0 copy-done
  3.8 0.0 copy-start.2
  3.8 0.8 copy-done.2
  4.7 39.7 %enter.1 = (bf16[1024,2048]{1,0:T(8,128)(2,1)S(1)}, s32[64,128]{1,0:T(8,128)S(1)}, bf16[2048,768]{1,0:T(8,128)(2,1)S(1)}, bf16[256,2048]{1,0:T(8,128)(2,1)S(1)}) custom-call(bf16[128,2048]{1,0:T(8,128)(2,1)S(1)} %copy-done, s32[8,128]{1,0:T(8,128)S(1)} %broadcast_in_dim.7.refs_1_, bf16[128,768]{1,0:T(8,128)(2,1)S(1)} %copy.15.refs_2_, ...), custom_call_target="tpu_custom_call" | custom-call | tf_op jit(solution)/shard_map/enter/pallas_call | solution.py:416
  44.3 0.0 copy-start.1
  44.3 1.0 copy-done.1
  45.3 0.6 convert_reduce_fusion
  45.9 1.2 fusion.2
  47.1 0.0 copy-done.4
  47.2 0.0 copy-start.3
  47.2 5.1 %fusion.10.qkv = bf16[1024,768]{1,0:T(8,128)(2,1)} fusion(bf16[2048,768]{1,0:T(8,128)(2,1)S(1)} %get-tuple-element.10, bf16[1024,2048]{1,0:T(8,128)(2,1)S(1)} %get-tuple-element.9, f32[2048]{0:T(1024)S(1)} %copy-done.4, f32[1024]{0:T(1024)S(1)} %add_rsqrt_fusion, f32[1024]{0:T(1024)S(1)} %broadcast_multiply_fusion), kind=kOutput, calls=%fused_computation.11 | convolution fusion | flops 3232497664 | bytes 8929280 | tf_op jit(solution)/shard_map/dot_general | solution.py:830
  52.3 0.1 fusion.28
  52.4 0.6 broadcast_in_dim.9.position
  53.0 0.0 copy-done.3
  53.0 0.7 fusion.13.pick
  53.7 159.3 %block.1 = bf16[128,2048]{1,0:T(8,128)(2,1)} custom-call(bf16[1024,768]{1,0:T(8,128)(2,1)} %fusion.10.qkv, bf16[256,2048]{1,0:T(8,128)(2,1)} %copy-done.1, bf16[128,2048]{1,0:T(8,128)(2,1)} %tokens.1, f32[1,2048]{1,0:T(1,128)} %bitcast.24, bf16[128,1024]{1,0:T(8,128)(2,1)} %up.1, bf16[1024,128]{1,0:T(8,128)(2,1)} %down.1, ...), custom_call_target="tpu_custom_call" | custom-call | tf_op jit(solution)/shard_map/block/pallas_call | solution.py:416
  213.0 1.9 copy.17
  (6 shorter events, 0.1 us)
Async XLA Ops:
  0.0 47.1 %copy-start.4 = (f32[2048]{0:T(1024)S(1)}, f32[2048]{0:T(1024)}, u32[]{:S(2)}) copy-start(f32[2048]{0:T(1024)} %param.11) | copy-start | bytes 24580
  2.8 1.0 copy-start
  3.8 0.8 copy-start.2
  44.3 1.0 copy-start.1
  47.2 5.8 %copy-start.3 = (s32[128,1]{0,1:T(1,128)S(1)}, s32[128,1]{0,1:T(1,128)}, u32[]{:S(2)}) copy-start(s32[128,1]{0,1:T(1,128)} %param.17) | copy-start | bytes 1540

commit v9 on v8

--- a/solution.py
+++ b/solution.py
@@ -66,7 +66,7 @@
         out, arrival = make(dst), make(arriving)
         out.start()
         self.finish.append(out)
-        rate, delay = (600e3, 1.0) if name == "c" else (46e3, 2.0)
+        rate, delay = (600e3, 1.0) if name == "c" else (46e3, 2.6)
         begin = max(self.now, self.free.get(name[:2], 0.0))
         self.free[name[:2]] = begin + math.prod(arriving.shape) * arriving.dtype.itemsize / rate
         return arrival, self.free[name[:2]] + delay
@@ -810,11 +810,13 @@
 
     def start():
         for j in range(tiles):
-            net.work(1.2, functools.partial(expert_up, j))
+            expert_up(j)
+            net.spend(1.3)
         for i, after in ((1, lambda: start_all(first)), (0, go)):
             for j in range(tiles):
-                net.work(0.6, functools.partial(expert_down, i, j))
-            net.work(0.0, after)
+                expert_down(i, j)
+                net.spend(0.7)
+            after()
 
     return finish_dense, start, gate
 

time: 215 us -> 211 us (0.981)
  Pallas kernels: 199 us -> 194 us
    pallas_call x2, Pallas kernels: 199 us -> 194 us  [communicate(): pl.pallas_call(body, out_shape=shapes, in_specs=[pl.BlockSpec(memory_spac...]
where the time goes in v9:
time: 211 us; the launch traced here: 210 us
  Pallas kernels  194 us (92%)
  local copies, waits for them, and re-layouts  6.6 us (3%)
  matrix products  5.12 us (2%)
  other arithmetic  4.17 us (2%)
    pallas_call x2, Pallas kernels, communicate(): pl.pallas_call(body, out_shape=shapes, in_specs=[pl.BlockSpec(memory_spac...  194 us
    unnamed x12, local copies, waits for them, and re-layouts  5.83 us
    dot_general x1, matrix products, matmul(): return jnp.dot(a, b, preferred_element_type=jnp.float32)  5.12 us

profile of v9, /device:TPU:2, one launch (start us, length us, event | category | flops | bytes accessed | tf_op | source)
XLA Modules:
  0.0 210.4 jit_solution(11364969059634741034)
XLA Ops:
  0.0 0.0 copy-start.4
  0.0 0.8 convert_reduce_fusion.1
  0.8 0.7 multiply_add_fusion
  1.5 1.1 copy.14
  2.6 0.2 copy.15.refs_2_
  2.8 0.0 copy-start
  2.8 1.0 copy-done
  3.8 0.0 copy-start.2
  3.8 0.8 copy-done.2
  4.7 39.7 %enter.1 = (bf16[1024,2048]{1,0:T(8,128)(2,1)S(1)}, s32[64,128]{1,0:T(8,128)S(1)}, bf16[2048,768]{1,0:T(8,128)(2,1)S(1)}, bf16[256,2048]{1,0:T(8,128)(2,1)S(1)}) custom-call(bf16[128,2048]{1,0:T(8,128)(2,1)S(1)} %copy-done, s32[8,128]{1,0:T(8,128)S(1)} %broadcast_in_dim.7.refs_1_, bf16[128,768]{1,0:T(8,128)(2,1)S(1)} %copy.15.refs_2_, ...), custom_call_target="tpu_custom_call" | custom-call | tf_op jit(solution)/shard_map/enter/pallas_call | solution.py:416
  44.3 0.0 copy-start.1
  44.3 1.0 copy-done.1
  45.3 0.6 convert_reduce_fusion
  45.9 1.2 fusion.2
  47.1 0.0 copy-done.4
  47.2 0.0 copy-start.3
  47.2 5.1 %fusion.10.qkv = bf16[1024,768]{1,0:T(8,128)(2,1)} fusion(bf16[2048,768]{1,0:T(8,128)(2,1)S(1)} %get-tuple-element.10, bf16[1024,2048]{1,0:T(8,128)(2,1)S(1)} %get-tuple-element.9, f32[2048]{0:T(1024)S(1)} %copy-done.4, f32[1024]{0:T(1024)S(1)} %add_rsqrt_fusion, f32[1024]{0:T(1024)S(1)} %broadcast_multiply_fusion), kind=kOutput, calls=%fused_computation.11 | convolution fusion | flops 3232497664 | bytes 8929280 | tf_op jit(solution)/shard_map/dot_general | solution.py:832
  52.3 0.1 fusion.28
  52.4 0.6 broadcast_in_dim.9.position
  53.0 0.0 copy-done.3
  53.0 0.7 fusion.13.pick
  53.7 154.8 %block.1 = bf16[128,2048]{1,0:T(8,128)(2,1)} custom-call(bf16[1024,768]{1,0:T(8,128)(2,1)} %fusion.10.qkv, bf16[256,2048]{1,0:T(8,128)(2,1)} %copy-done.1, bf16[128,2048]{1,0:T(8,128)(2,1)} %tokens.1, f32[1,2048]{1,0:T(1,128)} %bitcast.24, bf16[128,1024]{1,0:T(8,128)(2,1)} %up.1, bf16[1024,128]{1,0:T(8,128)(2,1)} %down.1, ...), custom_call_target="tpu_custom_call" | custom-call | tf_op jit(solution)/shard_map/block/pallas_call | solution.py:416
  208.5 1.9 copy.17
  (6 shorter events, 0.1 us)
Async XLA Ops:
  0.0 47.1 %copy-start.4 = (f32[2048]{0:T(1024)S(1)}, f32[2048]{0:T(1024)}, u32[]{:S(2)}) copy-start(f32[2048]{0:T(1024)} %param.11) | copy-start | bytes 24580
  2.8 1.0 copy-start
  3.8 0.8 copy-start.2
  44.3 1.0 copy-start.1
  47.2 5.8 %copy-start.3 = (s32[128,1]{0,1:T(1,128)S(1)}, s32[128,1]{0,1:T(1,128)}, u32[]{:S(2)}) copy-start(s32[128,1]{0,1:T(1,128)} %param.17) | copy-start | bytes 1540

commit v10 on v9

--- a/solution.py
+++ b/solution.py
@@ -483,9 +483,8 @@
         def _(i):
             at = pl.ds(pl.multiple_of(column(i) * size, size), size)
 
-            @pl.loop(0, heads)
-            def _(h):
-                part = lambda k: pl.ds(pl.multiple_of((3 * h + k) * dim, dim), dim)
+            for h in range(heads):
+                part = lambda k, h=h: pl.ds((3 * h + k) * dim, dim)
                 scores = lax.dot_general(
                     qkv[at, part(0)], qkv[:, part(1)], (((1,), (1,)), ((), ())), preferred_element_type=jnp.float32
                 )
@@ -493,7 +492,7 @@
                 chances = jnp.exp2((scores - jnp.max(scores, axis=-1, keepdims=True)) * scale)
                 total = jnp.sum(chances, axis=-1, keepdims=True)
                 value = matmul(chances.astype(jnp.bfloat16), qkv[:, part(2)]) / total
-                mixed[:, pl.ds(pl.multiple_of(h * dim, dim), dim)] = value.astype(jnp.bfloat16)
+                mixed[:, pl.ds(h * dim, dim)] = value.astype(jnp.bfloat16)
 
             @pl.loop(0, weight.shape[1] // 512)
             def _(j):

time: 211 us -> 210 us (level)
  no operation moved by 1% of the time
where the time goes in v10:
time: 210 us
  Pallas kernels  194 us (92%)
  local copies, waits for them, and re-layouts  6.6 us (3%)
  matrix products  5.12 us (2%)
  other arithmetic  4.17 us (2%)
    pallas_call x2, Pallas kernels, communicate(): pl.pallas_call(body, out_shape=shapes, in_specs=[pl.BlockSpec(memory_spac...  194 us
    unnamed x12, local copies, waits for them, and re-layouts  5.83 us
    dot_general x1, matrix products, matmul(): return jnp.dot(a, b, preferred_element_type=jnp.float32)  5.12 us

profile of v10, /device:TPU:2, one launch (start us, length us, event | category | flops | bytes accessed | tf_op | source)
XLA Modules:
  0.0 210.0 jit_solution(5848393788820851297)
XLA Ops:
  0.0 0.0 copy-start.4
  0.0 0.8 convert_reduce_fusion.1
  0.8 0.7 multiply_add_fusion
  1.5 1.1 copy.14
  2.6 0.2 copy.15.refs_2_
  2.8 0.0 copy-start
  2.8 1.0 copy-done
  3.8 0.0 copy-start.2
  3.8 0.8 copy-done.2
  4.7 39.7 %enter.1 = (bf16[1024,2048]{1,0:T(8,128)(2,1)S(1)}, s32[64,128]{1,0:T(8,128)S(1)}, bf16[2048,768]{1,0:T(8,128)(2,1)S(1)}, bf16[256,2048]{1,0:T(8,128)(2,1)S(1)}) custom-call(bf16[128,2048]{1,0:T(8,128)(2,1)S(1)} %copy-done, s32[8,128]{1,0:T(8,128)S(1)} %broadcast_in_dim.7.refs_1_, bf16[128,768]{1,0:T(8,128)(2,1)S(1)} %copy.15.refs_2_, ...), custom_call_target="tpu_custom_call" | custom-call | tf_op jit(solution)/shard_map/enter/pallas_call | solution.py:416
  44.3 0.0 copy-start.1
  44.3 1.0 copy-done.1
  45.3 0.6 convert_reduce_fusion
  45.9 1.2 fusion.2
  47.1 0.0 copy-done.4
  47.2 0.0 copy-start.3
  47.2 5.1 %fusion.10.qkv = bf16[1024,768]{1,0:T(8,128)(2,1)} fusion(bf16[2048,768]{1,0:T(8,128)(2,1)S(1)} %get-tuple-element.10, bf16[1024,2048]{1,0:T(8,128)(2,1)S(1)} %get-tuple-element.9, f32[2048]{0:T(1024)S(1)} %copy-done.4, f32[1024]{0:T(1024)S(1)} %add_rsqrt_fusion, f32[1024]{0:T(1024)S(1)} %broadcast_multiply_fusion), kind=kOutput, calls=%fused_computation.11 | convolution fusion | flops 3232497664 | bytes 8929280 | tf_op jit(solution)/shard_map/dot_general | solution.py:831
  52.3 0.1 fusion.28
  52.4 0.6 broadcast_in_dim.9.position
  53.0 0.0 copy-done.3
  53.0 0.7 fusion.13.pick
  53.7 154.4 %block.1 = bf16[128,2048]{1,0:T(8,128)(2,1)} custom-call(bf16[1024,768]{1,0:T(8,128)(2,1)} %fusion.10.qkv, bf16[256,2048]{1,0:T(8,128)(2,1)} %copy-done.1, bf16[128,2048]{1,0:T(8,128)(2,1)} %tokens.1, f32[1,2048]{1,0:T(1,128)} %bitcast.24, bf16[128,1024]{1,0:T(8,128)(2,1)} %up.1, bf16[1024,128]{1,0:T(8,128)(2,1)} %down.1, ...), custom_call_target="tpu_custom_call" | custom-call | tf_op jit(solution)/shard_map/block/pallas_call | solution.py:416
  208.1 1.9 copy.17
  (6 shorter events, 0.1 us)
Async XLA Ops:
  0.0 47.1 %copy-start.4 = (f32[2048]{0:T(1024)S(1)}, f32[2048]{0:T(1024)}, u32[]{:S(2)}) copy-start(f32[2048]{0:T(1024)} %param.11) | copy-start | bytes 24580
  2.8 1.0 copy-start
  3.8 0.8 copy-start.2
  44.3 1.0 copy-start.1
  47.2 5.8 %copy-start.3 = (s32[128,1]{0,1:T(1,128)S(1)}, s32[128,1]{0,1:T(1,128)}, u32[]{:S(2)}) copy-start(s32[128,1]{0,1:T(1,128)} %param.17) | copy-start | bytes 1540
